TPU v7x, 128 devices: a whole 4x4x4 slice. The times are simulated.
128 devices in a mesh: dp: 32 (over x, z, core), tensor: 4 (over y).
Axes of the slice: x: 4, y: 4, z: 4, core: 2. Of those that a mesh axis runs over, the one named last changes fastest.
Arguments:
- tokens: bfloat16 [16384, 4096], P(('dp', 'tensor')), may hold values from -6 to 6
- norm_gain: float32 [4096], replicated, may hold values from 0.1 to 1.9
- w_query: bfloat16 [4096, 2048], P(None, 'tensor'), may hold values from -2 to 2
- key_weight: bfloat16 [4096, 512], P(None, 'tensor'), may hold values from -0.09375 to 0.09375
- value_weight: bfloat16 [4096, 512], P(None, 'tensor'), may hold values from -0.09375 to 0.09375
- w_out: bfloat16 [2048, 4096], P('tensor'), may hold values from -0.125 to 0.125
- lengths: int32 [16], replicated, may hold values from 1 to 8704, 16384 in all
Outputs:
- layer_out: bfloat16 [16384, 4096], P(('dp', 'tensor'))
Inputs may be any that keep to these rules, and one draw needn't show every extreme that they name: The lengths sum to 16384, and some document has exactly 8704 tokens.
All inputs are finite; a program needn't handle non-finite values.
Results may differ from a plain program's by a relative error of at most 0.0095.
The roundings to bfloat16 on the way count: a program that leaves them out, or rounds other values in their place, can miss the bound.
Values may be sent and summed in bfloat16 or wider, within the bound.
No kernel may reach another device: no remote copies, remote signals or barrier semaphores. Data moves between devices by JAX's collectives and lax.ppermute only.
A program may use at most 128 MiB of HBM per device.

v0:
```python
import functools

import jax
import jax.numpy as jnp
from jax import lax
from jax.experimental import pallas as pl
from jax.experimental.pallas import tpu as pltpu
from jax.sharding import PartitionSpec as P


HEAD_SIZE = 128

epsilon = 1e-05
rope_base = 500000.0
masked = -1e30
initial_peak = -1e29
ROWS = 256
PIECE_SPACE = pltpu.HBM
exp2_scale = 1.4426950408889634 * HEAD_SIZE ** (-0.5)

RING = 4
RELATIVE = (0, 3, 1, 2)


def ring_shift(step):
    return [(i, (i + step) % RING) for i in range(RING)]


def plane_shift(step, first_axis):
    pairs = []
    for d in range(32):
        x, z, core = d // 8, d // 2 % 4, d % 2
        if (core == 0) == first_axis:
            z = (z + step) % 4
        else:
            x = (x + step) % 4
        pairs.append((d, x * 8 + z * 2 + core))
    return pairs


CORE_SWAP = [(d, d ^ 1) for d in range(32)]


def ring_gather(piece, axis, shift):
    half = piece.shape[0] // 2
    behind = lax.ppermute(piece, axis, shift(1))
    ahead = lax.ppermute(piece, axis, shift(-1))
    upper = lax.ppermute(behind[:half], axis, shift(1))
    lower = lax.ppermute(ahead[half:], axis, shift(-1))
    return [piece, behind, ahead, upper, lower]


def gather_plane(keys, values):
    core = lax.axis_index("dp") & 1
    other = lax.ppermute(jnp.where(core == 0, values, keys), "dp", CORE_SWAP)
    mine = jnp.where(
        core == 0,
        jnp.concatenate([keys, other], axis=0),
        jnp.concatenate([other, values], axis=0),
    )
    line = ring_gather(mine, "dp", functools.partial(plane_shift, first_axis=True))
    plane = ring_gather(
        jnp.concatenate(line, axis=0), "dp", functools.partial(plane_shift, first_axis=False)
    )
    return plane, [lax.ppermute(piece, "dp", CORE_SWAP) for piece in plane]


def doc_starts(lengths, positions):
    order = jnp.arange(lengths.shape[0], dtype=jnp.int32)
    doc_ends = jnp.sum(jnp.where(order[:, None] <= order[None, :], lengths[:, None], 0), axis=0)
    closed = (doc_ends[None, :] <= positions[:, None]).astype(jnp.int32)
    return jnp.sum(closed * lengths[None, :], axis=1)


def angles_of(offsets):
    lane = jnp.arange(HEAD_SIZE, dtype=jnp.int32)
    half_width = HEAD_SIZE // 2
    exponent = (lane & (half_width - 1)).astype(jnp.float32) * (-2.0 / HEAD_SIZE)
    frequency = rope_base**exponent
    angles = offsets.astype(jnp.float32)[:, None] * frequency[None, :]
    sign = jnp.where(lane < half_width, -1.0, 1.0).astype(jnp.float32)
    return jnp.cos(angles), jnp.sin(angles) * sign[None, :]


def norm(tokens, norm_gain):
    wide = tokens.astype(jnp.float32)
    inverse = lax.rsqrt(jnp.mean(wide * wide, axis=1, keepdims=True) + epsilon)
    return (wide * inverse * norm_gain[None, :]).astype(jnp.bfloat16)


def wide_dot(a, b):
    return jnp.dot(a, b, preferred_element_type=jnp.float32)


def attend_kernel(ids, lengths, query, cos_part, sin_part, *refs, quarters):
    pieces, refs = refs[:10], refs[10:]
    out, rows, peak, summed, starts, query_at, key_at, block, sems = refs
    own_planes, swapped = pieces[:5], pieces[5:]
    count = query.shape[0]
    heads = query.shape[1] // HEAD_SIZE
    size = block.shape[2]
    span = count // len(quarters)
    docs = lengths.shape[0]
    dp, mine = ids[0], ids[1]
    own_x, own_z, core = dp >> 3, (dp >> 1) & 3, dp & 1

    def quarter_base(quarter):
        return ((mine + RELATIVE[quarter]) & 3) * span

    bases = [dp * (RING * span) + quarter_base(q) for q in quarters]
    first = functools.reduce(jnp.minimum, bases)
    last = functools.reduce(jnp.maximum, bases) + (span - 1)
    ends, end = [], jnp.int32(0)
    for d in range(docs):
        end = end + lengths[d]
        ends.append(end)

    def start_of(at):
        start = jnp.zeros_like(at)
        for end in ends:
            start = jnp.where(at >= end, end, start)
        return start

    first_start, last_start = start_of(first), start_of(last)
    low, high = first_start // size, last // size + 1
    full_low, full_high = (last_start + size - 1) // size, (first + 1) // size

    def place(step):
        return jnp.where(step == 0, 0, jnp.where(step == 1, 2, jnp.where(step == 2, 3, 1)))

    def start_copies(chip):
        slot = chip & 1
        at_x, at_z = place(((chip >> 2) - own_x) & 3), place(((chip & 3) - own_z) & 3)
        outer = jnp.where(core == 0, at_x, at_z)
        inner = jnp.where(core == 0, at_z, at_x)
        for sources, kind, major, minor in (
            (own_planes, core, outer, inner),
            (swapped, 1 - core, inner, outer),
        ):
            index = jnp.where((major == 3) & (minor >= 2), 4, major)
            row = pl.multiple_of(jnp.where(major == 3, minor & 1, minor) * size, size)
            for n, source in enumerate(sources):

                @pl.when(index == n)
                def _():
                    pltpu.make_async_copy(
                        source.at[pl.ds(row, size)], block.at[slot, kind], sems.at[slot, kind]
                    ).start()

    def wait_copies(chip):
        slot = chip & 1
        for kind in range(2):
            pltpu.make_async_copy(
                own_planes[0].at[pl.ds(0, size)], block.at[slot, kind], sems.at[slot, kind]
            ).wait()

    start_copies(low)
    for h in range(heads):
        at = slice(h * HEAD_SIZE, (h + 1) * HEAD_SIZE)
        head = query[:, at]
        turned = head * cos_part[...] + pltpu.roll(head, HEAD_SIZE // 2, 1) * sin_part[...]
        rows[h * count : (h + 1) * count, :] = turned.astype(jnp.bfloat16)
    for i, base in enumerate(bases):
        at = base + lax.broadcasted_iota(jnp.int32, (span, 1), 0)
        query_at[i * span : (i + 1) * span, :] = at
        starts[i * span : (i + 1) * span, :] = start_of(at)
    for i in range(size // span):
        base = (i // RING) * (RING * span) + quarter_base(i % RING)
        lane = lax.broadcasted_iota(jnp.int32, (1, span), 1)
        key_at[:, i * span : (i + 1) * span] = base + lane
    peak[...] = jnp.full(peak.shape, initial_peak, jnp.float32)
    summed[...] = jnp.zeros(summed.shape, jnp.float32)

    def step(chip, cut):
        slot = chip & 1
        block_keys = block[slot, 0]
        block_values = jnp.concatenate(
            [block[slot, 1], jnp.ones((size, HEAD_SIZE), jnp.bfloat16)], axis=1
        )
        if cut:
            where = chip * size + key_at[...]
            visible = (where >= starts[...]) & (where <= query_at[...])
            if count < ROWS:
                visible = jnp.concatenate([visible] * (ROWS // count), axis=0)
        for r in range(heads * count // ROWS):
            at = slice(r * ROWS, (r + 1) * ROWS)
            scores = lax.dot_general(
                rows[at, :], block_keys, (((1,), (1,)), ((), ())), preferred_element_type=jnp.float32
            )
            if cut:
                local = (r * ROWS) % max(count, ROWS)
                scores = jnp.where(visible[local : local + ROWS], scores, masked)
            parts = [scores[:, c : c + HEAD_SIZE] for c in range(0, size, HEAD_SIZE)]
            old = peak[at, :]
            best = functools.reduce(jnp.maximum, parts)
            fresh = jnp.maximum(old, jnp.max(best, axis=1, keepdims=True))
            peak[at, :] = fresh
            shrink = jnp.exp2((old - fresh) * exp2_scale)
            probs = [jnp.exp2((part - fresh) * exp2_scale).astype(jnp.bfloat16) for part in parts]
            update = wide_dot(jnp.concatenate(probs, axis=1), block_values)
            summed[at, :HEAD_SIZE] = summed[at, :HEAD_SIZE] * shrink + update[:, :HEAD_SIZE]
            summed[at, HEAD_SIZE:] = summed[at, HEAD_SIZE:] * shrink + update[:, HEAD_SIZE:]

    def one_block(chip, carry):
        wait_copies(chip)

        @pl.when(chip + 1 < high)
        def _():
            start_copies(chip + 1)

        whole = (chip >= full_low) & (chip < full_high)

        @pl.when(whole)
        def _():
            step(chip, False)

        @pl.when(jnp.logical_not(whole))
        def _():
            step(chip, True)

        return carry

    lax.fori_loop(low, high, one_block, 0)
    for h in range(heads):
        at = slice(h * count, (h + 1) * count)
        attended = summed[at, :HEAD_SIZE] / summed[at, HEAD_SIZE:]
        out[:, h * HEAD_SIZE : (h + 1) * HEAD_SIZE] = attended.astype(jnp.bfloat16)


def attend(ids, lengths, query, cos_part, sin_part, pieces, quarters):
    count, width = query.shape
    rows = count * width // HEAD_SIZE
    size = 2 * RING * count // len(quarters)
    vmem = pl.BlockSpec(memory_space=pltpu.VMEM)
    smem = pl.BlockSpec(memory_space=pltpu.SMEM)
    hbm = pl.BlockSpec(memory_space=PIECE_SPACE)
    return pl.pallas_call(
        functools.partial(attend_kernel, quarters=quarters),
        out_shape=jax.ShapeDtypeStruct((count, width), jnp.bfloat16),
        in_specs=[smem, smem, vmem, vmem, vmem] + [hbm] * 10,
        out_specs=vmem,
        scratch_shapes=[
            pltpu.VMEM((rows, HEAD_SIZE), jnp.bfloat16),
            pltpu.VMEM((rows, HEAD_SIZE), jnp.float32),
            pltpu.VMEM((rows, 2 * HEAD_SIZE), jnp.float32),
            pltpu.VMEM((count, 1), jnp.int32),
            pltpu.VMEM((count, 1), jnp.int32),
            pltpu.VMEM((1, size), jnp.int32),
            pltpu.VMEM((2, 2, size, HEAD_SIZE), jnp.bfloat16),
            pltpu.SemaphoreType.DMA((2, 2)),
        ],
        compiler_params=pltpu.CompilerParams(vmem_limit_bytes=32 * 2**20),
        cost_estimate=pl.CostEstimate(
            flops=rows * 4096 * 512, transcendentals=rows * 4096, bytes_accessed=4 << 20
        ),
        name="attend",
    )(ids, lengths, query, cos_part, sin_part, *pieces)


def body(tokens, norm_gain, w_query, key_weight, value_weight, w_out, lengths):
    count = tokens.shape[0]
    dp, mine = lax.axis_index("dp"), lax.axis_index("tensor")
    normed = norm(tokens, norm_gain)
    quarter = (mine + jnp.array(RELATIVE, jnp.int32)) & 3
    local = (quarter[:, None] * count + jnp.arange(count, dtype=jnp.int32)[None, :]).reshape(-1)
    positions = dp * (RING * count) + local
    cos_part, sin_part = angles_of(positions - doc_starts(lengths, positions))
    ids = jnp.stack([dp, mine]).astype(jnp.int32)

    def project(piece, q):
        at = slice(q * count, (q + 1) * count)
        key = wide_dot(piece, key_weight)
        key = key * cos_part[at] + jnp.roll(key, HEAD_SIZE // 2, axis=1) * sin_part[at]
        value = wide_dot(piece, value_weight)
        return key.astype(jnp.bfloat16), value.astype(jnp.bfloat16)

    own = normed
    behind = lax.ppermute(own, "tensor", ring_shift(1))
    ahead = lax.ppermute(own, "tensor", ring_shift(-1))
    query = [None] * RING
    keys, values = [None] * RING, [None] * RING
    keys[0], values[0] = project(own, 0)
    query[0] = wide_dot(own, w_query)
    behind, ahead, query[0], keys[0], values[0] = lax.optimization_barrier(
        (behind, ahead, query[0], keys[0], values[0])
    )
    half = count // 2
    upper = lax.ppermute(behind[:half], "tensor", ring_shift(1))
    lower = lax.ppermute(ahead[half:], "tensor", ring_shift(-1))
    keys[1], values[1] = project(behind, 1)
    keys[2], values[2] = project(ahead, 2)
    query[1] = wide_dot(behind, w_query)
    query[2] = wide_dot(ahead, w_query)
    upper, lower, query[1], query[2], keys[1], values[1], keys[2], values[2] = (
        lax.optimization_barrier(
            (upper, lower, query[1], query[2], keys[1], values[1], keys[2], values[2])
        )
    )
    far = jnp.concatenate([upper, lower], axis=0)
    keys[3], values[3] = project(far, 3)
    pieces = gather_plane(jnp.concatenate(keys, axis=0), jnp.concatenate(values, axis=0))
    query[3] = wide_dot(far, w_query)
    plane, swapped = pieces
    pieces = list(plane) + list(swapped)

    def branch(quarters, after=None):
        at = slice(quarters[0] * count, (quarters[-1] + 1) * count)
        rows = jnp.concatenate([query[q] for q in quarters], axis=0)
        if after is not None:
            rows, after = lax.optimization_barrier((rows, after))
        attended = attend(ids, lengths, rows, cos_part[at], sin_part[at], pieces, quarters)
        return wide_dot(attended, w_out), after

    half = w_out.shape[1] // 2
    far, _ = branch((3,))
    far = far.astype(jnp.bfloat16)
    near, far = branch((1, 2), far)
    from_behind = lax.ppermute(far[:, :half], "tensor", ring_shift(1))
    from_ahead = lax.ppermute(far[:, half:], "tensor", ring_shift(-1))
    to_behind, to_ahead = near[:count], near[count:]
    plain_up = to_ahead[:, half:].astype(jnp.bfloat16)
    plain_up = lax.ppermute(plain_up, "tensor", ring_shift(1))
    plain_down = to_behind[:, :half].astype(jnp.bfloat16)
    plain_down = lax.ppermute(plain_down, "tensor", ring_shift(-1))
    sum_up = (to_ahead[:, :half] + from_behind.astype(jnp.float32)).astype(jnp.bfloat16)
    sum_down = (to_behind[:, half:] + from_ahead.astype(jnp.float32)).astype(jnp.bfloat16)
    here, (sum_up, sum_down) = branch((0,), (sum_up, sum_down))
    sum_up = lax.ppermute(sum_up, "tensor", ring_shift(1))
    sum_down = lax.ppermute(sum_down, "tensor", ring_shift(-1))
    wide = [a.astype(jnp.float32) for a in (sum_up, plain_down, plain_up, sum_down)]
    total = here + jnp.concatenate([wide[0] + wide[1], wide[2] + wide[3]], axis=1)
    return (tokens.astype(jnp.float32) + total).astype(jnp.bfloat16)


def solution(mesh):
    in_specs = (
        P(("dp", "tensor"), None),
        P(),
        P(None, "tensor"),
        P(None, "tensor"),
        P(None, "tensor"),
        P("tensor", None),
        P(),
    )
    out_specs = P(("dp", "tensor"), None)
    return jax.shard_map(body, mesh=mesh, in_specs=in_specs, out_specs=out_specs, check_vma=False)
```

profile of v0, /device:TPU:100, one launch (start us, length us, event | category | flops | bytes accessed | tf_op | source)
XLA Modules:
  0.0 161.7 jit_solution(10645770155209876641)
XLA Ops:
  0.0 1.6 fusion.2
  1.6 1.6 fusion.4
  3.2 3.1 %collective-permute-start.1 = (bf16[128,4096]{1,0:T(8,128)(2,1)S(1)}, bf16[128,4096]{1,0:T(8,128)(2,1)S(1)}, u32[]{:S(2)}, u32[]{:S(2)}) collective-permute-start(bf16[128,4096]{1,0:T(8,128)(2,1)S(1)} %fusion.4), channel_id=1, source_target_pairs={{0,3},{1,0},{2,1},{3,2},{4,7},{5,4},{6,5},{7,6},{8,11},{9,8},{10,9... | collective-permute-start | bytes 3145736 | tf_op jit(solution)/shard_map/ppermute | solution.py:279
  8.6 1.6 %fusion.26 = f32[128,128]{1,0:T(8,128)S(1)} fusion(bf16[128,4096]{1,0:T(8,128)(2,1)S(1)} %fusion.4, bf16[4096,128]{1,0:T(8,128)(2,1)} %param.11), kind=kOutput, calls=%fused_computation.75 | convolution fusion | flops 134217728 | bytes 2162688 | tf_op jit(solution)/shard_map/dot_general | solution.py:92
  10.2 1.0 multiply_cosine_fusion
  11.9 3.0 %fusion.25.query = f32[128,512]{1,0:T(8,128)S(1)} fusion(bf16[128,4096]{1,0:T(8,128)(2,1)S(1)} %fusion.4, bf16[4096,512]{1,0:T(8,128)(2,1)} %param.10), kind=kOutput, calls=%fused_computation.74 | convolution fusion | flops 536870912 | bytes 5505024 | tf_op jit(solution)/shard_map/dot_general | solution.py:92
  14.9 13.8 %collective-permute-done.1 = bf16[128,4096]{1,0:T(8,128)(2,1)S(1)} collective-permute-done((bf16[128,4096]{1,0:T(8,128)(2,1)S(1)}, bf16[128,4096]{1,0:T(8,128)(2,1)S(1)}, u32[]{:S(2)}, u32[]{:S(2)}) %collective-permute-start.1) | collective-permute-done | bytes 1048608 | tf_op jit(solution)/shard_map/ppermute | solution.py:279
  28.7 3.5 %collective-permute-done = bf16[128,4096]{1,0:T(8,128)(2,1)} collective-permute-done((bf16[128,4096]{1,0:T(8,128)(2,1)S(1)}, bf16[128,4096]{1,0:T(8,128)(2,1)}, u32[]{:S(2)}, u32[]{:S(2)}) %collective-permute-start) | collective-permute-done | bytes 1048608 | tf_op jit(solution)/shard_map/ppermute | solution.py:278
  32.2 1.8 %convolution_convert_fusion.3 = bf16[128,128]{1,0:T(8,128)(2,1)S(1)} fusion(bf16[128,4096]{1,0:T(8,128)(2,1)} %collective-permute-done, bf16[4096,128]{1,0:T(8,128)(2,1)S(1)} %copy-done), kind=kOutput, calls=%fused_computation.11 | convolution fusion | flops 134234112 | bytes 2129920 | tf_op jit(solution)/shard_map/dot_general | solution.py:92
  34.0 1.7 %fusion.29 = f32[128,128]{1,0:T(8,128)S(1)} fusion(bf16[128,4096]{1,0:T(8,128)(2,1)} %collective-permute-done, bf16[4096,128]{1,0:T(8,128)(2,1)S(1)} %copy-done.4), kind=kOutput, calls=%fused_computation.78 | convolution fusion | flops 134217728 | bytes 2162688 | tf_op jit(solution)/shard_map/dot_general | solution.py:92
  36.6 2.0 %fusion.27 = f32[128,512]{1,0:T(8,128)S(1)} fusion(bf16[128,4096]{1,0:T(8,128)(2,1)} %collective-permute-done, bf16[4096,512]{1,0:T(8,128)(2,1)S(1)} %copy-done.2), kind=kOutput, calls=%fused_computation.76 | convolution fusion | flops 536870912 | bytes 5505024 | tf_op jit(solution)/shard_map/dot_general | solution.py:92
  38.6 1.1 slice.108
  40.1 1.8 %collective-permute-start.2 = (bf16[64,4096]{1,0:T(8,128)(2,1)S(1)}, bf16[64,4096]{1,0:T(8,128)(2,1)S(1)}, u32[]{:S(2)}, u32[]{:S(2)}) collective-permute-start(bf16[64,4096]{1,0:T(8,128)(2,1)S(1)} %slice.108), channel_id=1, source_target_pairs={{0,1},{1,2},{2,3},{3,0},{4,5},{5,6},{6,7},{7,4},{8,9},{9,10},{10,1... | collective-permute-start | bytes 1572872 | tf_op jit(solution)/shard_map/ppermute | solution.py:288
  42.8 9.6 %collective-permute-done.3 = bf16[64,4096]{1,0:T(8,128)(2,1)S(1)} collective-permute-done((bf16[64,4096]{1,0:T(8,128)(2,1)S(1)}, bf16[64,4096]{1,0:T(8,128)(2,1)S(1)}, u32[]{:S(2)}, u32[]{:S(2)}) %collective-permute-start.3) | collective-permute-done | bytes 524320 | tf_op jit(solution)/shard_map/ppermute | solution.py:289
  52.4 1.4 collective-permute-done.2
  55.1 1.3 collective-permute-done.4
  57.1 2.8 %collective-permute-start.5 = (bf16[1024,128]{1,0:T(8,128)(2,1)S(1)}, bf16[1024,128]{1,0:T(8,128)(2,1)S(1)}, u32[]{:S(2)}, u32[]{:S(2)}) collective-permute-start(bf16[1024,128]{1,0:T(8,128)(2,1)S(1)} %get-tuple-element.42), channel_id=1, source_target_pairs={{0,8},{4,36},{8,16},{12,44},{16,24},{20,52},{24,0},{28,60},{32,40}... | collective-permute-start | bytes 786440 | tf_op jit(solution)/shard_map/ppermute | solution.py:46
  60.0 4.3 %collective-permute-done.6 = bf16[1024,128]{1,0:T(8,128)(2,1)S(1)} collective-permute-done((bf16[1024,128]{1,0:T(8,128)(2,1)S(1)}, bf16[1024,128]{1,0:T(8,128)(2,1)S(1)}, u32[]{:S(2)}, u32[]{:S(2)}) %collective-permute-start.6) | collective-permute-done | bytes 262176 | tf_op jit(solution)/shard_map/ppermute | solution.py:47
  64.4 3.3 %collective-permute-start.7 = (bf16[512,128]{1,0:T(8,128)(2,1)S(1)}, bf16[512,128]{1,0:T(8,128)(2,1)S(1)}, u32[]{:S(2)}, u32[]{:S(2)}) collective-permute-start(bf16[512,128]{1,0:T(8,128)(2,1)S(1)} %slice.150), channel_id=1, source_target_pairs={{0,8},{4,36},{8,16},{12,44},{16,24},{20,52},{24,0},{28,60},{32,40}... | collective-permute-start | bytes 393224 | tf_op jit(solution)/shard_map/ppermute | solution.py:48
  67.8 2.4 %collective-permute-done.7 = bf16[512,128]{1,0:T(8,128)(2,1)S(1)} collective-permute-done((bf16[512,128]{1,0:T(8,128)(2,1)S(1)}, bf16[512,128]{1,0:T(8,128)(2,1)S(1)}, u32[]{:S(2)}, u32[]{:S(2)}) %collective-permute-start.7) | collective-permute-done | bytes 131104 | tf_op jit(solution)/shard_map/ppermute | solution.py:48
  71.2 1.5 collective-permute-start.9
  72.7 12.8 %collective-permute-done.10.refs_2_ = bf16[4096,128]{1,0:T(8,128)(2,1)S(1)} collective-permute-done((bf16[4096,128]{1,0:T(8,128)(2,1)S(1)}, bf16[4096,128]{1,0:T(8,128)(2,1)S(1)}, u32[]{:S(2)}, u32[]{:S(2)}) %collective-permute-start.10) | collective-permute-done | bytes 1048608 | tf_op jit(solution)/shard_map/ppermute | solution.py:47
  86.3 2.0 %collective-permute-start.11 = (bf16[2048,128]{1,0:T(8,128)(2,1)S(1)}, bf16[2048,128]{1,0:T(8,128)(2,1)S(1)}, u32[]{:S(2)}, u32[]{:S(2)}) collective-permute-start(bf16[2048,128]{1,0:T(8,128)(2,1)S(1)} %slice.152), channel_id=1, source_target_pairs={{0,32},{4,12},{8,40},{12,20},{16,48},{20,28},{24,56},{28,4},{32,64... | collective-permute-start | bytes 1572872 | tf_op jit(solution)/shard_map/ppermute | solution.py:48
  88.8 6.5 %collective-permute-done.12.refs_4_ = bf16[2048,128]{1,0:T(8,128)(2,1)S(1)} collective-permute-done((bf16[2048,128]{1,0:T(8,128)(2,1)S(1)}, bf16[2048,128]{1,0:T(8,128)(2,1)S(1)}, u32[]{:S(2)}, u32[]{:S(2)}) %collective-permute-start.12) | collective-permute-done | bytes 524320 | tf_op jit(solution)/shard_map/ppermute | solution.py:49
  98.0 14.4 %attend.3 = bf16[128,512]{1,0:T(8,128)(2,1)S(1)} custom-call(s32[2]{0:T(128)S(1)} %pad_add_fusion.ids, s32[16]{0:T(128)S(1)} %copy-done.1, f32[128,512]{1,0:T(8,128)S(1)} %fusion.31.query, f32[128,128]{1,0:T(8,128)S(1)} %get-tuple-element.56.cos_part, f32[128,128]{1,0:T(8,128)S(1)} %get-tuple-element.57.sin_part, ...), custom_call_target="tpu_custom_call" | custom-call | flops 1073741824 | bytes 4194304 | tf_op jit(solution)/shard_map/attend/pallas_call | solution.py:237
  113.3 2.0 %collective-permute-start.18 = (bf16[128,2048]{1,0:T(8,128)(2,1)S(1)}, bf16[128,2048]{1,0:T(8,128)(2,1)S(1)}, u32[]{:S(2)}, u32[]{:S(2)}) collective-permute-start(bf16[128,2048]{1,0:T(8,128)(2,1)S(1)} %get-tuple-element.50), channel_id=1, source_target_pairs={{0,1},{1,2},{2,3},{3,0},{4,5},{5,6},{6,7},{7,4},{8,9},{9,10},{10,1... | collective-permute-start | bytes 1572872 | tf_op jit(solution)/shard_map/ppermute | solution.py:318
  115.3 22.7 %attend.4 = bf16[256,512]{1,0:T(8,128)(2,1)S(1)} custom-call(s32[2]{0:T(128)S(1)} %pad_add_fusion.ids, s32[16]{0:T(128)S(1)} %copy-done.1, f32[256,512]{1,0:T(8,128)S(1)} %pad_maximum_fusion.query, f32[256,128]{1,0:T(8,128)S(1)} %slice.154.cos_part, f32[256,128]{1,0:T(8,128)S(1)} %slice.155.sin_part, ...), custom_call_target="tpu_custom_call" | custom-call | flops 2147483648 | bytes 4194304 | tf_op jit(solution)/shard_map/attend/pallas_call | solution.py:237
  138.0 1.3 fusion.24
  139.4 1.4 collective-permute-start.21
  142.0 3.2 %collective-permute-start.23 = (bf16[128,2048]{1,0:T(8,128)(2,1)S(1)}, bf16[128,2048]{1,0:T(8,128)(2,1)S(1)}, u32[]{:S(2)}, u32[]{:S(2)}) collective-permute-start(bf16[128,2048]{1,0:T(8,128)(2,1)S(1)} %get-tuple-element.40), channel_id=1, source_target_pairs={{0,3},{1,0},{2,1},{3,2},{4,7},{5,4},{6,5},{7,6},{8,11},{9,8},{10,9... | collective-permute-start | bytes 1572872 | tf_op jit(solution)/shard_map/ppermute | solution.py:329
  145.1 13.5 %attend.5 = bf16[128,512]{1,0:T(8,128)(2,1)S(1)} custom-call(s32[2]{0:T(128)S(1)} %pad_add_fusion.ids, s32[16]{0:T(128)S(1)} %copy-done.1, f32[128,512]{1,0:T(8,128)S(1)} %fusion.25.query, f32[128,128]{1,0:T(8,128)S(1)} %get-tuple-element.55.cos_part, f32[128,128]{1,0:T(8,128)S(1)} %get-tuple-element.53.sin_part, ...), custom_call_target="tpu_custom_call" | custom-call | flops 1073741824 | bytes 4194304 | tf_op jit(solution)/shard_map/attend/pallas_call | solution.py:237
  159.9 1.8 %fusion.1 = bf16[128,4096]{1,0:T(8,128)(2,1)} fusion(bf16[128,512]{1,0:T(8,128)(2,1)S(1)} %attend.5, bf16[512,4096]{1,0:T(8,128)(2,1)S(1)} %copy-done.3, bf16[128,4096]{1,0:T(8,128)(2,1)S(1)} %copy-done.5, f32[128,2048]{1,0:T(8,128)S(1)} %convert_add_fusion, f32[128,2048]{1,0:T(8,128)S(1)} %convert_add_fusion.1), kind=kOutput, calls=%fused_computation.2 | convolution fusion | flops 539492352 | bytes 8519680 | tf_op jit(solution)/shard_map/dot_general | solution.py:92
  (94 shorter events, 15.5 us)
Async XLA Ops:
  0.0 11.4 %copy-start = (bf16[4096,128]{1,0:T(8,128)(2,1)S(1)}, bf16[4096,128]{1,0:T(8,128)(2,1)}, u32[]{:S(2)}) copy-start(bf16[4096,128]{1,0:T(8,128)(2,1)} %param.12) | copy-start | bytes 3145732
  3.2 25.5 %collective-permute-start.1 = (bf16[128,4096]{1,0:T(8,128)(2,1)S(1)}, bf16[128,4096]{1,0:T(8,128)(2,1)S(1)}, u32[]{:S(2)}, u32[]{:S(2)}) collective-permute-start(bf16[128,4096]{1,0:T(8,128)(2,1)S(1)} %fusion.4), channel_id=1, source_target_pairs={{0,3},{1,0},{2,1},{3,2},{4,7},{5,4},{6,5},{7,6},{8,11},{9,8},{10,9... | collective-permute-start | bytes 3145736 | tf_op jit(solution)/shard_map/ppermute | solution.py:279
  6.3 25.9 %collective-permute-start = (bf16[128,4096]{1,0:T(8,128)(2,1)S(1)}, bf16[128,4096]{1,0:T(8,128)(2,1)}, u32[]{:S(2)}, u32[]{:S(2)}) collective-permute-start(bf16[128,4096]{1,0:T(8,128)(2,1)S(1)} %fusion.4), channel_id=1, source_target_pairs={{0,1},{1,2},{2,3},{3,0},{4,5},{5,6},{6,7},{7,4},{8,9},{9,10},{10,1... | collective-permute-start | bytes 3145736 | tf_op jit(solution)/shard_map/ppermute | solution.py:278
  11.9 22.1 %copy-start.4 = (bf16[4096,128]{1,0:T(8,128)(2,1)S(1)}, bf16[4096,128]{1,0:T(8,128)(2,1)}, u32[]{:S(2)}) copy-start(bf16[4096,128]{1,0:T(8,128)(2,1)} %param.11) | copy-start | bytes 3145732
  32.2 4.4 %copy-start.2 = (bf16[4096,512]{1,0:T(8,128)(2,1)S(1)}, bf16[4096,512]{1,0:T(8,128)(2,1)}, u32[]{:S(2)}) copy-start(bf16[4096,512]{1,0:T(8,128)(2,1)} %param.10) | copy-start | bytes 12582916
  39.9 12.6 %collective-permute-start.3 = (bf16[64,4096]{1,0:T(8,128)(2,1)S(1)}, bf16[64,4096]{1,0:T(8,128)(2,1)S(1)}, u32[]{:S(2)}, u32[]{:S(2)}) collective-permute-start(bf16[64,4096]{1,0:T(8,128)(2,1)S(1)} %slice.109), channel_id=1, source_target_pairs={{0,3},{1,0},{2,1},{3,2},{4,7},{5,4},{6,5},{7,6},{8,11},{9,8},{10,9... | collective-permute-start | bytes 1572872 | tf_op jit(solution)/shard_map/ppermute | solution.py:289
  40.1 13.7 %collective-permute-start.2 = (bf16[64,4096]{1,0:T(8,128)(2,1)S(1)}, bf16[64,4096]{1,0:T(8,128)(2,1)S(1)}, u32[]{:S(2)}, u32[]{:S(2)}) collective-permute-start(bf16[64,4096]{1,0:T(8,128)(2,1)S(1)} %slice.108), channel_id=1, source_target_pairs={{0,1},{1,2},{2,3},{3,0},{4,5},{5,6},{6,7},{7,4},{8,9},{9,10},{10,1... | collective-permute-start | bytes 1572872 | tf_op jit(solution)/shard_map/ppermute | solution.py:288
  55.0 1.4 collective-permute-start.4
  56.6 7.7 %collective-permute-start.6 = (bf16[1024,128]{1,0:T(8,128)(2,1)S(1)}, bf16[1024,128]{1,0:T(8,128)(2,1)S(1)}, u32[]{:S(2)}, u32[]{:S(2)}) collective-permute-start(bf16[1024,128]{1,0:T(8,128)(2,1)S(1)} %get-tuple-element.42), channel_id=1, source_target_pairs={{0,24},{4,100},{8,0},{12,108},{16,8},{20,116},{24,16},{28,124},{32... | collective-permute-start | bytes 786440 | tf_op jit(solution)/shard_map/ppermute | solution.py:47
  57.1 7.3 %collective-permute-start.5 = (bf16[1024,128]{1,0:T(8,128)(2,1)S(1)}, bf16[1024,128]{1,0:T(8,128)(2,1)S(1)}, u32[]{:S(2)}, u32[]{:S(2)}) collective-permute-start(bf16[1024,128]{1,0:T(8,128)(2,1)S(1)} %get-tuple-element.42), channel_id=1, source_target_pairs={{0,8},{4,36},{8,16},{12,44},{16,24},{20,52},{24,0},{28,60},{32,40}... | collective-permute-start | bytes 786440 | tf_op jit(solution)/shard_map/ppermute | solution.py:46
  64.3 6.2 %collective-permute-start.8 = (bf16[512,128]{1,0:T(8,128)(2,1)S(1)}, bf16[512,128]{1,0:T(8,128)(2,1)S(1)}, u32[]{:S(2)}, u32[]{:S(2)}) collective-permute-start(bf16[512,128]{1,0:T(8,128)(2,1)S(1)} %slice.151), channel_id=1, source_target_pairs={{0,24},{4,100},{8,0},{12,108},{16,8},{20,116},{24,16},{28,124},{32... | collective-permute-start | bytes 393224 | tf_op jit(solution)/shard_map/ppermute | solution.py:49
  64.4 5.8 %collective-permute-start.7 = (bf16[512,128]{1,0:T(8,128)(2,1)S(1)}, bf16[512,128]{1,0:T(8,128)(2,1)S(1)}, u32[]{:S(2)}, u32[]{:S(2)}) collective-permute-start(bf16[512,128]{1,0:T(8,128)(2,1)S(1)} %slice.150), channel_id=1, source_target_pairs={{0,8},{4,36},{8,16},{12,44},{16,24},{20,52},{24,0},{28,60},{32,40}... | collective-permute-start | bytes 393224 | tf_op jit(solution)/shard_map/ppermute | solution.py:48
  70.6 14.9 %collective-permute-start.10 = (bf16[4096,128]{1,0:T(8,128)(2,1)S(1)}, bf16[4096,128]{1,0:T(8,128)(2,1)S(1)}, u32[]{:S(2)}, u32[]{:S(2)}) collective-permute-start(bf16[4096,128]{1,0:T(8,128)(2,1)S(1)} %constant_dynamic-update-slice_fusion.12.refs_0_), channel_id=1, source_target_pairs={{0,96},{4,28},{8,104},{12,4},{16,112},{20,12},{24,120},{28,20},{32... | collective-permute-start | bytes 3145736 | tf_op jit(solution)/shard_map/ppermute | solution.py:47
  71.2 15.1 %collective-permute-start.9 = (bf16[4096,128]{1,0:T(8,128)(2,1)S(1)}, bf16[4096,128]{1,0:T(8,128)(2,1)S(1)}, u32[]{:S(2)}, u32[]{:S(2)}) collective-permute-start(bf16[4096,128]{1,0:T(8,128)(2,1)S(1)} %constant_dynamic-update-slice_fusion.12.refs_0_), channel_id=1, source_target_pairs={{0,32},{4,12},{8,40},{12,20},{16,48},{20,28},{24,56},{28,4},{32,64... | collective-permute-start | bytes 3145736 | tf_op jit(solution)/shard_map/ppermute | solution.py:46
  85.5 12.5 %copy-start.1 = (s32[16]{0:T(128)S(1)}, s32[16]{0:T(128)}, u32[]{:S(2)}) copy-start(s32[16]{0:T(128)} %lengths.5) | copy-start | bytes 196
  85.5 9.8 %collective-permute-start.12 = (bf16[2048,128]{1,0:T(8,128)(2,1)S(1)}, bf16[2048,128]{1,0:T(8,128)(2,1)S(1)}, u32[]{:S(2)}, u32[]{:S(2)}) collective-permute-start(bf16[2048,128]{1,0:T(8,128)(2,1)S(1)} %slice.153), channel_id=1, source_target_pairs={{0,96},{4,28},{8,104},{12,4},{16,112},{20,12},{24,120},{28,20},{32... | collective-permute-start | bytes 1572872 | tf_op jit(solution)/shard_map/ppermute | solution.py:49
  86.3 9.2 %collective-permute-start.11 = (bf16[2048,128]{1,0:T(8,128)(2,1)S(1)}, bf16[2048,128]{1,0:T(8,128)(2,1)S(1)}, u32[]{:S(2)}, u32[]{:S(2)}) collective-permute-start(bf16[2048,128]{1,0:T(8,128)(2,1)S(1)} %slice.152), channel_id=1, source_target_pairs={{0,32},{4,12},{8,40},{12,20},{16,48},{20,28},{24,56},{28,4},{32,64... | collective-permute-start | bytes 1572872 | tf_op jit(solution)/shard_map/ppermute | solution.py:48
  88.3 8.5 %collective-permute-start.13 = (bf16[4096,128]{1,0:T(8,128)(2,1)S(1)}, bf16[4096,128]{1,0:T(8,128)(2,1)S(1)}, u32[]{:S(2)}, u32[]{:S(2)}) collective-permute-start(bf16[4096,128]{1,0:T(8,128)(2,1)S(1)} %constant_dynamic-update-slice_fusion.12.refs_0_), channel_id=1, source_target_pairs={{0,4},{4,0},{8,12},{12,8},{16,20},{20,16},{24,28},{28,24},{32,36},... | collective-permute-start | bytes 3145736 | tf_op jit(solution)/shard_map/ppermute | solution.py:65
  88.3 9.7 %collective-permute-start.15 = (bf16[4096,128]{1,0:T(8,128)(2,1)S(1)}, bf16[4096,128]{1,0:T(8,128)(2,1)S(1)}, u32[]{:S(2)}, u32[]{:S(2)}) collective-permute-start(bf16[4096,128]{1,0:T(8,128)(2,1)S(1)} %collective-permute-done.10.refs_2_), channel_id=1, source_target_pairs={{0,4},{4,0},{8,12},{12,8},{16,20},{20,16},{24,28},{28,24},{32,36},... | collective-permute-start | bytes 3145736 | tf_op jit(solution)/shard_map/ppermute | solution.py:65
  88.8 9.2 %collective-permute-start.14 = (bf16[4096,128]{1,0:T(8,128)(2,1)S(1)}, bf16[4096,128]{1,0:T(8,128)(2,1)S(1)}, u32[]{:S(2)}, u32[]{:S(2)}) collective-permute-start(bf16[4096,128]{1,0:T(8,128)(2,1)S(1)} %collective-permute-done.9.refs_1_), channel_id=1, source_target_pairs={{0,4},{4,0},{8,12},{12,8},{16,20},{20,16},{24,28},{28,24},{32,36},... | collective-permute-start | bytes 3145736 | tf_op jit(solution)/shard_map/ppermute | solution.py:65
  95.3 1.9 %collective-permute-start.17 = (bf16[2048,128]{1,0:T(8,128)(2,1)S(1)}, bf16[2048,128]{1,0:T(8,128)(2,1)S(1)}, u32[]{:S(2)}, u32[]{:S(2)}) collective-permute-start(bf16[2048,128]{1,0:T(8,128)(2,1)S(1)} %collective-permute-done.12.refs_4_), channel_id=1, source_target_pairs={{0,4},{4,0},{8,12},{12,8},{16,20},{20,16},{24,28},{28,24},{32,36},... | collective-permute-start | bytes 1572872 | tf_op jit(solution)/shard_map/ppermute | solution.py:65
  95.6 2.4 %collective-permute-start.16 = (bf16[2048,128]{1,0:T(8,128)(2,1)S(1)}, bf16[2048,128]{1,0:T(8,128)(2,1)S(1)}, u32[]{:S(2)}, u32[]{:S(2)}) collective-permute-start(bf16[2048,128]{1,0:T(8,128)(2,1)S(1)} %collective-permute-done.11.refs_3_), channel_id=1, source_target_pairs={{0,4},{4,0},{8,12},{12,8},{16,20},{20,16},{24,28},{28,24},{32,36},... | collective-permute-start | bytes 1572872 | tf_op jit(solution)/shard_map/ppermute | solution.py:65
  98.0 14.4 %copy-start.3 = (bf16[512,4096]{1,0:T(8,128)(2,1)S(1)}, bf16[512,4096]{1,0:T(8,128)(2,1)}, u32[]{:S(2)}) copy-start(bf16[512,4096]{1,0:T(8,128)(2,1)} %param.13) | copy-start | bytes 12582916
  113.2 27.6 %collective-permute-start.19 = (bf16[128,2048]{1,0:T(8,128)(2,1)S(1)}, bf16[128,2048]{1,0:T(8,128)(2,1)S(1)}, u32[]{:S(2)}, u32[]{:S(2)}) collective-permute-start(bf16[128,2048]{1,0:T(8,128)(2,1)S(1)} %get-tuple-element.49), channel_id=1, source_target_pairs={{0,3},{1,0},{2,1},{3,2},{4,7},{5,4},{6,5},{7,6},{8,11},{9,8},{10,9... | collective-permute-start | bytes 1572872 | tf_op jit(solution)/shard_map/ppermute | solution.py:319
  113.3 27.5 %collective-permute-start.18 = (bf16[128,2048]{1,0:T(8,128)(2,1)S(1)}, bf16[128,2048]{1,0:T(8,128)(2,1)S(1)}, u32[]{:S(2)}, u32[]{:S(2)}) collective-permute-start(bf16[128,2048]{1,0:T(8,128)(2,1)S(1)} %get-tuple-element.50), channel_id=1, source_target_pairs={{0,1},{1,2},{2,3},{3,0},{4,5},{5,6},{6,7},{7,4},{8,9},{9,10},{10,1... | collective-permute-start | bytes 1572872 | tf_op jit(solution)/shard_map/ppermute | solution.py:318
  139.4 19.3 %collective-permute-start.21 = (bf16[128,2048]{1,0:T(8,128)(2,1)S(1)}, bf16[128,2048]{1,0:T(8,128)(2,1)S(1)}, u32[]{:S(2)}, u32[]{:S(2)}) collective-permute-start(bf16[128,2048]{1,0:T(8,128)(2,1)S(1)} %get-tuple-element.47), channel_id=1, source_target_pairs={{0,3},{1,0},{2,1},{3,2},{4,7},{5,4},{6,5},{7,6},{8,11},{9,8},{10,9... | collective-permute-start | bytes 1572872 | tf_op jit(solution)/shard_map/ppermute | solution.py:324
  141.1 17.6 %collective-permute-start.20 = (bf16[128,2048]{1,0:T(8,128)(2,1)S(1)}, bf16[128,2048]{1,0:T(8,128)(2,1)S(1)}, u32[]{:S(2)}, u32[]{:S(2)}) collective-permute-start(bf16[128,2048]{1,0:T(8,128)(2,1)S(1)} %get-tuple-element.39), channel_id=1, source_target_pairs={{0,1},{1,2},{2,3},{3,0},{4,5},{5,6},{6,7},{7,4},{8,9},{9,10},{10,1... | collective-permute-start | bytes 1572872 | tf_op jit(solution)/shard_map/ppermute | solution.py:328
  141.9 17.0 %collective-permute-start.22 = (bf16[128,2048]{1,0:T(8,128)(2,1)S(1)}, bf16[128,2048]{1,0:T(8,128)(2,1)S(1)}, u32[]{:S(2)}, u32[]{:S(2)}) collective-permute-start(bf16[128,2048]{1,0:T(8,128)(2,1)S(1)} %get-tuple-element.48), channel_id=1, source_target_pairs={{0,1},{1,2},{2,3},{3,0},{4,5},{5,6},{6,7},{7,4},{8,9},{9,10},{10,1... | collective-permute-start | bytes 1572872 | tf_op jit(solution)/shard_map/ppermute | solution.py:322
  142.0 16.9 %collective-permute-start.23 = (bf16[128,2048]{1,0:T(8,128)(2,1)S(1)}, bf16[128,2048]{1,0:T(8,128)(2,1)S(1)}, u32[]{:S(2)}, u32[]{:S(2)}) collective-permute-start(bf16[128,2048]{1,0:T(8,128)(2,1)S(1)} %get-tuple-element.40), channel_id=1, source_target_pairs={{0,3},{1,0},{2,1},{3,2},{4,7},{5,4},{6,5},{7,6},{8,11},{9,8},{10,9... | collective-permute-start | bytes 1572872 | tf_op jit(solution)/shard_map/ppermute | solution.py:329
  158.7 1.2 copy-start.5
where the time goes:
time: 162 us
  waiting for transfers between devices  57.5 us (35%)
  Pallas kernels  50.6 us (31%)
  starting transfers between devices  25 us (15%)
  matrix products  17.5 us (11%)
  other arithmetic  7.53 us (5%)
  local copies, waits for them, and re-layouts  2.96 us (2%)
    pallas_call x3, Pallas kernels, attend(): pl.pallas_call(functools.partial(attend_kernel, quarters=quarters), out_s...  50.6 us
    dot_general x15, matrix products, wide_dot(): return jnp.dot(a, b, preferred_element_type=jnp.float32)  17.5 us
    ppermute x2, waiting for transfers between devices, ring_gather(): ahead = lax.ppermute(piece, axis, shift(-1))  17.1 us
    ppermute x1, waiting for transfers between devices, body(): ahead = lax.ppermute(own, 'tensor', ring_shift(-1))  13.8 us
    ppermute x1, waiting for transfers between devices, body(): lower = lax.ppermute(ahead[half:], 'tensor', ring_shift(-1))  9.59 us
    ppermute x2, waiting for transfers between devices, ring_gather(): lower = lax.ppermute(ahead[half:], axis, shift(-1))  6.82 us
    ppermute x2, starting transfers between devices, ring_gather(): upper = lax.ppermute(behind[:half], axis, shift(1))  5.25 us
    ppermute x2, starting transfers between devices, ring_gather(): behind = lax.ppermute(piece, axis, shift(1))  4.32 us
  transfers between devices with their start and end apart: 24, of which 13 were waited for; matrix products, arithmetic and copies ran while one was open for 8% of the time, Pallas kernels for 22%

commit v1 on v0

--- a/solution.py
+++ b/solution.py
@@ -20,6 +20,7 @@
 
 RING = 4
 RELATIVE = (0, 3, 1, 2)
+KEY_ORDER = ((0, 0), (0, 1), (0, 2), (1, 0), (1, 1), (1, 2), (0, 3), (1, 3))
 
 
 def ring_shift(step):
@@ -58,11 +59,11 @@
         jnp.concatenate([keys, other], axis=0),
         jnp.concatenate([other, values], axis=0),
     )
-    line = ring_gather(mine, "dp", functools.partial(plane_shift, first_axis=True))
-    plane = ring_gather(
-        jnp.concatenate(line, axis=0), "dp", functools.partial(plane_shift, first_axis=False)
-    )
-    return plane, [lax.ppermute(piece, "dp", CORE_SWAP) for piece in plane]
+    shift = functools.partial(plane_shift, first_axis=True)
+    line = ring_gather(mine, "dp", shift)
+    shift = functools.partial(plane_shift, first_axis=False)
+    plane = ring_gather(jnp.concatenate(line, axis=0), "dp", shift)
+    return plane + [lax.ppermute(piece, "dp", CORE_SWAP) for piece in plane]
 
 
 def doc_starts(lengths, positions):
@@ -93,9 +94,8 @@
 
 
 def attend_kernel(ids, lengths, query, cos_part, sin_part, *refs, quarters):
-    pieces, refs = refs[:10], refs[10:]
+    bulk, rest, refs = refs[:10], refs[10:20], refs[20:]
     out, rows, peak, summed, starts, query_at, key_at, block, sems = refs
-    own_planes, swapped = pieces[:5], pieces[5:]
     count = query.shape[0]
     heads = query.shape[1] // HEAD_SIZE
     size = block.shape[2]
@@ -133,25 +133,25 @@
         at_x, at_z = place(((chip >> 2) - own_x) & 3), place(((chip & 3) - own_z) & 3)
         outer = jnp.where(core == 0, at_x, at_z)
         inner = jnp.where(core == 0, at_z, at_x)
-        for sources, kind, major, minor in (
-            (own_planes, core, outer, inner),
-            (swapped, 1 - core, inner, outer),
-        ):
+        for side, kind, major, minor in ((0, core, outer, inner), (5, 1 - core, inner, outer)):
             index = jnp.where((major == 3) & (minor >= 2), 4, major)
-            row = pl.multiple_of(jnp.where(major == 3, minor & 1, minor) * size, size)
-            for n, source in enumerate(sources):
+            line = jnp.where(major == 3, minor & 1, minor)
+            for n in range(5):
 
                 @pl.when(index == n)
                 def _():
-                    pltpu.make_async_copy(
-                        source.at[pl.ds(row, size)], block.at[slot, kind], sems.at[slot, kind]
-                    ).start()
+                    for sources, at, length in ((bulk, 0, 6 * span), (rest, 6 * span, 2 * span)):
+                        pltpu.make_async_copy(
+                            sources[side + n].at[pl.ds(pl.multiple_of(line * length, length), length)],
+                            block.at[slot, kind, at : at + length],
+                            sems.at[slot, kind],
+                        ).start()
 
     def wait_copies(chip):
         slot = chip & 1
         for kind in range(2):
             pltpu.make_async_copy(
-                own_planes[0].at[pl.ds(0, size)], block.at[slot, kind], sems.at[slot, kind]
+                bulk[0].at[pl.ds(0, size)], block.at[slot, kind], sems.at[slot, kind]
             ).wait()
 
     start_copies(low)
@@ -164,8 +164,8 @@
         at = base + lax.broadcasted_iota(jnp.int32, (span, 1), 0)
         query_at[i * span : (i + 1) * span, :] = at
         starts[i * span : (i + 1) * span, :] = start_of(at)
-    for i in range(size // span):
-        base = (i // RING) * (RING * span) + quarter_base(i % RING)
+    for i, (half, quarter) in enumerate(KEY_ORDER):
+        base = half * (RING * span) + quarter_base(quarter)
         lane = lax.broadcasted_iota(jnp.int32, (1, span), 1)
         key_at[:, i * span : (i + 1) * span] = base + lane
     peak[...] = jnp.full(peak.shape, initial_peak, jnp.float32)
@@ -237,7 +237,7 @@
     return pl.pallas_call(
         functools.partial(attend_kernel, quarters=quarters),
         out_shape=jax.ShapeDtypeStruct((count, width), jnp.bfloat16),
-        in_specs=[smem, smem, vmem, vmem, vmem] + [hbm] * 10,
+        in_specs=[smem, smem, vmem, vmem, vmem] + [hbm] * 20,
         out_specs=vmem,
         scratch_shapes=[
             pltpu.VMEM((rows, HEAD_SIZE), jnp.bfloat16),
@@ -249,7 +249,7 @@
             pltpu.VMEM((2, 2, size, HEAD_SIZE), jnp.bfloat16),
             pltpu.SemaphoreType.DMA((2, 2)),
         ],
-        compiler_params=pltpu.CompilerParams(vmem_limit_bytes=32 * 2**20),
+        compiler_params=pltpu.CompilerParams(vmem_limit_bytes=56 * 2**20),
         cost_estimate=pl.CostEstimate(
             flops=rows * 4096 * 512, transcendentals=rows * 4096, bytes_accessed=4 << 20
         ),
@@ -274,34 +274,35 @@
         value = wide_dot(piece, value_weight)
         return key.astype(jnp.bfloat16), value.astype(jnp.bfloat16)
 
-    own = normed
-    behind = lax.ppermute(own, "tensor", ring_shift(1))
-    ahead = lax.ppermute(own, "tensor", ring_shift(-1))
+    half = count // 2
     query = [None] * RING
     keys, values = [None] * RING, [None] * RING
-    keys[0], values[0] = project(own, 0)
-    query[0] = wide_dot(own, w_query)
-    behind, ahead, query[0], keys[0], values[0] = lax.optimization_barrier(
-        (behind, ahead, query[0], keys[0], values[0])
+    keys[0], values[0] = project(normed, 0)
+    query[0] = wide_dot(normed, w_query)
+    behind_top = lax.ppermute(normed[:half], "tensor", ring_shift(1))
+    ahead_low = lax.ppermute(normed[half:], "tensor", ring_shift(-1))
+    behind_low = lax.ppermute(normed[half:], "tensor", ring_shift(1))
+    ahead_top = lax.ppermute(normed[:half], "tensor", ring_shift(-1))
+    far_top = lax.ppermute(behind_top, "tensor", ring_shift(1))
+    far_low = lax.ppermute(ahead_low, "tensor", ring_shift(-1))
+    behind_low, ahead_top, query[0], keys[0], values[0] = lax.optimization_barrier(
+        (behind_low, ahead_top, query[0], keys[0], values[0])
     )
-    half = count // 2
-    upper = lax.ppermute(behind[:half], "tensor", ring_shift(1))
-    lower = lax.ppermute(ahead[half:], "tensor", ring_shift(-1))
+    behind = jnp.concatenate([behind_top, behind_low], axis=0)
+    ahead = jnp.concatenate([ahead_top, ahead_low], axis=0)
     keys[1], values[1] = project(behind, 1)
     keys[2], values[2] = project(ahead, 2)
     query[1] = wide_dot(behind, w_query)
     query[2] = wide_dot(ahead, w_query)
-    upper, lower, query[1], query[2], keys[1], values[1], keys[2], values[2] = (
-        lax.optimization_barrier(
-            (upper, lower, query[1], query[2], keys[1], values[1], keys[2], values[2])
-        )
+    bulk = gather_plane(jnp.concatenate(keys[:3], axis=0), jnp.concatenate(values[:3], axis=0))
+    far_top, far_low, query[1], query[2] = lax.optimization_barrier(
+        (far_top, far_low, query[1], query[2])
     )
-    far = jnp.concatenate([upper, lower], axis=0)
+    far = jnp.concatenate([far_top, far_low], axis=0)
     keys[3], values[3] = project(far, 3)
-    pieces = gather_plane(jnp.concatenate(keys, axis=0), jnp.concatenate(values, axis=0))
+    rest = gather_plane(keys[3], values[3])
     query[3] = wide_dot(far, w_query)
-    plane, swapped = pieces
-    pieces = list(plane) + list(swapped)
+    pieces = bulk + rest
 
     def branch(quarters, after=None):
         at = slice(quarters[0] * count, (quarters[-1] + 1) * count)

time: 162 us -> 174 us (1.074)
  the two profiles are of different devices: /device:TPU:100 before, /device:TPU:68 now
where the time goes in v1:
time: 174 us; the launch traced here: 173 us
  Pallas kernels  47.5 us (27%)
  starting transfers between devices  44.4 us (26%)
  waiting for transfers between devices  42.4 us (24%)
  matrix products  15.7 us (9%)
  local copies, waits for them, and re-layouts  11.7 us (7%)
  other arithmetic  10.9 us (6%)
    pallas_call x3, Pallas kernels, attend(): pl.pallas_call(functools.partial(attend_kernel, quarters=quarters), out_s...  47.5 us
    dot_general x15, matrix products, wide_dot(): return jnp.dot(a, b, preferred_element_type=jnp.float32)  15.7 us
    ppermute x4, starting transfers between devices, ring_gather(): upper = lax.ppermute(behind[:half], axis, shift(1))  10.6 us
    ppermute x1, waiting for transfers between devices, body(): behind_low = lax.ppermute(normed[half:], 'tensor', ring_shift(1))  9.8 us
    ppermute x4, waiting for transfers between devices, ring_gather(): ahead = lax.ppermute(piece, axis, shift(-1))  8.33 us
    ppermute x1, waiting for transfers between devices, body(): plain_up = lax.ppermute(plain_up, 'tensor', ring_shift(1))  7.82 us
    ppermute x4, starting transfers between devices, ring_gather(): behind = lax.ppermute(piece, axis, shift(1))  7.37 us
    unnamed x69, local copies, waits for them, and re-layouts  5.5 us
  transfers between devices with their start and end apart: 40, of which 13 were waited for; matrix products, arithmetic and copies ran while one was open for 14% of the time, Pallas kernels for 19%

profile of v1, /device:TPU:68, one launch (start us, length us, event | category | flops | bytes accessed | tf_op | source)
XLA Modules:
  0.0 173.2 jit_solution(11944359752484402525)
XLA Ops:
  0.0 1.7 fusion.2
  5.9 1.7 collective-permute-start.1
  7.5 1.8 %collective-permute-start.4 = (bf16[64,4096]{1,0:T(8,128)(2,1)}, bf16[64,4096]{1,0:T(8,128)(2,1)}, u32[]{:S(2)}, u32[]{:S(2)}) collective-permute-start(bf16[64,4096]{1,0:T(8,128)(2,1)} %get-tuple-element.46), channel_id=1, source_target_pairs={{0,3},{1,0},{2,1},{3,2},{4,7},{5,4},{6,5},{7,6},{8,11},{9,8},{10,9... | collective-permute-start | bytes 1572872 | tf_op jit(solution)/shard_map/ppermute | solution.py:283
  10.4 3.6 %fusion.26.query = f32[128,512]{1,0:T(8,128)} fusion(bf16[128,4096]{1,0:T(8,128)(2,1)S(1)} %fusion.4, bf16[4096,512]{1,0:T(8,128)(2,1)} %param.10), kind=kOutput, calls=%fused_computation.76 | convolution fusion | flops 536870912 | bytes 5505024 | tf_op jit(solution)/shard_map/dot_general | solution.py:93
  16.4 4.6 %collective-permute-done.1 = bf16[64,4096]{1,0:T(8,128)(2,1)} collective-permute-done((bf16[64,4096]{1,0:T(8,128)(2,1)}, bf16[64,4096]{1,0:T(8,128)(2,1)}, u32[]{:S(2)}, u32[]{:S(2)}) %collective-permute-start.1) | collective-permute-done | bytes 524320 | tf_op jit(solution)/shard_map/ppermute | solution.py:285
  21.0 9.8 %collective-permute-done = bf16[64,4096]{1,0:T(8,128)(2,1)} collective-permute-done((bf16[64,4096]{1,0:T(8,128)(2,1)}, bf16[64,4096]{1,0:T(8,128)(2,1)}, u32[]{:S(2)}, u32[]{:S(2)}) %collective-permute-start) | collective-permute-done | bytes 524320 | tf_op jit(solution)/shard_map/ppermute | solution.py:284
  39.0 2.7 %collective-permute-start.5 = (bf16[64,4096]{1,0:T(8,128)(2,1)}, bf16[64,4096]{1,0:T(8,128)(2,1)S(1)}, u32[]{:S(2)}, u32[]{:S(2)}) collective-permute-start(bf16[64,4096]{1,0:T(8,128)(2,1)} %collective-permute-done.4), channel_id=1, source_target_pairs={{0,3},{1,0},{2,1},{3,2},{4,7},{5,4},{6,5},{7,6},{8,11},{9,8},{10,9... | collective-permute-start | bytes 1572872 | tf_op jit(solution)/shard_map/ppermute | solution.py:287
  42.0 1.9 %collective-permute-start.7 = (bf16[768,128]{1,0:T(8,128)(2,1)S(1)}, bf16[768,128]{1,0:T(8,128)(2,1)S(1)}, u32[]{:S(2)}, u32[]{:S(2)}) collective-permute-start(bf16[768,128]{1,0:T(8,128)(2,1)S(1)} %get-tuple-element.38), channel_id=1, source_target_pairs={{0,8},{4,36},{8,16},{12,44},{16,24},{20,52},{24,0},{28,60},{32,40}... | collective-permute-start | bytes 589832 | tf_op jit(solution)/shard_map/ppermute | solution.py:47
  44.6 2.9 %collective-permute-done.8 = bf16[768,128]{1,0:T(8,128)(2,1)S(1)} collective-permute-done((bf16[768,128]{1,0:T(8,128)(2,1)S(1)}, bf16[768,128]{1,0:T(8,128)(2,1)S(1)}, u32[]{:S(2)}, u32[]{:S(2)}) %collective-permute-start.8) | collective-permute-done | bytes 196640 | tf_op jit(solution)/shard_map/ppermute | solution.py:48
  47.7 2.8 %collective-permute-start.9 = (bf16[384,128]{1,0:T(8,128)(2,1)S(1)}, bf16[384,128]{1,0:T(8,128)(2,1)S(1)}, u32[]{:S(2)}, u32[]{:S(2)}) collective-permute-start(bf16[384,128]{1,0:T(8,128)(2,1)S(1)} %slice.168), channel_id=1, source_target_pairs={{0,8},{4,36},{8,16},{12,44},{16,24},{20,52},{24,0},{28,60},{32,40}... | collective-permute-start | bytes 294920 | tf_op jit(solution)/shard_map/ppermute | solution.py:49
  50.6 3.6 %collective-permute-done.3 = bf16[64,4096]{1,0:T(8,128)(2,1)S(1)} collective-permute-done((bf16[64,4096]{1,0:T(8,128)(2,1)}, bf16[64,4096]{1,0:T(8,128)(2,1)S(1)}, u32[]{:S(2)}, u32[]{:S(2)}) %collective-permute-start.3) | collective-permute-done | bytes 524320 | tf_op jit(solution)/shard_map/ppermute | solution.py:286
  57.0 1.9 %collective-permute-start.21 = (bf16[256,128]{1,0:T(8,128)(2,1)S(1)}, bf16[256,128]{1,0:T(8,128)(2,1)S(1)}, u32[]{:S(2)}, u32[]{:S(2)}) collective-permute-start(bf16[256,128]{1,0:T(8,128)(2,1)S(1)} %get-tuple-element.34), channel_id=1, source_target_pairs={{0,8},{4,36},{8,16},{12,44},{16,24},{20,52},{24,0},{28,60},{32,40}... | collective-permute-start | bytes 196616 | tf_op jit(solution)/shard_map/ppermute | solution.py:47
  61.5 2.5 %collective-permute-start.23 = (bf16[128,128]{1,0:T(8,128)(2,1)S(1)}, bf16[128,128]{1,0:T(8,128)(2,1)S(1)}, u32[]{:S(2)}, u32[]{:S(2)}) collective-permute-start(bf16[128,128]{1,0:T(8,128)(2,1)S(1)} %slice.174), channel_id=1, source_target_pairs={{0,8},{4,36},{8,16},{12,44},{16,24},{20,52},{24,0},{28,60},{32,40}... | collective-permute-start | bytes 98312 | tf_op jit(solution)/shard_map/ppermute | solution.py:49
  64.1 1.7 %collective-permute-done.23 = bf16[128,128]{1,0:T(8,128)(2,1)S(1)} collective-permute-done((bf16[128,128]{1,0:T(8,128)(2,1)S(1)}, bf16[128,128]{1,0:T(8,128)(2,1)S(1)}, u32[]{:S(2)}, u32[]{:S(2)}) %collective-permute-start.23) | collective-permute-done | bytes 32800 | tf_op jit(solution)/shard_map/ppermute | solution.py:49
  66.8 2.0 %collective-permute-start.25 = (bf16[1024,128]{1,0:T(8,128)(2,1)S(1)}, bf16[1024,128]{1,0:T(8,128)(2,1)S(1)}, u32[]{:S(2)}, u32[]{:S(2)}) collective-permute-start(bf16[1024,128]{1,0:T(8,128)(2,1)S(1)} %constant_dynamic-update-slice_fusion.11.refs_10_), channel_id=1, source_target_pairs={{0,32},{4,12},{8,40},{12,20},{16,48},{20,28},{24,56},{28,4},{32,64... | collective-permute-start | bytes 786440 | tf_op jit(solution)/shard_map/ppermute | solution.py:47
  68.8 5.4 %collective-permute-done.26.refs_12_ = bf16[1024,128]{1,0:T(8,128)(2,1)S(1)} collective-permute-done((bf16[1024,128]{1,0:T(8,128)(2,1)S(1)}, bf16[1024,128]{1,0:T(8,128)(2,1)S(1)}, u32[]{:S(2)}, u32[]{:S(2)}) %collective-permute-start.26) | collective-permute-done | bytes 262176 | tf_op jit(solution)/shard_map/ppermute | solution.py:48
  74.9 1.8 %collective-permute-start.28 = (bf16[512,128]{1,0:T(8,128)(2,1)S(1)}, bf16[512,128]{1,0:T(8,128)(2,1)S(1)}, u32[]{:S(2)}, u32[]{:S(2)}) collective-permute-start(bf16[512,128]{1,0:T(8,128)(2,1)S(1)} %slice.177), channel_id=1, source_target_pairs={{0,96},{4,28},{8,104},{12,4},{16,112},{20,12},{24,120},{28,20},{32... | collective-permute-start | bytes 393224 | tf_op jit(solution)/shard_map/ppermute | solution.py:50
  76.8 3.6 %collective-permute-done.28.refs_14_ = bf16[512,128]{1,0:T(8,128)(2,1)S(1)} collective-permute-done((bf16[512,128]{1,0:T(8,128)(2,1)S(1)}, bf16[512,128]{1,0:T(8,128)(2,1)S(1)}, u32[]{:S(2)}, u32[]{:S(2)}) %collective-permute-start.28) | collective-permute-done | bytes 131104 | tf_op jit(solution)/shard_map/ppermute | solution.py:50
  80.4 3.2 %collective-permute-start.27 = (bf16[512,128]{1,0:T(8,128)(2,1)S(1)}, bf16[512,128]{1,0:T(8,128)(2,1)S(1)}, u32[]{:S(2)}, u32[]{:S(2)}) collective-permute-start(bf16[512,128]{1,0:T(8,128)(2,1)S(1)} %slice.176), channel_id=1, source_target_pairs={{0,32},{4,12},{8,40},{12,20},{16,48},{20,28},{24,56},{28,4},{32,64... | collective-permute-start | bytes 393224 | tf_op jit(solution)/shard_map/ppermute | solution.py:49
  83.9 2.1 %collective-permute-start.13 = (bf16[1536,128]{1,0:T(8,128)(2,1)S(1)}, bf16[1536,128]{1,0:T(8,128)(2,1)S(1)}, u32[]{:S(2)}, u32[]{:S(2)}) collective-permute-start(bf16[1536,128]{1,0:T(8,128)(2,1)S(1)} %slice.170), channel_id=1, source_target_pairs={{0,32},{4,12},{8,40},{12,20},{16,48},{20,28},{24,56},{28,4},{32,64... | collective-permute-start | bytes 1179656 | tf_op jit(solution)/shard_map/ppermute | solution.py:49
  91.8 2.0 %collective-permute-start.18 = (bf16[1536,128]{1,0:T(8,128)(2,1)S(1)}, bf16[1536,128]{1,0:T(8,128)(2,1)S(1)}, u32[]{:S(2)}, u32[]{:S(2)}) collective-permute-start(bf16[1536,128]{1,0:T(8,128)(2,1)S(1)} %collective-permute-done.13.refs_3_), channel_id=1, source_target_pairs={{0,4},{4,0},{8,12},{12,8},{16,20},{20,16},{24,28},{28,24},{32,36},... | collective-permute-start | bytes 1179656 | tf_op jit(solution)/shard_map/ppermute | solution.py:66
  98.4 13.9 %attend.3 = bf16[128,512]{1,0:T(8,128)(2,1)} custom-call(s32[2]{0:T(128)} %pad_add_fusion.ids, s32[16]{0:T(128)} %lengths.5, f32[128,512]{1,0:T(8,128)} %fusion.30.query, f32[128,128]{1,0:T(8,128)} %get-tuple-element.52.cos_part, f32[128,128]{1,0:T(8,128)} %get-tuple-element.53.sin_part, bf16[3072,128]{1,0:T(8,128)(2,1)} %copy-done.7, ...), custom_call_target="tpu_custom_call" | custom-call | flops 1073741824 | bytes 4194304 | tf_op jit(solution)/shard_map/attend/pallas_call | solution.py:237
  112.3 1.6 convolution_convert_fusion
  114.0 3.0 %collective-permute-start.35 = (bf16[128,2048]{1,0:T(8,128)(2,1)S(1)}, bf16[128,2048]{1,0:T(8,128)(2,1)}, u32[]{:S(2)}, u32[]{:S(2)}) collective-permute-start(bf16[128,2048]{1,0:T(8,128)(2,1)S(1)} %get-tuple-element.43), channel_id=1, source_target_pairs={{0,3},{1,0},{2,1},{3,2},{4,7},{5,4},{6,5},{7,6},{8,11},{9,8},{10,9... | collective-permute-start | bytes 1572872 | tf_op jit(solution)/shard_map/ppermute | solution.py:320
  117.1 19.9 %attend.4 = bf16[256,512]{1,0:T(8,128)(2,1)} custom-call(s32[2]{0:T(128)} %pad_add_fusion.ids, s32[16]{0:T(128)} %lengths.5, f32[256,512]{1,0:T(8,128)} %pad_maximum_fusion.query, f32[256,128]{1,0:T(8,128)} %slice.178.cos_part, f32[256,128]{1,0:T(8,128)} %slice.179.sin_part, bf16[3072,128]{1,0:T(8,128)(2,1)} %copy-done.7, bf16[3072,128]{1,0:T(8,128)(2,1)} %copy-done.5, ...), custom_call_target="tpu_custom_call" | custom-call | flops 2147483648 | bytes 4194304 | tf_op jit(solution)/shard_map/attend/pallas_call | solution.py:237
  137.0 2.2 %fusion.25 = (bf16[256,4096]{1,0:T(8,128)(2,1)S(1)}, f32[256,4096]{1,0:T(8,128)S(1)}) fusion(bf16[256,512]{1,0:T(8,128)(2,1)} %attend.4, bf16[512,4096]{1,0:T(8,128)(2,1)S(1)} %copy-done.2), kind=kOutput, calls=%fused_computation.75 | convolution fusion | flops 1074790400 | bytes 10747904 | tf_op jit(solution)/shard_map/dot_general | solution.py:93
  139.3 3.3 %collective-permute-start.37 = (bf16[128,2048]{1,0:T(8,128)(2,1)S(1)}, bf16[128,2048]{1,0:T(8,128)(2,1)S(1)}, u32[]{:S(2)}, u32[]{:S(2)}) collective-permute-start(bf16[128,2048]{1,0:T(8,128)(2,1)S(1)} %get-tuple-element.41), channel_id=1, source_target_pairs={{0,3},{1,0},{2,1},{3,2},{4,7},{5,4},{6,5},{7,6},{8,11},{9,8},{10,9... | collective-permute-start | bytes 1572872 | tf_op jit(solution)/shard_map/ppermute | solution.py:325
  142.6 2.5 %fusion.5 = (bf16[128,2048]{1,0:T(8,128)(2,1)}, bf16[128,2048]{1,0:T(8,128)(2,1)}) fusion(f32[256,4096]{1,0:T(8,128)S(1)} %get-tuple-element.66, bf16[128,2048]{1,0:T(8,128)(2,1)} %collective-permute-done.35, bf16[128,2048]{1,0:T(8,128)(2,1)} %collective-permute-done.34), kind=kLoop, calls=%fused_computation.14 | loop fusion | flops 1572864 | bytes 4194304 | tf_op jit(solution)/shard_map/convert_element_type | solution.py:327
  145.1 3.3 %collective-permute-start.39 = (bf16[128,2048]{1,0:T(8,128)(2,1)}, bf16[128,2048]{1,0:T(8,128)(2,1)S(1)}, u32[]{:S(2)}, u32[]{:S(2)}) collective-permute-start(bf16[128,2048]{1,0:T(8,128)(2,1)} %get-tuple-element.32), channel_id=1, source_target_pairs={{0,3},{1,0},{2,1},{3,2},{4,7},{5,4},{6,5},{7,6},{8,11},{9,8},{10,9... | collective-permute-start | bytes 1572872 | tf_op jit(solution)/shard_map/ppermute | solution.py:330
  148.4 13.6 %attend.5 = bf16[128,512]{1,0:T(8,128)(2,1)} custom-call(s32[2]{0:T(128)} %pad_add_fusion.ids, s32[16]{0:T(128)} %lengths.5, f32[128,512]{1,0:T(8,128)} %fusion.26.query, f32[128,128]{1,0:T(8,128)} %get-tuple-element.51.cos_part, f32[128,128]{1,0:T(8,128)} %get-tuple-element.49.sin_part, bf16[3072,128]{1,0:T(8,128)(2,1)} %copy-done.7, ...), custom_call_target="tpu_custom_call" | custom-call | flops 1073741824 | bytes 4194304 | tf_op jit(solution)/shard_map/attend/pallas_call | solution.py:237
  163.3 7.8 %collective-permute-done.38 = bf16[128,2048]{1,0:T(8,128)(2,1)S(1)} collective-permute-done((bf16[128,2048]{1,0:T(8,128)(2,1)S(1)}, bf16[128,2048]{1,0:T(8,128)(2,1)S(1)}, u32[]{:S(2)}, u32[]{:S(2)}) %collective-permute-start.38) | collective-permute-done | bytes 524320 | tf_op jit(solution)/shard_map/ppermute | solution.py:323
  171.3 1.9 %fusion.1 = bf16[128,4096]{1,0:T(8,128)(2,1)} fusion(bf16[128,512]{1,0:T(8,128)(2,1)S(1)} %copy-done.27, bf16[512,4096]{1,0:T(8,128)(2,1)S(1)} %copy-done.2, bf16[128,4096]{1,0:T(8,128)(2,1)S(1)} %copy-done.6, f32[128,2048]{1,0:T(8,128)S(1)} %convert_add_fusion, f32[128,2048]{1,0:T(8,128)S(1)} %convert_add_fusion.1), kind=kOutput, calls=%fused_computation.2 | convolution fusion | flops 539492352 | bytes 8519680 | tf_op jit(solution)/shard_map/dot_general | solution.py:93
  (177 shorter events, 35.8 us)
Async XLA Ops:
  4.3 29.6 %collective-permute-start.2 = (bf16[64,4096]{1,0:T(8,128)(2,1)}, bf16[64,4096]{1,0:T(8,128)(2,1)}, u32[]{:S(2)}, u32[]{:S(2)}) collective-permute-start(bf16[64,4096]{1,0:T(8,128)(2,1)} %get-tuple-element.45), channel_id=1, source_target_pairs={{0,1},{1,2},{2,3},{3,0},{4,5},{5,6},{6,7},{7,4},{8,9},{9,10},{10,1... | collective-permute-start | bytes 1572872 | tf_op jit(solution)/shard_map/ppermute | solution.py:282
  5.9 15.1 %collective-permute-start.1 = (bf16[64,4096]{1,0:T(8,128)(2,1)}, bf16[64,4096]{1,0:T(8,128)(2,1)}, u32[]{:S(2)}, u32[]{:S(2)}) collective-permute-start(bf16[64,4096]{1,0:T(8,128)(2,1)} %get-tuple-element.45), channel_id=1, source_target_pairs={{0,3},{1,0},{2,1},{3,2},{4,7},{5,4},{6,5},{7,6},{8,11},{9,8},{10,9... | collective-permute-start | bytes 1572872 | tf_op jit(solution)/shard_map/ppermute | solution.py:285
  7.5 24.3 %collective-permute-start.4 = (bf16[64,4096]{1,0:T(8,128)(2,1)}, bf16[64,4096]{1,0:T(8,128)(2,1)}, u32[]{:S(2)}, u32[]{:S(2)}) collective-permute-start(bf16[64,4096]{1,0:T(8,128)(2,1)} %get-tuple-element.46), channel_id=1, source_target_pairs={{0,3},{1,0},{2,1},{3,2},{4,7},{5,4},{6,5},{7,6},{8,11},{9,8},{10,9... | collective-permute-start | bytes 1572872 | tf_op jit(solution)/shard_map/ppermute | solution.py:283
  9.3 21.4 %collective-permute-start = (bf16[64,4096]{1,0:T(8,128)(2,1)}, bf16[64,4096]{1,0:T(8,128)(2,1)}, u32[]{:S(2)}, u32[]{:S(2)}) collective-permute-start(bf16[64,4096]{1,0:T(8,128)(2,1)} %get-tuple-element.46), channel_id=1, source_target_pairs={{0,1},{1,2},{2,3},{3,0},{4,5},{5,6},{6,7},{7,4},{8,9},{9,10},{10,1... | collective-permute-start | bytes 1572872 | tf_op jit(solution)/shard_map/ppermute | solution.py:284
  38.4 15.8 %collective-permute-start.3 = (bf16[64,4096]{1,0:T(8,128)(2,1)}, bf16[64,4096]{1,0:T(8,128)(2,1)S(1)}, u32[]{:S(2)}, u32[]{:S(2)}) collective-permute-start(bf16[64,4096]{1,0:T(8,128)(2,1)} %collective-permute-done.2), channel_id=1, source_target_pairs={{0,1},{1,2},{2,3},{3,0},{4,5},{5,6},{6,7},{7,4},{8,9},{9,10},{10,1... | collective-permute-start | bytes 1572872 | tf_op jit(solution)/shard_map/ppermute | solution.py:286
  39.0 15.2 %collective-permute-start.5 = (bf16[64,4096]{1,0:T(8,128)(2,1)}, bf16[64,4096]{1,0:T(8,128)(2,1)S(1)}, u32[]{:S(2)}, u32[]{:S(2)}) collective-permute-start(bf16[64,4096]{1,0:T(8,128)(2,1)} %collective-permute-done.4), channel_id=1, source_target_pairs={{0,3},{1,0},{2,1},{3,2},{4,7},{5,4},{6,5},{7,6},{8,11},{9,8},{10,9... | collective-permute-start | bytes 1572872 | tf_op jit(solution)/shard_map/ppermute | solution.py:287
  41.8 5.7 %collective-permute-start.8 = (bf16[768,128]{1,0:T(8,128)(2,1)S(1)}, bf16[768,128]{1,0:T(8,128)(2,1)S(1)}, u32[]{:S(2)}, u32[]{:S(2)}) collective-permute-start(bf16[768,128]{1,0:T(8,128)(2,1)S(1)} %get-tuple-element.38), channel_id=1, source_target_pairs={{0,24},{4,100},{8,0},{12,108},{16,8},{20,116},{24,16},{28,124},{32... | collective-permute-start | bytes 589832 | tf_op jit(solution)/shard_map/ppermute | solution.py:48
  42.0 5.8 %collective-permute-start.7 = (bf16[768,128]{1,0:T(8,128)(2,1)S(1)}, bf16[768,128]{1,0:T(8,128)(2,1)S(1)}, u32[]{:S(2)}, u32[]{:S(2)}) collective-permute-start(bf16[768,128]{1,0:T(8,128)(2,1)S(1)} %get-tuple-element.38), channel_id=1, source_target_pairs={{0,8},{4,36},{8,16},{12,44},{16,24},{20,52},{24,0},{28,60},{32,40}... | collective-permute-start | bytes 589832 | tf_op jit(solution)/shard_map/ppermute | solution.py:47
  47.5 11.3 %collective-permute-start.10 = (bf16[384,128]{1,0:T(8,128)(2,1)S(1)}, bf16[384,128]{1,0:T(8,128)(2,1)S(1)}, u32[]{:S(2)}, u32[]{:S(2)}) collective-permute-start(bf16[384,128]{1,0:T(8,128)(2,1)S(1)} %slice.169), channel_id=1, source_target_pairs={{0,24},{4,100},{8,0},{12,108},{16,8},{20,116},{24,16},{28,124},{32... | collective-permute-start | bytes 294920 | tf_op jit(solution)/shard_map/ppermute | solution.py:50
  47.7 7.7 %collective-permute-start.9 = (bf16[384,128]{1,0:T(8,128)(2,1)S(1)}, bf16[384,128]{1,0:T(8,128)(2,1)S(1)}, u32[]{:S(2)}, u32[]{:S(2)}) collective-permute-start(bf16[384,128]{1,0:T(8,128)(2,1)S(1)} %slice.168), channel_id=1, source_target_pairs={{0,8},{4,36},{8,16},{12,44},{16,24},{20,52},{24,0},{28,60},{32,40}... | collective-permute-start | bytes 294920 | tf_op jit(solution)/shard_map/ppermute | solution.py:49
  58.9 27.4 %collective-permute-start.15 = (bf16[3072,128]{1,0:T(8,128)(2,1)S(1)}, bf16[3072,128]{1,0:T(8,128)(2,1)S(1)}, u32[]{:S(2)}, u32[]{:S(2)}) collective-permute-start(bf16[3072,128]{1,0:T(8,128)(2,1)S(1)} %constant_dynamic-update-slice_fusion.6.refs_0_), channel_id=1, source_target_pairs={{0,4},{4,0},{8,12},{12,8},{16,20},{20,16},{24,28},{28,24},{32,36},... | collective-permute-start | bytes 2359304 | tf_op jit(solution)/shard_map/ppermute | solution.py:66
  59.0 24.6 %collective-permute-start.12 = (bf16[3072,128]{1,0:T(8,128)(2,1)S(1)}, bf16[3072,128]{1,0:T(8,128)(2,1)S(1)}, u32[]{:S(2)}, u32[]{:S(2)}) collective-permute-start(bf16[3072,128]{1,0:T(8,128)(2,1)S(1)} %constant_dynamic-update-slice_fusion.6.refs_0_), channel_id=1, source_target_pairs={{0,96},{4,28},{8,104},{12,4},{16,112},{20,12},{24,120},{28,20},{32... | collective-permute-start | bytes 2359304 | tf_op jit(solution)/shard_map/ppermute | solution.py:48
  59.6 24.1 %collective-permute-start.11 = (bf16[3072,128]{1,0:T(8,128)(2,1)S(1)}, bf16[3072,128]{1,0:T(8,128)(2,1)S(1)}, u32[]{:S(2)}, u32[]{:S(2)}) collective-permute-start(bf16[3072,128]{1,0:T(8,128)(2,1)S(1)} %constant_dynamic-update-slice_fusion.6.refs_0_), channel_id=1, source_target_pairs={{0,32},{4,12},{8,40},{12,20},{16,48},{20,28},{24,56},{28,4},{32,64... | collective-permute-start | bytes 2359304 | tf_op jit(solution)/shard_map/ppermute | solution.py:47
  61.1 5.1 %collective-permute-start.24 = (bf16[128,128]{1,0:T(8,128)(2,1)S(1)}, bf16[128,128]{1,0:T(8,128)(2,1)S(1)}, u32[]{:S(2)}, u32[]{:S(2)}) collective-permute-start(bf16[128,128]{1,0:T(8,128)(2,1)S(1)} %slice.175), channel_id=1, source_target_pairs={{0,24},{4,100},{8,0},{12,108},{16,8},{20,116},{24,16},{28,124},{32... | collective-permute-start | bytes 98312 | tf_op jit(solution)/shard_map/ppermute | solution.py:50
  66.2 8.0 %collective-permute-start.26 = (bf16[1024,128]{1,0:T(8,128)(2,1)S(1)}, bf16[1024,128]{1,0:T(8,128)(2,1)S(1)}, u32[]{:S(2)}, u32[]{:S(2)}) collective-permute-start(bf16[1024,128]{1,0:T(8,128)(2,1)S(1)} %constant_dynamic-update-slice_fusion.11.refs_10_), channel_id=1, source_target_pairs={{0,96},{4,28},{8,104},{12,4},{16,112},{20,12},{24,120},{28,20},{32... | collective-permute-start | bytes 786440 | tf_op jit(solution)/shard_map/ppermute | solution.py:48
  66.8 8.1 %collective-permute-start.25 = (bf16[1024,128]{1,0:T(8,128)(2,1)S(1)}, bf16[1024,128]{1,0:T(8,128)(2,1)S(1)}, u32[]{:S(2)}, u32[]{:S(2)}) collective-permute-start(bf16[1024,128]{1,0:T(8,128)(2,1)S(1)} %constant_dynamic-update-slice_fusion.11.refs_10_), channel_id=1, source_target_pairs={{0,32},{4,12},{8,40},{12,20},{16,48},{20,28},{24,56},{28,4},{32,64... | collective-permute-start | bytes 786440 | tf_op jit(solution)/shard_map/ppermute | solution.py:47
  74.2 9.6 %collective-permute-start.29 = (bf16[1024,128]{1,0:T(8,128)(2,1)S(1)}, bf16[1024,128]{1,0:T(8,128)(2,1)S(1)}, u32[]{:S(2)}, u32[]{:S(2)}) collective-permute-start(bf16[1024,128]{1,0:T(8,128)(2,1)S(1)} %constant_dynamic-update-slice_fusion.11.refs_10_), channel_id=1, source_target_pairs={{0,4},{4,0},{8,12},{12,8},{16,20},{20,16},{24,28},{28,24},{32,36},... | collective-permute-start | bytes 786440 | tf_op jit(solution)/shard_map/ppermute | solution.py:66
  74.9 5.5 %collective-permute-start.28 = (bf16[512,128]{1,0:T(8,128)(2,1)S(1)}, bf16[512,128]{1,0:T(8,128)(2,1)S(1)}, u32[]{:S(2)}, u32[]{:S(2)}) collective-permute-start(bf16[512,128]{1,0:T(8,128)(2,1)S(1)} %slice.177), channel_id=1, source_target_pairs={{0,96},{4,28},{8,104},{12,4},{16,112},{20,12},{24,120},{28,20},{32... | collective-permute-start | bytes 393224 | tf_op jit(solution)/shard_map/ppermute | solution.py:50
  80.4 5.8 %collective-permute-start.27 = (bf16[512,128]{1,0:T(8,128)(2,1)S(1)}, bf16[512,128]{1,0:T(8,128)(2,1)S(1)}, u32[]{:S(2)}, u32[]{:S(2)}) collective-permute-start(bf16[512,128]{1,0:T(8,128)(2,1)S(1)} %slice.176), channel_id=1, source_target_pairs={{0,32},{4,12},{8,40},{12,20},{16,48},{20,28},{24,56},{28,4},{32,64... | collective-permute-start | bytes 393224 | tf_op jit(solution)/shard_map/ppermute | solution.py:49
  83.7 7.8 %collective-permute-start.14 = (bf16[1536,128]{1,0:T(8,128)(2,1)S(1)}, bf16[1536,128]{1,0:T(8,128)(2,1)S(1)}, u32[]{:S(2)}, u32[]{:S(2)}) collective-permute-start(bf16[1536,128]{1,0:T(8,128)(2,1)S(1)} %slice.171), channel_id=1, source_target_pairs={{0,96},{4,28},{8,104},{12,4},{16,112},{20,12},{24,120},{28,20},{32... | collective-permute-start | bytes 1179656 | tf_op jit(solution)/shard_map/ppermute | solution.py:50
  83.9 7.9 %collective-permute-start.13 = (bf16[1536,128]{1,0:T(8,128)(2,1)S(1)}, bf16[1536,128]{1,0:T(8,128)(2,1)S(1)}, u32[]{:S(2)}, u32[]{:S(2)}) collective-permute-start(bf16[1536,128]{1,0:T(8,128)(2,1)S(1)} %slice.170), channel_id=1, source_target_pairs={{0,32},{4,12},{8,40},{12,20},{16,48},{20,28},{24,56},{28,4},{32,64... | collective-permute-start | bytes 1179656 | tf_op jit(solution)/shard_map/ppermute | solution.py:49
  86.3 10.6 %collective-permute-start.17 = (bf16[3072,128]{1,0:T(8,128)(2,1)S(1)}, bf16[3072,128]{1,0:T(8,128)(2,1)S(1)}, u32[]{:S(2)}, u32[]{:S(2)}) collective-permute-start(bf16[3072,128]{1,0:T(8,128)(2,1)S(1)} %collective-permute-done.12.refs_2_), channel_id=1, source_target_pairs={{0,4},{4,0},{8,12},{12,8},{16,20},{20,16},{24,28},{28,24},{32,36},... | collective-permute-start | bytes 2359304 | tf_op jit(solution)/shard_map/ppermute | solution.py:66
  86.8 10.1 %collective-permute-start.16 = (bf16[3072,128]{1,0:T(8,128)(2,1)S(1)}, bf16[3072,128]{1,0:T(8,128)(2,1)S(1)}, u32[]{:S(2)}, u32[]{:S(2)}) collective-permute-start(bf16[3072,128]{1,0:T(8,128)(2,1)S(1)} %collective-permute-done.11.refs_1_), channel_id=1, source_target_pairs={{0,4},{4,0},{8,12},{12,8},{16,20},{20,16},{24,28},{28,24},{32,36},... | collective-permute-start | bytes 2359304 | tf_op jit(solution)/shard_map/ppermute | solution.py:66
  88.4 6.2 %collective-permute-start.32 = (bf16[512,128]{1,0:T(8,128)(2,1)S(1)}, bf16[512,128]{1,0:T(8,128)(2,1)S(1)}, u32[]{:S(2)}, u32[]{:S(2)}) collective-permute-start(bf16[512,128]{1,0:T(8,128)(2,1)S(1)} %collective-permute-done.27.refs_13_), channel_id=1, source_target_pairs={{0,4},{4,0},{8,12},{12,8},{16,20},{20,16},{24,28},{28,24},{32,36},... | collective-permute-start | bytes 393224 | tf_op jit(solution)/shard_map/ppermute | solution.py:66
  91.6 5.3 %collective-permute-start.19 = (bf16[1536,128]{1,0:T(8,128)(2,1)S(1)}, bf16[1536,128]{1,0:T(8,128)(2,1)S(1)}, u32[]{:S(2)}, u32[]{:S(2)}) collective-permute-start(bf16[1536,128]{1,0:T(8,128)(2,1)S(1)} %collective-permute-done.14.refs_4_), channel_id=1, source_target_pairs={{0,4},{4,0},{8,12},{12,8},{16,20},{20,16},{24,28},{28,24},{32,36},... | collective-permute-start | bytes 1179656 | tf_op jit(solution)/shard_map/ppermute | solution.py:66
  91.8 5.1 %collective-permute-start.18 = (bf16[1536,128]{1,0:T(8,128)(2,1)S(1)}, bf16[1536,128]{1,0:T(8,128)(2,1)S(1)}, u32[]{:S(2)}, u32[]{:S(2)}) collective-permute-start(bf16[1536,128]{1,0:T(8,128)(2,1)S(1)} %collective-permute-done.13.refs_3_), channel_id=1, source_target_pairs={{0,4},{4,0},{8,12},{12,8},{16,20},{20,16},{24,28},{28,24},{32,36},... | collective-permute-start | bytes 1179656 | tf_op jit(solution)/shard_map/ppermute | solution.py:66
  114.0 28.5 %collective-permute-start.35 = (bf16[128,2048]{1,0:T(8,128)(2,1)S(1)}, bf16[128,2048]{1,0:T(8,128)(2,1)}, u32[]{:S(2)}, u32[]{:S(2)}) collective-permute-start(bf16[128,2048]{1,0:T(8,128)(2,1)S(1)} %get-tuple-element.43), channel_id=1, source_target_pairs={{0,3},{1,0},{2,1},{3,2},{4,7},{5,4},{6,5},{7,6},{8,11},{9,8},{10,9... | collective-permute-start | bytes 1572872 | tf_op jit(solution)/shard_map/ppermute | solution.py:320
  117.1 25.5 %collective-permute-start.34 = (bf16[128,2048]{1,0:T(8,128)(2,1)S(1)}, bf16[128,2048]{1,0:T(8,128)(2,1)}, u32[]{:S(2)}, u32[]{:S(2)}) collective-permute-start(bf16[128,2048]{1,0:T(8,128)(2,1)S(1)} %get-tuple-element.44), channel_id=1, source_target_pairs={{0,1},{1,2},{2,3},{3,0},{4,5},{5,6},{6,7},{7,4},{8,9},{9,10},{10,1... | collective-permute-start | bytes 1572872 | tf_op jit(solution)/shard_map/ppermute | solution.py:319
  139.3 22.8 %collective-permute-start.37 = (bf16[128,2048]{1,0:T(8,128)(2,1)S(1)}, bf16[128,2048]{1,0:T(8,128)(2,1)S(1)}, u32[]{:S(2)}, u32[]{:S(2)}) collective-permute-start(bf16[128,2048]{1,0:T(8,128)(2,1)S(1)} %get-tuple-element.41), channel_id=1, source_target_pairs={{0,3},{1,0},{2,1},{3,2},{4,7},{5,4},{6,5},{7,6},{8,11},{9,8},{10,9... | collective-permute-start | bytes 1572872 | tf_op jit(solution)/shard_map/ppermute | solution.py:325
  145.1 16.9 %collective-permute-start.36 = (bf16[128,2048]{1,0:T(8,128)(2,1)}, bf16[128,2048]{1,0:T(8,128)(2,1)}, u32[]{:S(2)}, u32[]{:S(2)}) collective-permute-start(bf16[128,2048]{1,0:T(8,128)(2,1)} %get-tuple-element.31), channel_id=1, source_target_pairs={{0,1},{1,2},{2,3},{3,0},{4,5},{5,6},{6,7},{7,4},{8,9},{9,10},{10,1... | collective-permute-start | bytes 1572872 | tf_op jit(solution)/shard_map/ppermute | solution.py:329
  145.1 26.0 %collective-permute-start.38 = (bf16[128,2048]{1,0:T(8,128)(2,1)S(1)}, bf16[128,2048]{1,0:T(8,128)(2,1)S(1)}, u32[]{:S(2)}, u32[]{:S(2)}) collective-permute-start(bf16[128,2048]{1,0:T(8,128)(2,1)S(1)} %get-tuple-element.42), channel_id=1, source_target_pairs={{0,1},{1,2},{2,3},{3,0},{4,5},{5,6},{6,7},{7,4},{8,9},{9,10},{10,1... | collective-permute-start | bytes 1572872 | tf_op jit(solution)/shard_map/ppermute | solution.py:323
  145.1 26.0 %collective-permute-start.39 = (bf16[128,2048]{1,0:T(8,128)(2,1)}, bf16[128,2048]{1,0:T(8,128)(2,1)S(1)}, u32[]{:S(2)}, u32[]{:S(2)}) collective-permute-start(bf16[128,2048]{1,0:T(8,128)(2,1)} %get-tuple-element.32), channel_id=1, source_target_pairs={{0,3},{1,0},{2,1},{3,2},{4,7},{5,4},{6,5},{7,6},{8,11},{9,8},{10,9... | collective-permute-start | bytes 1572872 | tf_op jit(solution)/shard_map/ppermute | solution.py:330
  (38 other events, 328.5 us)

commit v2 on v1

--- a/solution.py
+++ b/solution.py
@@ -15,6 +15,7 @@
 masked = -1e30
 initial_peak = -1e29
 ROWS = 256
+SLOTS = 4
 PIECE_SPACE = pltpu.HBM
 exp2_scale = 1.4426950408889634 * HEAD_SIZE ** (-0.5)
 
@@ -51,7 +52,7 @@
     return [piece, behind, ahead, upper, lower]
 
 
-def gather_plane(keys, values):
+def gather_plane(keys, values, whole):
     core = lax.axis_index("dp") & 1
     other = lax.ppermute(jnp.where(core == 0, values, keys), "dp", CORE_SWAP)
     mine = jnp.where(
@@ -63,7 +64,11 @@
     line = ring_gather(mine, "dp", shift)
     shift = functools.partial(plane_shift, first_axis=False)
     plane = ring_gather(jnp.concatenate(line, axis=0), "dp", shift)
-    return plane + [lax.ppermute(piece, "dp", CORE_SWAP) for piece in plane]
+    if whole:
+        plane = [jnp.concatenate(plane, axis=0)]
+    traded = [lax.ppermute(piece, "dp", CORE_SWAP) for piece in plane[:3]]
+    traded += [lax.ppermute(piece, "dp", CORE_SWAP) for piece in plane[3:]]
+    return plane + traded
 
 
 def doc_starts(lengths, positions):
@@ -94,8 +99,8 @@
 
 
 def attend_kernel(ids, lengths, query, cos_part, sin_part, *refs, quarters):
-    bulk, rest, refs = refs[:10], refs[10:20], refs[20:]
-    out, rows, peak, summed, starts, query_at, key_at, block, sems = refs
+    bulk, rest, refs = refs[:10], refs[10:12], refs[12:]
+    out, rows, scores, peak, summed, starts, query_at, key_at, block, sems = refs
     count = query.shape[0]
     heads = query.shape[1] // HEAD_SIZE
     size = block.shape[2]
@@ -125,11 +130,13 @@
     low, high = first_start // size, last // size + 1
     full_low, full_high = (last_start + size - 1) // size, (first + 1) // size
 
+    most, few = 6 * span, 2 * span
+
     def place(step):
         return jnp.where(step == 0, 0, jnp.where(step == 1, 2, jnp.where(step == 2, 3, 1)))
 
     def start_copies(chip):
-        slot = chip & 1
+        slot = chip & (SLOTS - 1)
         at_x, at_z = place(((chip >> 2) - own_x) & 3), place(((chip & 3) - own_z) & 3)
         outer = jnp.where(core == 0, at_x, at_z)
         inner = jnp.where(core == 0, at_z, at_x)
@@ -140,25 +147,37 @@
 
                 @pl.when(index == n)
                 def _():
-                    for sources, at, length in ((bulk, 0, 6 * span), (rest, 6 * span, 2 * span)):
-                        pltpu.make_async_copy(
-                            sources[side + n].at[pl.ds(pl.multiple_of(line * length, length), length)],
-                            block.at[slot, kind, at : at + length],
-                            sems.at[slot, kind],
-                        ).start()
+                    pltpu.make_async_copy(
+                        bulk[side + n].at[pl.ds(pl.multiple_of(line * most, most), most)],
+                        block.at[slot, kind, :most],
+                        sems.at[slot, kind],
+                    ).start()
+
+            pltpu.make_async_copy(
+                rest[side // 5].at[
+                    pl.ds(pl.multiple_of((RING * major + minor) * few, few), few)
+                ],
+                block.at[slot, kind, most:],
+                sems.at[slot, kind],
+            ).start()
 
     def wait_copies(chip):
-        slot = chip & 1
+        slot = chip & (SLOTS - 1)
         for kind in range(2):
             pltpu.make_async_copy(
                 bulk[0].at[pl.ds(0, size)], block.at[slot, kind], sems.at[slot, kind]
             ).wait()
 
-    start_copies(low)
+    def begin(chip, carry):
+        start_copies(chip)
+        return carry
+
+    lax.fori_loop(low, jnp.minimum(low + (SLOTS - 1), high), begin, 0)
+    here = slice(quarters[0] * span, quarters[0] * span + count)
     for h in range(heads):
         at = slice(h * HEAD_SIZE, (h + 1) * HEAD_SIZE)
         head = query[:, at]
-        turned = head * cos_part[...] + pltpu.roll(head, HEAD_SIZE // 2, 1) * sin_part[...]
+        turned = head * cos_part[here, :] + pltpu.roll(head, HEAD_SIZE // 2, 1) * sin_part[here, :]
         rows[h * count : (h + 1) * count, :] = turned.astype(jnp.bfloat16)
     for i, base in enumerate(bases):
         at = base + lax.broadcasted_iota(jnp.int32, (span, 1), 0)
@@ -171,42 +190,56 @@
     peak[...] = jnp.full(peak.shape, initial_peak, jnp.float32)
     summed[...] = jnp.zeros(summed.shape, jnp.float32)
 
+    def score(chip, at):
+        scores[at, :] = lax.dot_general(
+            rows[at, :],
+            block[chip & (SLOTS - 1), 0],
+            (((1,), (1,)), ((), ())),
+            preferred_element_type=jnp.float32,
+        )
+
     def step(chip, cut):
-        slot = chip & 1
-        block_keys = block[slot, 0]
+        slot = chip & (SLOTS - 1)
         block_values = jnp.concatenate(
             [block[slot, 1], jnp.ones((size, HEAD_SIZE), jnp.bfloat16)], axis=1
         )
         if cut:
             where = chip * size + key_at[...]
-            visible = (where >= starts[...]) & (where <= query_at[...])
+            scores_seen = (where >= starts[...]) & (where <= query_at[...])
             if count < ROWS:
-                visible = jnp.concatenate([visible] * (ROWS // count), axis=0)
+                scores_seen = jnp.concatenate([scores_seen] * (ROWS // count), axis=0)
         for r in range(heads * count // ROWS):
             at = slice(r * ROWS, (r + 1) * ROWS)
-            scores = lax.dot_general(
-                rows[at, :], block_keys, (((1,), (1,)), ((), ())), preferred_element_type=jnp.float32
-            )
-            if cut:
-                local = (r * ROWS) % max(count, ROWS)
-                scores = jnp.where(visible[local : local + ROWS], scores, masked)
-            parts = [scores[:, c : c + HEAD_SIZE] for c in range(0, size, HEAD_SIZE)]
+            local = (r * ROWS) % max(count, ROWS)
+
+            def part(c):
+                here = scores[at, c : c + HEAD_SIZE]
+                if cut:
+                    here = jnp.where(
+                        scores_seen[local : local + ROWS, c : c + HEAD_SIZE], here, masked
+                    )
+                return here
+
             old = peak[at, :]
-            best = functools.reduce(jnp.maximum, parts)
+            columns = range(0, size, HEAD_SIZE)
+            best = functools.reduce(jnp.maximum, [part(c) for c in columns])
             fresh = jnp.maximum(old, jnp.max(best, axis=1, keepdims=True))
             peak[at, :] = fresh
             shrink = jnp.exp2((old - fresh) * exp2_scale)
-            probs = [jnp.exp2((part - fresh) * exp2_scale).astype(jnp.bfloat16) for part in parts]
+            probs = [jnp.exp2((part(c) - fresh) * exp2_scale).astype(jnp.bfloat16) for c in columns]
             update = wide_dot(jnp.concatenate(probs, axis=1), block_values)
             summed[at, :HEAD_SIZE] = summed[at, :HEAD_SIZE] * shrink + update[:, :HEAD_SIZE]
             summed[at, HEAD_SIZE:] = summed[at, HEAD_SIZE:] * shrink + update[:, HEAD_SIZE:]
+            score(chip + 1, at)
 
     def one_block(chip, carry):
-        wait_copies(chip)
-
         @pl.when(chip + 1 < high)
         def _():
-            start_copies(chip + 1)
+            wait_copies(chip + 1)
+
+        @pl.when(chip + (SLOTS - 1) < high)
+        def _():
+            start_copies(chip + (SLOTS - 1))
 
         whole = (chip >= full_low) & (chip < full_high)
 
@@ -220,6 +253,9 @@
 
         return carry
 
+    wait_copies(low)
+    for r in range(heads * count // ROWS):
+        score(low, slice(r * ROWS, (r + 1) * ROWS))
     lax.fori_loop(low, high, one_block, 0)
     for h in range(heads):
         at = slice(h * count, (h + 1) * count)
@@ -237,17 +273,18 @@
     return pl.pallas_call(
         functools.partial(attend_kernel, quarters=quarters),
         out_shape=jax.ShapeDtypeStruct((count, width), jnp.bfloat16),
-        in_specs=[smem, smem, vmem, vmem, vmem] + [hbm] * 20,
+        in_specs=[smem, smem, vmem, vmem, vmem] + [hbm] * 12,
         out_specs=vmem,
         scratch_shapes=[
             pltpu.VMEM((rows, HEAD_SIZE), jnp.bfloat16),
+            pltpu.VMEM((rows, size), jnp.float32),
             pltpu.VMEM((rows, HEAD_SIZE), jnp.float32),
             pltpu.VMEM((rows, 2 * HEAD_SIZE), jnp.float32),
             pltpu.VMEM((count, 1), jnp.int32),
             pltpu.VMEM((count, 1), jnp.int32),
             pltpu.VMEM((1, size), jnp.int32),
-            pltpu.VMEM((2, 2, size, HEAD_SIZE), jnp.bfloat16),
-            pltpu.SemaphoreType.DMA((2, 2)),
+            pltpu.VMEM((SLOTS, 2, size, HEAD_SIZE), jnp.bfloat16),
+            pltpu.SemaphoreType.DMA((SLOTS, 2)),
         ],
         compiler_params=pltpu.CompilerParams(vmem_limit_bytes=56 * 2**20),
         cost_estimate=pl.CostEstimate(
@@ -267,8 +304,8 @@
     cos_part, sin_part = angles_of(positions - doc_starts(lengths, positions))
     ids = jnp.stack([dp, mine]).astype(jnp.int32)
 
-    def project(piece, q):
-        at = slice(q * count, (q + 1) * count)
+    def project(piece, first):
+        at = slice(first, first + piece.shape[0])
         key = wide_dot(piece, key_weight)
         key = key * cos_part[at] + jnp.roll(key, HEAD_SIZE // 2, axis=1) * sin_part[at]
         value = wide_dot(piece, value_weight)
@@ -276,8 +313,7 @@
 
     half = count // 2
     query = [None] * RING
-    keys, values = [None] * RING, [None] * RING
-    keys[0], values[0] = project(normed, 0)
+    kv_own = project(normed, 0)
     query[0] = wide_dot(normed, w_query)
     behind_top = lax.ppermute(normed[:half], "tensor", ring_shift(1))
     ahead_low = lax.ppermute(normed[half:], "tensor", ring_shift(-1))
@@ -285,31 +321,30 @@
     ahead_top = lax.ppermute(normed[:half], "tensor", ring_shift(-1))
     far_top = lax.ppermute(behind_top, "tensor", ring_shift(1))
     far_low = lax.ppermute(ahead_low, "tensor", ring_shift(-1))
-    behind_low, ahead_top, query[0], keys[0], values[0] = lax.optimization_barrier(
-        (behind_low, ahead_top, query[0], keys[0], values[0])
+    kv_behind_top = project(behind_top, count)
+    kv_ahead_low = project(ahead_low, 2 * count + half)
+    behind_low, ahead_top, query[0], kv_own, kv_behind_top, kv_ahead_low, ids = (
+        lax.optimization_barrier(
+            (behind_low, ahead_top, query[0], kv_own, kv_behind_top, kv_ahead_low, ids)
+        )
     )
-    behind = jnp.concatenate([behind_top, behind_low], axis=0)
-    ahead = jnp.concatenate([ahead_top, ahead_low], axis=0)
-    keys[1], values[1] = project(behind, 1)
-    keys[2], values[2] = project(ahead, 2)
-    query[1] = wide_dot(behind, w_query)
-    query[2] = wide_dot(ahead, w_query)
-    bulk = gather_plane(jnp.concatenate(keys[:3], axis=0), jnp.concatenate(values[:3], axis=0))
-    far_top, far_low, query[1], query[2] = lax.optimization_barrier(
-        (far_top, far_low, query[1], query[2])
-    )
+    kv_behind_low = project(behind_low, count + half)
+    kv_ahead_top = project(ahead_top, 2 * count)
+    near = [wide_dot(a, w_query) for a in (behind_top, behind_low, ahead_top, ahead_low)]
+    kv_near = (kv_own, kv_behind_top, kv_behind_low, kv_ahead_top, kv_ahead_low)
+    bulk = gather_plane(*[jnp.concatenate(a, axis=0) for a in zip(*kv_near)], False)
+    far_top, far_low, near = lax.optimization_barrier((far_top, far_low, near))
     far = jnp.concatenate([far_top, far_low], axis=0)
-    keys[3], values[3] = project(far, 3)
-    rest = gather_plane(keys[3], values[3])
+    rest = gather_plane(*project(far, 3 * count), True)
     query[3] = wide_dot(far, w_query)
+    near_rows = jnp.concatenate(near, axis=0)
     pieces = bulk + rest
 
     def branch(quarters, after=None):
-        at = slice(quarters[0] * count, (quarters[-1] + 1) * count)
-        rows = jnp.concatenate([query[q] for q in quarters], axis=0)
+        rows = near_rows if len(quarters) == 2 else query[quarters[0]]
         if after is not None:
             rows, after = lax.optimization_barrier((rows, after))
-        attended = attend(ids, lengths, rows, cos_part[at], sin_part[at], pieces, quarters)
+        attended = attend(ids, lengths, rows, cos_part, sin_part, pieces, quarters)
         return wide_dot(attended, w_out), after
 
     half = w_out.shape[1] // 2

time: 174 us -> 184 us (1.057)
  the two profiles are of different devices: /device:TPU:68 before, /device:TPU:4 now
where the time goes in v2:
time: 184 us; the launch traced here: 182 us
  waiting for transfers between devices  54.5 us (30%)
  starting transfers between devices  42.5 us (23%)
  Pallas kernels  34.7 us (19%)
  matrix products  29.5 us (16%)
  other arithmetic  15.3 us (8%)
  local copies, waits for them, and re-layouts  5.23 us (3%)
    pallas_call x3, Pallas kernels, attend(): pl.pallas_call(functools.partial(attend_kernel, quarters=quarters), out_s...  34.7 us
    dot_general x21, matrix products, wide_dot(): return jnp.dot(a, b, preferred_element_type=jnp.float32)  29.5 us
    ppermute x4, waiting for transfers between devices, ring_gather(): upper = lax.ppermute(behind[:half], axis, shift(1))  18.5 us
    ppermute x4, starting transfers between devices, ring_gather(): lower = lax.ppermute(ahead[half:], axis, shift(-1))  9.51 us
    ppermute x1, waiting for transfers between devices, body(): ahead_low = lax.ppermute(normed[half:], 'tensor', ring_shift(-1))  8.76 us
    ppermute x1, waiting for transfers between devices, body(): plain_up = lax.ppermute(plain_up, 'tensor', ring_shift(1))  8.61 us
    ppermute x4, starting transfers between devices, ring_gather(): ahead = lax.ppermute(piece, axis, shift(-1))  7.27 us
    ppermute x4, waiting for transfers between devices, ring_gather(): ahead = lax.ppermute(piece, axis, shift(-1))  5.24 us
  transfers between devices with their start and end apart: 36, of which 14 were waited for; matrix products, arithmetic and copies ran while one was open for 15% of the time, Pallas kernels for 14%

profile of v2, /device:TPU:4, one launch (start us, length us, event | category | flops | bytes accessed | tf_op | source)
XLA Modules:
  0.0 182.5 jit_solution(17177078762901769275)
XLA Ops:
  7.5 1.8 collective-permute-start.3
  15.7 4.9 %collective-permute-done.2 = bf16[64,4096]{1,0:T(8,128)(2,1)} collective-permute-done((bf16[64,4096]{1,0:T(8,128)(2,1)}, bf16[64,4096]{1,0:T(8,128)(2,1)}, u32[]{:S(2)}, u32[]{:S(2)}) %collective-permute-start.2) | collective-permute-done | bytes 524320 | tf_op jit(solution)/shard_map/ppermute | solution.py:318
  22.1 8.8 %collective-permute-done.3 = bf16[64,4096]{1,0:T(8,128)(2,1)} collective-permute-done((bf16[64,4096]{1,0:T(8,128)(2,1)}, bf16[64,4096]{1,0:T(8,128)(2,1)}, u32[]{:S(2)}, u32[]{:S(2)}) %collective-permute-start.3) | collective-permute-done | bytes 524320 | tf_op jit(solution)/shard_map/ppermute | solution.py:319
  37.2 1.9 %fusion.38 = f32[64,512]{1,0:T(8,128)S(1)} fusion(bf16[64,4096]{1,0:T(8,128)(2,1)} %collective-permute-done, bf16[4096,512]{1,0:T(8,128)(2,1)S(1)} %copy-done.2), kind=kOutput, calls=%fused_computation.121 | convolution fusion | flops 268435456 | bytes 4849664 | tf_op jit(solution)/shard_map/dot_general | solution.py:98
  40.5 1.9 %fusion.39 = f32[64,512]{1,0:T(8,128)S(1)} fusion(bf16[64,4096]{1,0:T(8,128)(2,1)} %collective-permute-done.1, bf16[4096,512]{1,0:T(8,128)(2,1)S(1)} %copy-done.2), kind=kOutput, calls=%fused_computation.122 | convolution fusion | flops 268435456 | bytes 4849664 | tf_op jit(solution)/shard_map/dot_general | solution.py:98
  47.2 1.9 %fusion.37 = f32[64,512]{1,0:T(8,128)S(1)} fusion(bf16[64,4096]{1,0:T(8,128)(2,1)} %collective-permute-done.2, bf16[4096,512]{1,0:T(8,128)(2,1)S(1)} %copy-done.2), kind=kOutput, calls=%fused_computation.120 | convolution fusion | flops 268435456 | bytes 4849664 | tf_op jit(solution)/shard_map/dot_general | solution.py:98
  52.5 4.1 %collective-permute-start.8 = (bf16[768,128]{1,0:T(8,128)(2,1)S(1)}, bf16[768,128]{1,0:T(8,128)(2,1)S(1)}, u32[]{:S(2)}, u32[]{:S(2)}) collective-permute-start(bf16[768,128]{1,0:T(8,128)(2,1)S(1)} %get-tuple-element.52), channel_id=1, source_target_pairs={{0,24},{4,100},{8,0},{12,108},{16,8},{20,116},{24,16},{28,124},{32... | collective-permute-start | bytes 589832 | tf_op jit(solution)/shard_map/ppermute | solution.py:49
  56.6 1.9 %fusion.40 = f32[64,512]{1,0:T(8,128)S(1)} fusion(bf16[64,4096]{1,0:T(8,128)(2,1)} %collective-permute-done.3, bf16[4096,512]{1,0:T(8,128)(2,1)S(1)} %copy-done.2), kind=kOutput, calls=%fused_computation.123 | convolution fusion | flops 268435456 | bytes 4849664 | tf_op jit(solution)/shard_map/dot_general | solution.py:98
  59.8 3.8 %collective-permute-start.10 = (bf16[384,128]{1,0:T(8,128)(2,1)S(1)}, bf16[384,128]{1,0:T(8,128)(2,1)S(1)}, u32[]{:S(2)}, u32[]{:S(2)}) collective-permute-start(bf16[384,128]{1,0:T(8,128)(2,1)S(1)} %slice.197), channel_id=1, source_target_pairs={{0,24},{4,100},{8,0},{12,108},{16,8},{20,116},{24,16},{28,124},{32... | collective-permute-start | bytes 294920 | tf_op jit(solution)/shard_map/ppermute | solution.py:51
  67.0 2.7 %collective-permute-done.9 = bf16[384,128]{1,0:T(8,128)(2,1)S(1)} collective-permute-done((bf16[384,128]{1,0:T(8,128)(2,1)S(1)}, bf16[384,128]{1,0:T(8,128)(2,1)S(1)}, u32[]{:S(2)}, u32[]{:S(2)}) %collective-permute-start.9) | collective-permute-done | bytes 98336 | tf_op jit(solution)/shard_map/ppermute | solution.py:50
  69.7 2.5 %collective-permute-start.22 = (bf16[256,128]{1,0:T(8,128)(2,1)S(1)}, bf16[256,128]{1,0:T(8,128)(2,1)S(1)}, u32[]{:S(2)}, u32[]{:S(2)}) collective-permute-start(bf16[256,128]{1,0:T(8,128)(2,1)S(1)} %get-tuple-element.48), channel_id=1, source_target_pairs={{0,24},{4,100},{8,0},{12,108},{16,8},{20,116},{24,16},{28,124},{32... | collective-permute-start | bytes 196616 | tf_op jit(solution)/shard_map/ppermute | solution.py:49
  72.3 1.9 %collective-permute-done.22 = bf16[256,128]{1,0:T(8,128)(2,1)S(1)} collective-permute-done((bf16[256,128]{1,0:T(8,128)(2,1)S(1)}, bf16[256,128]{1,0:T(8,128)(2,1)S(1)}, u32[]{:S(2)}, u32[]{:S(2)}) %collective-permute-start.22) | collective-permute-done | bytes 65568 | tf_op jit(solution)/shard_map/ppermute | solution.py:49
  74.2 3.6 %collective-permute-start.24 = (bf16[128,128]{1,0:T(8,128)(2,1)S(1)}, bf16[128,128]{1,0:T(8,128)(2,1)S(1)}, u32[]{:S(2)}, u32[]{:S(2)}) collective-permute-start(bf16[128,128]{1,0:T(8,128)(2,1)S(1)} %slice.205), channel_id=1, source_target_pairs={{0,24},{4,100},{8,0},{12,108},{16,8},{20,116},{24,16},{28,124},{32... | collective-permute-start | bytes 98312 | tf_op jit(solution)/shard_map/ppermute | solution.py:51
  77.8 5.4 %collective-permute-done.23 = bf16[128,128]{1,0:T(8,128)(2,1)S(1)} collective-permute-done((bf16[128,128]{1,0:T(8,128)(2,1)S(1)}, bf16[128,128]{1,0:T(8,128)(2,1)S(1)}, u32[]{:S(2)}, u32[]{:S(2)}) %collective-permute-start.23) | collective-permute-done | bytes 32800 | tf_op jit(solution)/shard_map/ppermute | solution.py:50
  85.7 2.0 %collective-permute-start.11 = (bf16[3072,128]{1,0:T(8,128)(2,1)S(1)}, bf16[3072,128]{1,0:T(8,128)(2,1)S(1)}, u32[]{:S(2)}, u32[]{:S(2)}) collective-permute-start(bf16[3072,128]{1,0:T(8,128)(2,1)S(1)} %constant_dynamic-update-slice_fusion.24.refs_0_), channel_id=1, source_target_pairs={{0,32},{4,12},{8,40},{12,20},{16,48},{20,28},{24,56},{28,4},{32,64... | collective-permute-start | bytes 2359304 | tf_op jit(solution)/shard_map/ppermute | solution.py:48
  87.6 2.0 %collective-permute-done.26 = bf16[1024,128]{1,0:T(8,128)(2,1)S(1)} collective-permute-done((bf16[1024,128]{1,0:T(8,128)(2,1)S(1)}, bf16[1024,128]{1,0:T(8,128)(2,1)S(1)}, u32[]{:S(2)}, u32[]{:S(2)}) %collective-permute-start.26) | collective-permute-done | bytes 262176 | tf_op jit(solution)/shard_map/ppermute | solution.py:49
  90.0 2.0 %collective-permute-start.27 = (bf16[512,128]{1,0:T(8,128)(2,1)S(1)}, bf16[512,128]{1,0:T(8,128)(2,1)S(1)}, u32[]{:S(2)}, u32[]{:S(2)}) collective-permute-start(bf16[512,128]{1,0:T(8,128)(2,1)S(1)} %slice.206), channel_id=1, source_target_pairs={{0,32},{4,12},{8,40},{12,20},{16,48},{20,28},{24,56},{28,4},{32,64... | collective-permute-start | bytes 393224 | tf_op jit(solution)/shard_map/ppermute | solution.py:50
  92.1 7.7 %collective-permute-done.27 = bf16[512,128]{1,0:T(8,128)(2,1)S(1)} collective-permute-done((bf16[512,128]{1,0:T(8,128)(2,1)S(1)}, bf16[512,128]{1,0:T(8,128)(2,1)S(1)}, u32[]{:S(2)}, u32[]{:S(2)}) %collective-permute-start.27) | collective-permute-done | bytes 131104 | tf_op jit(solution)/shard_map/ppermute | solution.py:50
  100.0 1.9 %collective-permute-start.14 = (bf16[1536,128]{1,0:T(8,128)(2,1)S(1)}, bf16[1536,128]{1,0:T(8,128)(2,1)S(1)}, u32[]{:S(2)}, u32[]{:S(2)}) collective-permute-start(bf16[1536,128]{1,0:T(8,128)(2,1)S(1)} %slice.199), channel_id=1, source_target_pairs={{0,96},{4,28},{8,104},{12,4},{16,112},{20,12},{24,120},{28,20},{32... | collective-permute-start | bytes 1179656 | tf_op jit(solution)/shard_map/ppermute | solution.py:51
  104.0 4.2 %collective-permute-done.14.refs_4_ = bf16[1536,128]{1,0:T(8,128)(2,1)S(1)} collective-permute-done((bf16[1536,128]{1,0:T(8,128)(2,1)S(1)}, bf16[1536,128]{1,0:T(8,128)(2,1)S(1)}, u32[]{:S(2)}, u32[]{:S(2)}) %collective-permute-start.14) | collective-permute-done | bytes 393248 | tf_op jit(solution)/shard_map/ppermute | solution.py:51
  108.2 2.8 %collective-permute-done.13.refs_3_ = bf16[1536,128]{1,0:T(8,128)(2,1)S(1)} collective-permute-done((bf16[1536,128]{1,0:T(8,128)(2,1)S(1)}, bf16[1536,128]{1,0:T(8,128)(2,1)S(1)}, u32[]{:S(2)}, u32[]{:S(2)}) %collective-permute-start.13) | collective-permute-done | bytes 393248 | tf_op jit(solution)/shard_map/ppermute | solution.py:50
  115.4 9.8 %attend.3 = bf16[128,512]{1,0:T(8,128)(2,1)} custom-call(s32[2]{0:T(128)} %pad_add_fusion.ids, s32[16]{0:T(128)} %lengths.5, f32[128,512]{1,0:T(8,128)} %fusion.41.query, f32[512,128]{1,0:T(8,128)} %copy-done.13, f32[512,128]{1,0:T(8,128)} %get-tuple-element.96.sin_part, bf16[3072,128]{1,0:T(8,128)(2,1)} %copy-done.9, bf16[3072,128]{1,0:T(8,128)(2,1)} %copy-done.7, ...), custom_call_target="tpu_custom_call" | custom-call | flops 1073741824 | bytes 4194304 | tf_op jit(solution)/shard_map/attend/pallas_call | solution.py:273
  127.0 3.2 %collective-permute-start.31 = (bf16[128,2048]{1,0:T(8,128)(2,1)S(1)}, bf16[128,2048]{1,0:T(8,128)(2,1)}, u32[]{:S(2)}, u32[]{:S(2)}) collective-permute-start(bf16[128,2048]{1,0:T(8,128)(2,1)S(1)} %get-tuple-element.61), channel_id=1, source_target_pairs={{0,3},{1,0},{2,1},{3,2},{4,7},{5,4},{6,5},{7,6},{8,11},{9,8},{10,9... | collective-permute-start | bytes 1572872 | tf_op jit(solution)/shard_map/ppermute | solution.py:355
  130.2 15.0 %attend.4 = bf16[256,512]{1,0:T(8,128)(2,1)} custom-call(s32[2]{0:T(128)} %pad_add_fusion.ids, s32[16]{0:T(128)} %lengths.5, f32[256,512]{1,0:T(8,128)} %pad_maximum_fusion.query, f32[512,128]{1,0:T(8,128)} %copy-done.13, f32[512,128]{1,0:T(8,128)} %get-tuple-element.96.sin_part, bf16[3072,128]{1,0:T(8,128)(2,1)} %copy-done.9, bf16[3072,128]{1,0:T(8,128)(2,1)} %copy-done.7, ...), custom_call_target="tpu_custom_call" | custom-call | flops 2147483648 | bytes 4194304 | tf_op jit(solution)/shard_map/attend/pallas_call | solution.py:273
  145.2 2.2 %fusion.32 = (bf16[256,4096]{1,0:T(8,128)(2,1)S(1)}, f32[256,4096]{1,0:T(8,128)S(1)}) fusion(bf16[256,512]{1,0:T(8,128)(2,1)} %attend.4, bf16[512,4096]{1,0:T(8,128)(2,1)S(1)} %copy-done.3), kind=kOutput, calls=%fused_computation.115 | convolution fusion | flops 1074790400 | bytes 10747904 | tf_op jit(solution)/shard_map/dot_general | solution.py:98
  147.5 3.3 %collective-permute-start.33 = (bf16[128,2048]{1,0:T(8,128)(2,1)S(1)}, bf16[128,2048]{1,0:T(8,128)(2,1)S(1)}, u32[]{:S(2)}, u32[]{:S(2)}) collective-permute-start(bf16[128,2048]{1,0:T(8,128)(2,1)S(1)} %get-tuple-element.59), channel_id=1, source_target_pairs={{0,3},{1,0},{2,1},{3,2},{4,7},{5,4},{6,5},{7,6},{8,11},{9,8},{10,9... | collective-permute-start | bytes 1572872 | tf_op jit(solution)/shard_map/ppermute | solution.py:360
  150.8 2.5 %fusion.5 = (bf16[128,2048]{1,0:T(8,128)(2,1)}, bf16[128,2048]{1,0:T(8,128)(2,1)}) fusion(f32[256,4096]{1,0:T(8,128)S(1)} %get-tuple-element.103, bf16[128,2048]{1,0:T(8,128)(2,1)} %collective-permute-done.31, bf16[128,2048]{1,0:T(8,128)(2,1)} %collective-permute-done.30), kind=kLoop, calls=%fused_computation.16 | loop fusion | flops 1572864 | bytes 4194304 | tf_op jit(solution)/shard_map/convert_element_type | solution.py:362
  153.3 3.3 %collective-permute-start.35 = (bf16[128,2048]{1,0:T(8,128)(2,1)}, bf16[128,2048]{1,0:T(8,128)(2,1)}, u32[]{:S(2)}, u32[]{:S(2)}) collective-permute-start(bf16[128,2048]{1,0:T(8,128)(2,1)} %get-tuple-element.46), channel_id=1, source_target_pairs={{0,3},{1,0},{2,1},{3,2},{4,7},{5,4},{6,5},{7,6},{8,11},{9,8},{10,9... | collective-permute-start | bytes 1572872 | tf_op jit(solution)/shard_map/ppermute | solution.py:365
  156.6 9.8 %attend.5 = bf16[128,512]{1,0:T(8,128)(2,1)} custom-call(s32[2]{0:T(128)} %pad_add_fusion.ids, s32[16]{0:T(128)} %lengths.5, f32[128,512]{1,0:T(8,128)} %fusion.33.query, f32[512,128]{1,0:T(8,128)} %copy-done.13, f32[512,128]{1,0:T(8,128)} %get-tuple-element.96.sin_part, bf16[3072,128]{1,0:T(8,128)(2,1)} %copy-done.9, bf16[3072,128]{1,0:T(8,128)(2,1)} %copy-done.7, ...), custom_call_target="tpu_custom_call" | custom-call | flops 1073741824 | bytes 4194304 | tf_op jit(solution)/shard_map/attend/pallas_call | solution.py:273
  166.4 3.2 %collective-permute-done.32 = bf16[128,2048]{1,0:T(8,128)(2,1)} collective-permute-done((bf16[128,2048]{1,0:T(8,128)(2,1)}, bf16[128,2048]{1,0:T(8,128)(2,1)}, u32[]{:S(2)}, u32[]{:S(2)}) %collective-permute-start.32) | collective-permute-done | bytes 524320 | tf_op jit(solution)/shard_map/ppermute | solution.py:364
  170.8 8.6 %collective-permute-done.34 = bf16[128,2048]{1,0:T(8,128)(2,1)S(1)} collective-permute-done((bf16[128,2048]{1,0:T(8,128)(2,1)S(1)}, bf16[128,2048]{1,0:T(8,128)(2,1)S(1)}, u32[]{:S(2)}, u32[]{:S(2)}) %collective-permute-start.34) | collective-permute-done | bytes 524320 | tf_op jit(solution)/shard_map/ppermute | solution.py:358
  180.6 1.9 %fusion.1 = bf16[128,4096]{1,0:T(8,128)(2,1)} fusion(bf16[128,512]{1,0:T(8,128)(2,1)S(1)} %copy-done.18, bf16[512,4096]{1,0:T(8,128)(2,1)S(1)} %copy-done.3, bf16[128,4096]{1,0:T(8,128)(2,1)S(1)} %copy-done.8, f32[128,2048]{1,0:T(8,128)S(1)} %convert_add_fusion, f32[128,2048]{1,0:T(8,128)S(1)} %convert_add_fusion.1), kind=kOutput, calls=%fused_computation.2 | convolution fusion | flops 539492352 | bytes 8519680 | tf_op jit(solution)/shard_map/dot_general | solution.py:98
  (174 shorter events, 49.5 us)
Async XLA Ops:
  4.3 16.3 %collective-permute-start.2 = (bf16[64,4096]{1,0:T(8,128)(2,1)}, bf16[64,4096]{1,0:T(8,128)(2,1)}, u32[]{:S(2)}, u32[]{:S(2)}) collective-permute-start(bf16[64,4096]{1,0:T(8,128)(2,1)} %get-tuple-element.63), channel_id=1, source_target_pairs={{0,1},{1,2},{2,3},{3,0},{4,5},{5,6},{6,7},{7,4},{8,9},{9,10},{10,1... | collective-permute-start | bytes 1572872 | tf_op jit(solution)/shard_map/ppermute | solution.py:318
  5.9 30.0 %collective-permute-start.1 = (bf16[64,4096]{1,0:T(8,128)(2,1)}, bf16[64,4096]{1,0:T(8,128)(2,1)}, u32[]{:S(2)}, u32[]{:S(2)}) collective-permute-start(bf16[64,4096]{1,0:T(8,128)(2,1)} %get-tuple-element.63), channel_id=1, source_target_pairs={{0,3},{1,0},{2,1},{3,2},{4,7},{5,4},{6,5},{7,6},{8,11},{9,8},{10,9... | collective-permute-start | bytes 1572872 | tf_op jit(solution)/shard_map/ppermute | solution.py:321
  7.5 23.3 %collective-permute-start.3 = (bf16[64,4096]{1,0:T(8,128)(2,1)}, bf16[64,4096]{1,0:T(8,128)(2,1)}, u32[]{:S(2)}, u32[]{:S(2)}) collective-permute-start(bf16[64,4096]{1,0:T(8,128)(2,1)} %get-tuple-element.64), channel_id=1, source_target_pairs={{0,3},{1,0},{2,1},{3,2},{4,7},{5,4},{6,5},{7,6},{8,11},{9,8},{10,9... | collective-permute-start | bytes 1572872 | tf_op jit(solution)/shard_map/ppermute | solution.py:319
  9.3 26.5 %collective-permute-start = (bf16[64,4096]{1,0:T(8,128)(2,1)}, bf16[64,4096]{1,0:T(8,128)(2,1)}, u32[]{:S(2)}, u32[]{:S(2)}) collective-permute-start(bf16[64,4096]{1,0:T(8,128)(2,1)} %get-tuple-element.64), channel_id=1, source_target_pairs={{0,1},{1,2},{2,3},{3,0},{4,5},{5,6},{6,7},{7,4},{8,9},{9,10},{10,1... | collective-permute-start | bytes 1572872 | tf_op jit(solution)/shard_map/ppermute | solution.py:320
  47.1 5.3 %collective-permute-start.6 = (bf16[384,128]{1,0:T(8,128)(2,1)S(1)}, bf16[384,128]{1,0:T(8,128)(2,1)S(1)}, u32[]{:S(2)}, u32[]{:S(2)}) collective-permute-start(bf16[384,128]{1,0:T(8,128)(2,1)S(1)} %broadcast_select_fusion.1), channel_id=1, source_target_pairs={{0,4},{4,0},{8,12},{12,8},{16,20},{20,16},{24,28},{28,24},{32,36},... | collective-permute-start | bytes 294920 | tf_op jit(solution)/shard_map/ppermute | solution.py:57
  49.1 15.8 %collective-permute-start.4 = (bf16[64,4096]{1,0:T(8,128)(2,1)}, bf16[64,4096]{1,0:T(8,128)(2,1)S(1)}, u32[]{:S(2)}, u32[]{:S(2)}) collective-permute-start(bf16[64,4096]{1,0:T(8,128)(2,1)} %collective-permute-done.2), channel_id=1, source_target_pairs={{0,1},{1,2},{2,3},{3,0},{4,5},{5,6},{6,7},{7,4},{8,9},{9,10},{10,1... | collective-permute-start | bytes 1572872 | tf_op jit(solution)/shard_map/ppermute | solution.py:322
  50.7 14.3 %collective-permute-start.5 = (bf16[64,4096]{1,0:T(8,128)(2,1)}, bf16[64,4096]{1,0:T(8,128)(2,1)S(1)}, u32[]{:S(2)}, u32[]{:S(2)}) collective-permute-start(bf16[64,4096]{1,0:T(8,128)(2,1)} %collective-permute-done.3), channel_id=1, source_target_pairs={{0,3},{1,0},{2,1},{3,2},{4,7},{5,4},{6,5},{7,6},{8,11},{9,8},{10,9... | collective-permute-start | bytes 1572872 | tf_op jit(solution)/shard_map/ppermute | solution.py:323
  52.5 7.3 %collective-permute-start.8 = (bf16[768,128]{1,0:T(8,128)(2,1)S(1)}, bf16[768,128]{1,0:T(8,128)(2,1)S(1)}, u32[]{:S(2)}, u32[]{:S(2)}) collective-permute-start(bf16[768,128]{1,0:T(8,128)(2,1)S(1)} %get-tuple-element.52), channel_id=1, source_target_pairs={{0,24},{4,100},{8,0},{12,108},{16,8},{20,116},{24,16},{28,124},{32... | collective-permute-start | bytes 589832 | tf_op jit(solution)/shard_map/ppermute | solution.py:49
  56.6 7.0 %collective-permute-start.7 = (bf16[768,128]{1,0:T(8,128)(2,1)S(1)}, bf16[768,128]{1,0:T(8,128)(2,1)S(1)}, u32[]{:S(2)}, u32[]{:S(2)}) collective-permute-start(bf16[768,128]{1,0:T(8,128)(2,1)S(1)} %get-tuple-element.52), channel_id=1, source_target_pairs={{0,8},{4,36},{8,16},{12,44},{16,24},{20,52},{24,0},{28,60},{32,40}... | collective-permute-start | bytes 589832 | tf_op jit(solution)/shard_map/ppermute | solution.py:48
  59.8 25.5 %collective-permute-start.10 = (bf16[384,128]{1,0:T(8,128)(2,1)S(1)}, bf16[384,128]{1,0:T(8,128)(2,1)S(1)}, u32[]{:S(2)}, u32[]{:S(2)}) collective-permute-start(bf16[384,128]{1,0:T(8,128)(2,1)S(1)} %slice.197), channel_id=1, source_target_pairs={{0,24},{4,100},{8,0},{12,108},{16,8},{20,116},{24,16},{28,124},{32... | collective-permute-start | bytes 294920 | tf_op jit(solution)/shard_map/ppermute | solution.py:51
  63.6 6.1 %collective-permute-start.9 = (bf16[384,128]{1,0:T(8,128)(2,1)S(1)}, bf16[384,128]{1,0:T(8,128)(2,1)S(1)}, u32[]{:S(2)}, u32[]{:S(2)}) collective-permute-start(bf16[384,128]{1,0:T(8,128)(2,1)S(1)} %slice.196), channel_id=1, source_target_pairs={{0,8},{4,36},{8,16},{12,44},{16,24},{20,52},{24,0},{28,60},{32,40}... | collective-permute-start | bytes 294920 | tf_op jit(solution)/shard_map/ppermute | solution.py:50
  72.3 5.5 %collective-permute-start.21 = (bf16[256,128]{1,0:T(8,128)(2,1)S(1)}, bf16[256,128]{1,0:T(8,128)(2,1)S(1)}, u32[]{:S(2)}, u32[]{:S(2)}) collective-permute-start(bf16[256,128]{1,0:T(8,128)(2,1)S(1)} %get-tuple-element.48), channel_id=1, source_target_pairs={{0,8},{4,36},{8,16},{12,44},{16,24},{20,52},{24,0},{28,60},{32,40}... | collective-permute-start | bytes 196616 | tf_op jit(solution)/shard_map/ppermute | solution.py:48
  74.2 9.0 %collective-permute-start.24 = (bf16[128,128]{1,0:T(8,128)(2,1)S(1)}, bf16[128,128]{1,0:T(8,128)(2,1)S(1)}, u32[]{:S(2)}, u32[]{:S(2)}) collective-permute-start(bf16[128,128]{1,0:T(8,128)(2,1)S(1)} %slice.205), channel_id=1, source_target_pairs={{0,24},{4,100},{8,0},{12,108},{16,8},{20,116},{24,16},{28,124},{32... | collective-permute-start | bytes 98312 | tf_op jit(solution)/shard_map/ppermute | solution.py:51
  77.8 5.4 %collective-permute-start.23 = (bf16[128,128]{1,0:T(8,128)(2,1)S(1)}, bf16[128,128]{1,0:T(8,128)(2,1)S(1)}, u32[]{:S(2)}, u32[]{:S(2)}) collective-permute-start(bf16[128,128]{1,0:T(8,128)(2,1)S(1)} %slice.204), channel_id=1, source_target_pairs={{0,8},{4,36},{8,16},{12,44},{16,24},{20,52},{24,0},{28,60},{32,40}... | collective-permute-start | bytes 98312 | tf_op jit(solution)/shard_map/ppermute | solution.py:50
  83.2 6.4 %collective-permute-start.26 = (bf16[1024,128]{1,0:T(8,128)(2,1)S(1)}, bf16[1024,128]{1,0:T(8,128)(2,1)S(1)}, u32[]{:S(2)}, u32[]{:S(2)}) collective-permute-start(bf16[1024,128]{1,0:T(8,128)(2,1)S(1)} %get-tuple-element.77), channel_id=1, source_target_pairs={{0,96},{4,28},{8,104},{12,4},{16,112},{20,12},{24,120},{28,20},{32... | collective-permute-start | bytes 786440 | tf_op jit(solution)/shard_map/ppermute | solution.py:49
  83.6 6.5 %collective-permute-start.25 = (bf16[1024,128]{1,0:T(8,128)(2,1)S(1)}, bf16[1024,128]{1,0:T(8,128)(2,1)S(1)}, u32[]{:S(2)}, u32[]{:S(2)}) collective-permute-start(bf16[1024,128]{1,0:T(8,128)(2,1)S(1)} %get-tuple-element.77), channel_id=1, source_target_pairs={{0,32},{4,12},{8,40},{12,20},{16,48},{20,28},{24,56},{28,4},{32,64... | collective-permute-start | bytes 786440 | tf_op jit(solution)/shard_map/ppermute | solution.py:48
  85.4 14.6 %collective-permute-start.12 = (bf16[3072,128]{1,0:T(8,128)(2,1)S(1)}, bf16[3072,128]{1,0:T(8,128)(2,1)S(1)}, u32[]{:S(2)}, u32[]{:S(2)}) collective-permute-start(bf16[3072,128]{1,0:T(8,128)(2,1)S(1)} %constant_dynamic-update-slice_fusion.24.refs_0_), channel_id=1, source_target_pairs={{0,96},{4,28},{8,104},{12,4},{16,112},{20,12},{24,120},{28,20},{32... | collective-permute-start | bytes 2359304 | tf_op jit(solution)/shard_map/ppermute | solution.py:49
  85.7 16.2 %collective-permute-start.11 = (bf16[3072,128]{1,0:T(8,128)(2,1)S(1)}, bf16[3072,128]{1,0:T(8,128)(2,1)S(1)}, u32[]{:S(2)}, u32[]{:S(2)}) collective-permute-start(bf16[3072,128]{1,0:T(8,128)(2,1)S(1)} %constant_dynamic-update-slice_fusion.24.refs_0_), channel_id=1, source_target_pairs={{0,32},{4,12},{8,40},{12,20},{16,48},{20,28},{24,56},{28,4},{32,64... | collective-permute-start | bytes 2359304 | tf_op jit(solution)/shard_map/ppermute | solution.py:48
  87.6 14.9 %collective-permute-start.15 = (bf16[3072,128]{1,0:T(8,128)(2,1)S(1)}, bf16[3072,128]{1,0:T(8,128)(2,1)S(1)}, u32[]{:S(2)}, u32[]{:S(2)}) collective-permute-start(bf16[3072,128]{1,0:T(8,128)(2,1)S(1)} %constant_dynamic-update-slice_fusion.24.refs_0_), channel_id=1, source_target_pairs={{0,4},{4,0},{8,12},{12,8},{16,20},{20,16},{24,28},{28,24},{32,36},... | collective-permute-start | bytes 2359304 | tf_op jit(solution)/shard_map/ppermute | solution.py:69
  89.7 10.1 %collective-permute-start.28 = (bf16[512,128]{1,0:T(8,128)(2,1)S(1)}, bf16[512,128]{1,0:T(8,128)(2,1)S(1)}, u32[]{:S(2)}, u32[]{:S(2)}) collective-permute-start(bf16[512,128]{1,0:T(8,128)(2,1)S(1)} %slice.207), channel_id=1, source_target_pairs={{0,96},{4,28},{8,104},{12,4},{16,112},{20,12},{24,120},{28,20},{32... | collective-permute-start | bytes 393224 | tf_op jit(solution)/shard_map/ppermute | solution.py:51
  90.0 9.7 %collective-permute-start.27 = (bf16[512,128]{1,0:T(8,128)(2,1)S(1)}, bf16[512,128]{1,0:T(8,128)(2,1)S(1)}, u32[]{:S(2)}, u32[]{:S(2)}) collective-permute-start(bf16[512,128]{1,0:T(8,128)(2,1)S(1)} %slice.206), channel_id=1, source_target_pairs={{0,32},{4,12},{8,40},{12,20},{16,48},{20,28},{24,56},{28,4},{32,64... | collective-permute-start | bytes 393224 | tf_op jit(solution)/shard_map/ppermute | solution.py:50
  99.8 15.5 %collective-permute-start.29 = (bf16[4096,128]{1,0:T(8,128)(2,1)S(1)}, bf16[4096,128]{1,0:T(8,128)(2,1)}, u32[]{:S(2)}, u32[]{:S(2)}) collective-permute-start(bf16[4096,128]{1,0:T(8,128)(2,1)S(1)} %constant_dynamic-update-slice_fusion.34.refs_10_), channel_id=1, source_target_pairs={{0,4},{4,0},{8,12},{12,8},{16,20},{20,16},{24,28},{28,24},{32,36},... | collective-permute-start | bytes 3145736 | tf_op jit(solution)/shard_map/ppermute | solution.py:69
  100.0 8.2 %collective-permute-start.14 = (bf16[1536,128]{1,0:T(8,128)(2,1)S(1)}, bf16[1536,128]{1,0:T(8,128)(2,1)S(1)}, u32[]{:S(2)}, u32[]{:S(2)}) collective-permute-start(bf16[1536,128]{1,0:T(8,128)(2,1)S(1)} %slice.199), channel_id=1, source_target_pairs={{0,96},{4,28},{8,104},{12,4},{16,112},{20,12},{24,120},{28,20},{32... | collective-permute-start | bytes 1179656 | tf_op jit(solution)/shard_map/ppermute | solution.py:51
  101.9 9.1 %collective-permute-start.13 = (bf16[1536,128]{1,0:T(8,128)(2,1)S(1)}, bf16[1536,128]{1,0:T(8,128)(2,1)S(1)}, u32[]{:S(2)}, u32[]{:S(2)}) collective-permute-start(bf16[1536,128]{1,0:T(8,128)(2,1)S(1)} %slice.198), channel_id=1, source_target_pairs={{0,32},{4,12},{8,40},{12,20},{16,48},{20,28},{24,56},{28,4},{32,64... | collective-permute-start | bytes 1179656 | tf_op jit(solution)/shard_map/ppermute | solution.py:50
  102.6 10.7 %collective-permute-start.17 = (bf16[3072,128]{1,0:T(8,128)(2,1)S(1)}, bf16[3072,128]{1,0:T(8,128)(2,1)S(1)}, u32[]{:S(2)}, u32[]{:S(2)}) collective-permute-start(bf16[3072,128]{1,0:T(8,128)(2,1)S(1)} %collective-permute-done.12.refs_2_), channel_id=1, source_target_pairs={{0,4},{4,0},{8,12},{12,8},{16,20},{20,16},{24,28},{28,24},{32,36},... | collective-permute-start | bytes 2359304 | tf_op jit(solution)/shard_map/ppermute | solution.py:69
  103.5 9.9 %collective-permute-start.16 = (bf16[3072,128]{1,0:T(8,128)(2,1)S(1)}, bf16[3072,128]{1,0:T(8,128)(2,1)S(1)}, u32[]{:S(2)}, u32[]{:S(2)}) collective-permute-start(bf16[3072,128]{1,0:T(8,128)(2,1)S(1)} %collective-permute-done.11.refs_1_), channel_id=1, source_target_pairs={{0,4},{4,0},{8,12},{12,8},{16,20},{20,16},{24,28},{28,24},{32,36},... | collective-permute-start | bytes 2359304 | tf_op jit(solution)/shard_map/ppermute | solution.py:69
  127.0 23.8 %collective-permute-start.31 = (bf16[128,2048]{1,0:T(8,128)(2,1)S(1)}, bf16[128,2048]{1,0:T(8,128)(2,1)}, u32[]{:S(2)}, u32[]{:S(2)}) collective-permute-start(bf16[128,2048]{1,0:T(8,128)(2,1)S(1)} %get-tuple-element.61), channel_id=1, source_target_pairs={{0,3},{1,0},{2,1},{3,2},{4,7},{5,4},{6,5},{7,6},{8,11},{9,8},{10,9... | collective-permute-start | bytes 1572872 | tf_op jit(solution)/shard_map/ppermute | solution.py:355
  130.2 20.6 %collective-permute-start.30 = (bf16[128,2048]{1,0:T(8,128)(2,1)S(1)}, bf16[128,2048]{1,0:T(8,128)(2,1)}, u32[]{:S(2)}, u32[]{:S(2)}) collective-permute-start(bf16[128,2048]{1,0:T(8,128)(2,1)S(1)} %get-tuple-element.62), channel_id=1, source_target_pairs={{0,1},{1,2},{2,3},{3,0},{4,5},{5,6},{6,7},{7,4},{8,9},{9,10},{10,1... | collective-permute-start | bytes 1572872 | tf_op jit(solution)/shard_map/ppermute | solution.py:354
  147.5 18.9 %collective-permute-start.33 = (bf16[128,2048]{1,0:T(8,128)(2,1)S(1)}, bf16[128,2048]{1,0:T(8,128)(2,1)S(1)}, u32[]{:S(2)}, u32[]{:S(2)}) collective-permute-start(bf16[128,2048]{1,0:T(8,128)(2,1)S(1)} %get-tuple-element.59), channel_id=1, source_target_pairs={{0,3},{1,0},{2,1},{3,2},{4,7},{5,4},{6,5},{7,6},{8,11},{9,8},{10,9... | collective-permute-start | bytes 1572872 | tf_op jit(solution)/shard_map/ppermute | solution.py:360
  153.3 16.3 %collective-permute-start.32 = (bf16[128,2048]{1,0:T(8,128)(2,1)}, bf16[128,2048]{1,0:T(8,128)(2,1)}, u32[]{:S(2)}, u32[]{:S(2)}) collective-permute-start(bf16[128,2048]{1,0:T(8,128)(2,1)} %get-tuple-element.45), channel_id=1, source_target_pairs={{0,1},{1,2},{2,3},{3,0},{4,5},{5,6},{6,7},{7,4},{8,9},{9,10},{10,1... | collective-permute-start | bytes 1572872 | tf_op jit(solution)/shard_map/ppermute | solution.py:364
  153.3 26.1 %collective-permute-start.34 = (bf16[128,2048]{1,0:T(8,128)(2,1)S(1)}, bf16[128,2048]{1,0:T(8,128)(2,1)S(1)}, u32[]{:S(2)}, u32[]{:S(2)}) collective-permute-start(bf16[128,2048]{1,0:T(8,128)(2,1)S(1)} %get-tuple-element.60), channel_id=1, source_target_pairs={{0,1},{1,2},{2,3},{3,0},{4,5},{5,6},{6,7},{7,4},{8,9},{9,10},{10,1... | collective-permute-start | bytes 1572872 | tf_op jit(solution)/shard_map/ppermute | solution.py:358
  153.3 26.1 %collective-permute-start.35 = (bf16[128,2048]{1,0:T(8,128)(2,1)}, bf16[128,2048]{1,0:T(8,128)(2,1)}, u32[]{:S(2)}, u32[]{:S(2)}) collective-permute-start(bf16[128,2048]{1,0:T(8,128)(2,1)} %get-tuple-element.46), channel_id=1, source_target_pairs={{0,3},{1,0},{2,1},{3,2},{4,7},{5,4},{6,5},{7,6},{8,11},{9,8},{10,9... | collective-permute-start | bytes 1572872 | tf_op jit(solution)/shard_map/ppermute | solution.py:365
  (25 other events, 248.9 us)

commit v3 on v2

--- a/solution.py
+++ b/solution.py
@@ -21,7 +21,6 @@
 
 RING = 4
 RELATIVE = (0, 3, 1, 2)
-KEY_ORDER = ((0, 0), (0, 1), (0, 2), (1, 0), (1, 1), (1, 2), (0, 3), (1, 3))
 
 
 def ring_shift(step):
@@ -52,7 +51,7 @@
     return [piece, behind, ahead, upper, lower]
 
 
-def gather_plane(keys, values, whole):
+def gather_plane(keys, values):
     core = lax.axis_index("dp") & 1
     other = lax.ppermute(jnp.where(core == 0, values, keys), "dp", CORE_SWAP)
     mine = jnp.where(
@@ -60,12 +59,9 @@
         jnp.concatenate([keys, other], axis=0),
         jnp.concatenate([other, values], axis=0),
     )
-    shift = functools.partial(plane_shift, first_axis=True)
-    line = ring_gather(mine, "dp", shift)
+    line = [mine] + [lax.ppermute(mine, "dp", plane_shift(n, True)) for n in (1, -1, 2)]
     shift = functools.partial(plane_shift, first_axis=False)
     plane = ring_gather(jnp.concatenate(line, axis=0), "dp", shift)
-    if whole:
-        plane = [jnp.concatenate(plane, axis=0)]
     traded = [lax.ppermute(piece, "dp", CORE_SWAP) for piece in plane[:3]]
     traded += [lax.ppermute(piece, "dp", CORE_SWAP) for piece in plane[3:]]
     return plane + traded
@@ -99,7 +95,7 @@
 
 
 def attend_kernel(ids, lengths, query, cos_part, sin_part, *refs, quarters):
-    bulk, rest, refs = refs[:10], refs[10:12], refs[12:]
+    pieces, refs = refs[:10], refs[10:]
     out, rows, scores, peak, summed, starts, query_at, key_at, block, sems = refs
     count = query.shape[0]
     heads = query.shape[1] // HEAD_SIZE
@@ -129,8 +125,6 @@
     first_start, last_start = start_of(first), start_of(last)
     low, high = first_start // size, last // size + 1
     full_low, full_high = (last_start + size - 1) // size, (first + 1) // size
-
-    most, few = 6 * span, 2 * span
 
     def place(step):
         return jnp.where(step == 0, 0, jnp.where(step == 1, 2, jnp.where(step == 2, 3, 1)))
@@ -148,24 +142,16 @@
                 @pl.when(index == n)
                 def _():
                     pltpu.make_async_copy(
-                        bulk[side + n].at[pl.ds(pl.multiple_of(line * most, most), most)],
-                        block.at[slot, kind, :most],
+                        pieces[side + n].at[pl.ds(pl.multiple_of(line * size, size), size)],
+                        block.at[slot, kind],
                         sems.at[slot, kind],
                     ).start()
-
-            pltpu.make_async_copy(
-                rest[side // 5].at[
-                    pl.ds(pl.multiple_of((RING * major + minor) * few, few), few)
-                ],
-                block.at[slot, kind, most:],
-                sems.at[slot, kind],
-            ).start()
 
     def wait_copies(chip):
         slot = chip & (SLOTS - 1)
         for kind in range(2):
             pltpu.make_async_copy(
-                bulk[0].at[pl.ds(0, size)], block.at[slot, kind], sems.at[slot, kind]
+                pieces[0].at[pl.ds(0, size)], block.at[slot, kind], sems.at[slot, kind]
             ).wait()
 
     def begin(chip, carry):
@@ -183,8 +169,8 @@
         at = base + lax.broadcasted_iota(jnp.int32, (span, 1), 0)
         query_at[i * span : (i + 1) * span, :] = at
         starts[i * span : (i + 1) * span, :] = start_of(at)
-    for i, (half, quarter) in enumerate(KEY_ORDER):
-        base = half * (RING * span) + quarter_base(quarter)
+    for i in range(size // span):
+        base = (i // RING) * (RING * span) + quarter_base(i % RING)
         lane = lax.broadcasted_iota(jnp.int32, (1, span), 1)
         key_at[:, i * span : (i + 1) * span] = base + lane
     peak[...] = jnp.full(peak.shape, initial_peak, jnp.float32)
@@ -273,7 +259,7 @@
     return pl.pallas_call(
         functools.partial(attend_kernel, quarters=quarters),
         out_shape=jax.ShapeDtypeStruct((count, width), jnp.bfloat16),
-        in_specs=[smem, smem, vmem, vmem, vmem] + [hbm] * 12,
+        in_specs=[smem, smem, vmem, vmem, vmem] + [hbm] * 10,
         out_specs=vmem,
         scratch_shapes=[
             pltpu.VMEM((rows, HEAD_SIZE), jnp.bfloat16),
@@ -286,7 +272,7 @@
             pltpu.VMEM((SLOTS, 2, size, HEAD_SIZE), jnp.bfloat16),
             pltpu.SemaphoreType.DMA((SLOTS, 2)),
         ],
-        compiler_params=pltpu.CompilerParams(vmem_limit_bytes=56 * 2**20),
+        compiler_params=pltpu.CompilerParams(vmem_limit_bytes=32 * 2**20),
         cost_estimate=pl.CostEstimate(
             flops=rows * 4096 * 512, transcendentals=rows * 4096, bytes_accessed=4 << 20
         ),
@@ -321,24 +307,21 @@
     ahead_top = lax.ppermute(normed[:half], "tensor", ring_shift(-1))
     far_top = lax.ppermute(behind_top, "tensor", ring_shift(1))
     far_low = lax.ppermute(ahead_low, "tensor", ring_shift(-1))
-    kv_behind_top = project(behind_top, count)
-    kv_ahead_low = project(ahead_low, 2 * count + half)
-    behind_low, ahead_top, query[0], kv_own, kv_behind_top, kv_ahead_low, ids = (
-        lax.optimization_barrier(
-            (behind_low, ahead_top, query[0], kv_own, kv_behind_top, kv_ahead_low, ids)
-        )
+    behind_low, ahead_top, query[0], kv_own, ids = lax.optimization_barrier(
+        (behind_low, ahead_top, query[0], kv_own, ids)
     )
-    kv_behind_low = project(behind_low, count + half)
-    kv_ahead_top = project(ahead_top, 2 * count)
-    near = [wide_dot(a, w_query) for a in (behind_top, behind_low, ahead_top, ahead_low)]
-    kv_near = (kv_own, kv_behind_top, kv_behind_low, kv_ahead_top, kv_ahead_low)
-    bulk = gather_plane(*[jnp.concatenate(a, axis=0) for a in zip(*kv_near)], False)
-    far_top, far_low, near = lax.optimization_barrier((far_top, far_low, near))
+    behind = jnp.concatenate([behind_top, behind_low], axis=0)
+    ahead = jnp.concatenate([ahead_top, ahead_low], axis=0)
+    kv_behind, kv_ahead = project(behind, count), project(ahead, 2 * count)
+    near = [wide_dot(behind, w_query), wide_dot(ahead, w_query)]
+    far_top, far_low, kv_behind, kv_ahead, near = lax.optimization_barrier(
+        (far_top, far_low, kv_behind, kv_ahead, near)
+    )
     far = jnp.concatenate([far_top, far_low], axis=0)
-    rest = gather_plane(*project(far, 3 * count), True)
+    kv = (kv_own, kv_behind, kv_ahead, project(far, 3 * count))
+    pieces = gather_plane(*[jnp.concatenate(a, axis=0) for a in zip(*kv)])
     query[3] = wide_dot(far, w_query)
     near_rows = jnp.concatenate(near, axis=0)
-    pieces = bulk + rest
 
     def branch(quarters, after=None):
         rows = near_rows if len(quarters) == 2 else query[quarters[0]]

time: 184 us -> 156 us (0.85)
  the two profiles are of different devices: /device:TPU:4 before, /device:TPU:68 now
where the time goes in v3:
time: 156 us; the launch traced here: 155 us
  waiting for transfers between devices  66.5 us (43%)
  Pallas kernels  37.3 us (24%)
  starting transfers between devices  26.7 us (17%)
  matrix products  13.7 us (9%)
  other arithmetic  5.68 us (4%)
  local copies, waits for them, and re-layouts  5.03 us (3%)
    pallas_call x3, Pallas kernels, attend(): pl.pallas_call(functools.partial(attend_kernel, quarters=quarters), out_s...  37.3 us
    dot_general x15, matrix products, wide_dot(): return jnp.dot(a, b, preferred_element_type=jnp.float32)  13.7 us
    ppermute x1, waiting for transfers between devices, ring_gather(): ahead = lax.ppermute(piece, axis, shift(-1))  12.8 us
    ppermute x1, waiting for transfers between devices, body(): far_top = lax.ppermute(behind_top, 'tensor', ring_shift(1))  9.99 us
    ppermute x1, waiting for transfers between devices, body(): behind_low = lax.ppermute(normed[half:], 'tensor', ring_shift(1))  9.8 us
    ppermute x1, waiting for transfers between devices, body(): plain_up = lax.ppermute(plain_up, 'tensor', ring_shift(1))  9.41 us
    ppermute x3, waiting for transfers between devices, gather_plane(): lax.ppermute(mine, 'dp', plane_shift(n, True))  7.59 us
    ppermute x1, waiting for transfers between devices, ring_gather(): lower = lax.ppermute(ahead[half:], axis, shift(-1))  6.93 us
  transfers between devices with their start and end apart: 25, of which 14 were waited for; matrix products, arithmetic and copies ran while one was open for 9% of the time, Pallas kernels for 17%

profile of v3, /device:TPU:68, one launch (start us, length us, event | category | flops | bytes accessed | tf_op | source)
XLA Modules:
  0.0 155.4 jit_solution(15442249441812219630)
XLA Ops:
  0.0 1.6 %fusion.2 = f32[128]{0:T(128)S(1)} fusion(bf16[128,4096]{1,0:T(8,128)(2,1)} %param.8), kind=kLoop, calls=%fused_computation.6 | loop fusion | flops 1572736 | bytes 1049088 | tf_op jit(solution)/shard_map/reduce_sum | solution.py:89
  1.6 1.6 fusion.4
  4.2 1.6 %collective-permute-start.2 = (bf16[64,4096]{1,0:T(8,128)(2,1)}, bf16[64,4096]{1,0:T(8,128)(2,1)S(1)}, u32[]{:S(2)}, u32[]{:S(2)}) collective-permute-start(bf16[64,4096]{1,0:T(8,128)(2,1)} %get-tuple-element.51), channel_id=1, source_target_pairs={{0,1},{1,2},{2,3},{3,0},{4,5},{5,6},{6,7},{7,4},{8,9},{9,10},{10,1... | collective-permute-start | bytes 1572872 | tf_op jit(solution)/shard_map/ppermute | solution.py:304
  5.8 1.7 %collective-permute-start.1 = (bf16[64,4096]{1,0:T(8,128)(2,1)}, bf16[64,4096]{1,0:T(8,128)(2,1)}, u32[]{:S(2)}, u32[]{:S(2)}) collective-permute-start(bf16[64,4096]{1,0:T(8,128)(2,1)} %get-tuple-element.51), channel_id=1, source_target_pairs={{0,3},{1,0},{2,1},{3,2},{4,7},{5,4},{6,5},{7,6},{8,11},{9,8},{10,9... | collective-permute-start | bytes 1572872 | tf_op jit(solution)/shard_map/ppermute | solution.py:307
  7.5 1.8 %collective-permute-start.4 = (bf16[64,4096]{1,0:T(8,128)(2,1)}, bf16[64,4096]{1,0:T(8,128)(2,1)}, u32[]{:S(2)}, u32[]{:S(2)}) collective-permute-start(bf16[64,4096]{1,0:T(8,128)(2,1)} %get-tuple-element.52), channel_id=1, source_target_pairs={{0,3},{1,0},{2,1},{3,2},{4,7},{5,4},{6,5},{7,6},{8,11},{9,8},{10,9... | collective-permute-start | bytes 1572872 | tf_op jit(solution)/shard_map/ppermute | solution.py:305
  10.3 1.7 %fusion.26 = f32[128,128]{1,0:T(8,128)S(1)} fusion(bf16[128,4096]{1,0:T(8,128)(2,1)S(1)} %fusion.4, bf16[4096,128]{1,0:T(8,128)(2,1)} %param.11), kind=kOutput, calls=%fused_computation.77 | convolution fusion | flops 134217728 | bytes 2162688 | tf_op jit(solution)/shard_map/dot_general | solution.py:94
  13.2 3.0 %fusion.25.query = f32[128,512]{1,0:T(8,128)S(1)} fusion(bf16[128,4096]{1,0:T(8,128)(2,1)S(1)} %fusion.4, bf16[4096,512]{1,0:T(8,128)(2,1)} %param.10), kind=kOutput, calls=%fused_computation.76 | convolution fusion | flops 536870912 | bytes 5505024 | tf_op jit(solution)/shard_map/dot_general | solution.py:94
  16.3 4.7 %collective-permute-done.1 = bf16[64,4096]{1,0:T(8,128)(2,1)} collective-permute-done((bf16[64,4096]{1,0:T(8,128)(2,1)}, bf16[64,4096]{1,0:T(8,128)(2,1)}, u32[]{:S(2)}, u32[]{:S(2)}) %collective-permute-start.1) | collective-permute-done | bytes 524320 | tf_op jit(solution)/shard_map/ppermute | solution.py:307
  20.9 9.8 %collective-permute-done = bf16[64,4096]{1,0:T(8,128)(2,1)} collective-permute-done((bf16[64,4096]{1,0:T(8,128)(2,1)}, bf16[64,4096]{1,0:T(8,128)(2,1)}, u32[]{:S(2)}, u32[]{:S(2)}) %collective-permute-start) | collective-permute-done | bytes 524320 | tf_op jit(solution)/shard_map/ppermute | solution.py:306
  31.8 1.1 constant_dynamic-update-slice_fusion.2
  34.6 1.1 constant_dynamic-update-slice_fusion
  37.3 2.7 %collective-permute-start.5 = (bf16[64,4096]{1,0:T(8,128)(2,1)}, bf16[64,4096]{1,0:T(8,128)(2,1)S(1)}, u32[]{:S(2)}, u32[]{:S(2)}) collective-permute-start(bf16[64,4096]{1,0:T(8,128)(2,1)} %collective-permute-done.4), channel_id=1, source_target_pairs={{0,3},{1,0},{2,1},{3,2},{4,7},{5,4},{6,5},{7,6},{8,11},{9,8},{10,9... | collective-permute-start | bytes 1572872 | tf_op jit(solution)/shard_map/ppermute | solution.py:309
  40.8 10.0 %collective-permute-done.3 = bf16[64,4096]{1,0:T(8,128)(2,1)S(1)} collective-permute-done((bf16[64,4096]{1,0:T(8,128)(2,1)S(1)}, bf16[64,4096]{1,0:T(8,128)(2,1)S(1)}, u32[]{:S(2)}, u32[]{:S(2)}) %collective-permute-start.3) | collective-permute-done | bytes 524320 | tf_op jit(solution)/shard_map/ppermute | solution.py:308
  52.2 1.3 collective-permute-done.6
  53.7 3.1 %collective-permute-start.8 = (bf16[1024,128]{1,0:T(8,128)(2,1)S(1)}, bf16[1024,128]{1,0:T(8,128)(2,1)S(1)}, u32[]{:S(2)}, u32[]{:S(2)}) collective-permute-start(bf16[1024,128]{1,0:T(8,128)(2,1)S(1)} %broadcast_select_fusion), channel_id=1, source_target_pairs={{0,24},{4,100},{8,0},{12,108},{16,8},{20,116},{24,16},{28,124},{32... | collective-permute-start | bytes 786440 | tf_op jit(solution)/shard_map/ppermute | solution.py:62
  56.8 4.9 %collective-permute-done.9 = bf16[1024,128]{1,0:T(8,128)(2,1)S(1)} collective-permute-done((bf16[1024,128]{1,0:T(8,128)(2,1)S(1)}, bf16[1024,128]{1,0:T(8,128)(2,1)S(1)}, u32[]{:S(2)}, u32[]{:S(2)}) %collective-permute-start.9) | collective-permute-done | bytes 262176 | tf_op jit(solution)/shard_map/ppermute | solution.py:62
  61.7 1.4 collective-permute-done.8
  63.0 1.4 collective-permute-done.7
  65.1 1.5 collective-permute-start.10
  66.6 12.8 %collective-permute-done.11.refs_2_ = bf16[4096,128]{1,0:T(8,128)(2,1)S(1)} collective-permute-done((bf16[4096,128]{1,0:T(8,128)(2,1)S(1)}, bf16[4096,128]{1,0:T(8,128)(2,1)S(1)}, u32[]{:S(2)}, u32[]{:S(2)}) %collective-permute-start.11) | collective-permute-done | bytes 1048608 | tf_op jit(solution)/shard_map/ppermute | solution.py:48
  80.0 2.1 %collective-permute-start.12 = (bf16[2048,128]{1,0:T(8,128)(2,1)S(1)}, bf16[2048,128]{1,0:T(8,128)(2,1)S(1)}, u32[]{:S(2)}, u32[]{:S(2)}) collective-permute-start(bf16[2048,128]{1,0:T(8,128)(2,1)S(1)} %slice.134), channel_id=1, source_target_pairs={{0,32},{4,12},{8,40},{12,20},{16,48},{20,28},{24,56},{28,4},{32,64... | collective-permute-start | bytes 1572872 | tf_op jit(solution)/shard_map/ppermute | solution.py:49
  82.1 6.9 %collective-permute-done.13.refs_4_ = bf16[2048,128]{1,0:T(8,128)(2,1)S(1)} collective-permute-done((bf16[2048,128]{1,0:T(8,128)(2,1)S(1)}, bf16[2048,128]{1,0:T(8,128)(2,1)S(1)}, u32[]{:S(2)}, u32[]{:S(2)}) %collective-permute-start.13) | collective-permute-done | bytes 524320 | tf_op jit(solution)/shard_map/ppermute | solution.py:50
  91.7 10.2 %attend.3 = bf16[128,512]{1,0:T(8,128)(2,1)S(1)} custom-call(s32[2]{0:T(128)S(1)} %pad_add_fusion.ids, s32[16]{0:T(128)S(1)} %copy-done.1, f32[128,512]{1,0:T(8,128)S(1)} %fusion.31.query, f32[512,128]{1,0:T(8,128)S(1)} %get-tuple-element.65.cos_part, f32[512,128]{1,0:T(8,128)S(1)} %get-tuple-element.66.sin_part, ...), custom_call_target="tpu_custom_call" | custom-call | flops 1073741824 | bytes 4194304 | tf_op jit(solution)/shard_map/attend/pallas_call | solution.py:259
  102.7 3.2 %collective-permute-start.20 = (bf16[128,2048]{1,0:T(8,128)(2,1)S(1)}, bf16[128,2048]{1,0:T(8,128)(2,1)S(1)}, u32[]{:S(2)}, u32[]{:S(2)}) collective-permute-start(bf16[128,2048]{1,0:T(8,128)(2,1)S(1)} %get-tuple-element.49), channel_id=1, source_target_pairs={{0,3},{1,0},{2,1},{3,2},{4,7},{5,4},{6,5},{7,6},{8,11},{9,8},{10,9... | collective-permute-start | bytes 1572872 | tf_op jit(solution)/shard_map/ppermute | solution.py:338
  106.0 16.9 %attend.4 = bf16[256,512]{1,0:T(8,128)(2,1)S(1)} custom-call(s32[2]{0:T(128)S(1)} %pad_add_fusion.ids, s32[16]{0:T(128)S(1)} %copy-done.1, f32[256,512]{1,0:T(8,128)S(1)} %pad_maximum_fusion.1.query, f32[512,128]{1,0:T(8,128)S(1)} %get-tuple-element.65.cos_part, f32[512,128]{1,0:T(8,128)S(1)} %get-tuple-element.66.sin_part, ...), custom_call_target="tpu_custom_call" | custom-call | flops 2147483648 | bytes 4194304 | tf_op jit(solution)/shard_map/attend/pallas_call | solution.py:259
  122.9 1.3 fusion.24
  124.2 3.3 %collective-permute-start.22 = (bf16[128,2048]{1,0:T(8,128)(2,1)S(1)}, bf16[128,2048]{1,0:T(8,128)(2,1)S(1)}, u32[]{:S(2)}, u32[]{:S(2)}) collective-permute-start(bf16[128,2048]{1,0:T(8,128)(2,1)S(1)} %get-tuple-element.47), channel_id=1, source_target_pairs={{0,3},{1,0},{2,1},{3,2},{4,7},{5,4},{6,5},{7,6},{8,11},{9,8},{10,9... | collective-permute-start | bytes 1572872 | tf_op jit(solution)/shard_map/ppermute | solution.py:343
  128.0 3.2 %collective-permute-start.24 = (bf16[128,2048]{1,0:T(8,128)(2,1)S(1)}, bf16[128,2048]{1,0:T(8,128)(2,1)S(1)}, u32[]{:S(2)}, u32[]{:S(2)}) collective-permute-start(bf16[128,2048]{1,0:T(8,128)(2,1)S(1)} %get-tuple-element.42), channel_id=1, source_target_pairs={{0,3},{1,0},{2,1},{3,2},{4,7},{5,4},{6,5},{7,6},{8,11},{9,8},{10,9... | collective-permute-start | bytes 1572872 | tf_op jit(solution)/shard_map/ppermute | solution.py:348
  131.3 10.2 %attend.5 = bf16[128,512]{1,0:T(8,128)(2,1)S(1)} custom-call(s32[2]{0:T(128)S(1)} %pad_add_fusion.ids, s32[16]{0:T(128)S(1)} %copy-done.1, f32[128,512]{1,0:T(8,128)S(1)} %fusion.25.query, f32[512,128]{1,0:T(8,128)S(1)} %get-tuple-element.65.cos_part, f32[512,128]{1,0:T(8,128)S(1)} %get-tuple-element.66.sin_part, ...), custom_call_target="tpu_custom_call" | custom-call | flops 1073741824 | bytes 4194304 | tf_op jit(solution)/shard_map/attend/pallas_call | solution.py:259
  141.5 2.4 %collective-permute-done.21 = bf16[128,2048]{1,0:T(8,128)(2,1)S(1)} collective-permute-done((bf16[128,2048]{1,0:T(8,128)(2,1)S(1)}, bf16[128,2048]{1,0:T(8,128)(2,1)S(1)}, u32[]{:S(2)}, u32[]{:S(2)}) %collective-permute-start.21) | collective-permute-done | bytes 524320 | tf_op jit(solution)/shard_map/ppermute | solution.py:347
  144.1 9.4 %collective-permute-done.23 = bf16[128,2048]{1,0:T(8,128)(2,1)S(1)} collective-permute-done((bf16[128,2048]{1,0:T(8,128)(2,1)S(1)}, bf16[128,2048]{1,0:T(8,128)(2,1)S(1)}, u32[]{:S(2)}, u32[]{:S(2)}) %collective-permute-start.23) | collective-permute-done | bytes 524320 | tf_op jit(solution)/shard_map/ppermute | solution.py:341
  153.6 1.8 %fusion.1 = bf16[128,4096]{1,0:T(8,128)(2,1)} fusion(bf16[128,512]{1,0:T(8,128)(2,1)S(1)} %attend.5, bf16[512,4096]{1,0:T(8,128)(2,1)S(1)} %copy-done.3, bf16[128,4096]{1,0:T(8,128)(2,1)S(1)} %copy-done.5, f32[128,2048]{1,0:T(8,128)S(1)} %convert_add_fusion, f32[128,2048]{1,0:T(8,128)S(1)} %convert_add_fusion.1), kind=kOutput, calls=%fused_computation.2 | convolution fusion | flops 539492352 | bytes 8519680 | tf_op jit(solution)/shard_map/dot_general | solution.py:94
  (94 shorter events, 15.5 us)
Async XLA Ops:
  0.0 9.9 %copy-start = (bf16[4096,128]{1,0:T(8,128)(2,1)S(1)}, bf16[4096,128]{1,0:T(8,128)(2,1)}, u32[]{:S(2)}) copy-start(bf16[4096,128]{1,0:T(8,128)(2,1)} %param.12) | copy-start | bytes 3145732
  0.0 9.6 %copy-start.6 = (s32[4]{0:T(128)S(1)}, s32[4]{0:T(128)}, u32[]{:S(2)}) copy-start(s32[4]{0:T(128)} %constant.41.clone) | copy-start | bytes 52
  0.0 9.5 %copy-start.1 = (s32[16]{0:T(128)S(1)}, s32[16]{0:T(128)}, u32[]{:S(2)}) copy-start(s32[16]{0:T(128)} %lengths.5) | copy-start | bytes 196
  4.2 30.3 %collective-permute-start.2 = (bf16[64,4096]{1,0:T(8,128)(2,1)}, bf16[64,4096]{1,0:T(8,128)(2,1)S(1)}, u32[]{:S(2)}, u32[]{:S(2)}) collective-permute-start(bf16[64,4096]{1,0:T(8,128)(2,1)} %get-tuple-element.51), channel_id=1, source_target_pairs={{0,1},{1,2},{2,3},{3,0},{4,5},{5,6},{6,7},{7,4},{8,9},{9,10},{10,1... | collective-permute-start | bytes 1572872 | tf_op jit(solution)/shard_map/ppermute | solution.py:304
  5.8 15.1 %collective-permute-start.1 = (bf16[64,4096]{1,0:T(8,128)(2,1)}, bf16[64,4096]{1,0:T(8,128)(2,1)}, u32[]{:S(2)}, u32[]{:S(2)}) collective-permute-start(bf16[64,4096]{1,0:T(8,128)(2,1)} %get-tuple-element.51), channel_id=1, source_target_pairs={{0,3},{1,0},{2,1},{3,2},{4,7},{5,4},{6,5},{7,6},{8,11},{9,8},{10,9... | collective-permute-start | bytes 1572872 | tf_op jit(solution)/shard_map/ppermute | solution.py:307
  7.5 24.3 %collective-permute-start.4 = (bf16[64,4096]{1,0:T(8,128)(2,1)}, bf16[64,4096]{1,0:T(8,128)(2,1)}, u32[]{:S(2)}, u32[]{:S(2)}) collective-permute-start(bf16[64,4096]{1,0:T(8,128)(2,1)} %get-tuple-element.52), channel_id=1, source_target_pairs={{0,3},{1,0},{2,1},{3,2},{4,7},{5,4},{6,5},{7,6},{8,11},{9,8},{10,9... | collective-permute-start | bytes 1572872 | tf_op jit(solution)/shard_map/ppermute | solution.py:305
  9.3 21.4 %collective-permute-start = (bf16[64,4096]{1,0:T(8,128)(2,1)}, bf16[64,4096]{1,0:T(8,128)(2,1)}, u32[]{:S(2)}, u32[]{:S(2)}) collective-permute-start(bf16[64,4096]{1,0:T(8,128)(2,1)} %get-tuple-element.52), channel_id=1, source_target_pairs={{0,1},{1,2},{2,3},{3,0},{4,5},{5,6},{6,7},{7,4},{8,9},{9,10},{10,1... | collective-permute-start | bytes 1572872 | tf_op jit(solution)/shard_map/ppermute | solution.py:306
  13.2 19.7 %copy-start.4 = (bf16[4096,128]{1,0:T(8,128)(2,1)S(1)}, bf16[4096,128]{1,0:T(8,128)(2,1)}, u32[]{:S(2)}) copy-start(bf16[4096,128]{1,0:T(8,128)(2,1)} %param.11) | copy-start | bytes 3145732
  16.2 17.6 %copy-start.2 = (bf16[4096,512]{1,0:T(8,128)(2,1)S(1)}, bf16[4096,512]{1,0:T(8,128)(2,1)}, u32[]{:S(2)}) copy-start(bf16[4096,512]{1,0:T(8,128)(2,1)} %param.10) | copy-start | bytes 12582916
  36.7 14.1 %collective-permute-start.3 = (bf16[64,4096]{1,0:T(8,128)(2,1)S(1)}, bf16[64,4096]{1,0:T(8,128)(2,1)S(1)}, u32[]{:S(2)}, u32[]{:S(2)}) collective-permute-start(bf16[64,4096]{1,0:T(8,128)(2,1)S(1)} %collective-permute-done.2), channel_id=1, source_target_pairs={{0,1},{1,2},{2,3},{3,0},{4,5},{5,6},{6,7},{7,4},{8,9},{9,10},{10,1... | collective-permute-start | bytes 1572872 | tf_op jit(solution)/shard_map/ppermute | solution.py:308
  37.3 13.6 %collective-permute-start.5 = (bf16[64,4096]{1,0:T(8,128)(2,1)}, bf16[64,4096]{1,0:T(8,128)(2,1)S(1)}, u32[]{:S(2)}, u32[]{:S(2)}) collective-permute-start(bf16[64,4096]{1,0:T(8,128)(2,1)} %collective-permute-done.4), channel_id=1, source_target_pairs={{0,3},{1,0},{2,1},{3,2},{4,7},{5,4},{6,5},{7,6},{8,11},{9,8},{10,9... | collective-permute-start | bytes 1572872 | tf_op jit(solution)/shard_map/ppermute | solution.py:309
  52.1 1.4 collective-permute-start.6
  53.6 8.1 %collective-permute-start.9 = (bf16[1024,128]{1,0:T(8,128)(2,1)S(1)}, bf16[1024,128]{1,0:T(8,128)(2,1)S(1)}, u32[]{:S(2)}, u32[]{:S(2)}) collective-permute-start(bf16[1024,128]{1,0:T(8,128)(2,1)S(1)} %broadcast_select_fusion), channel_id=1, source_target_pairs={{0,16},{4,68},{8,24},{12,76},{16,0},{20,84},{24,8},{28,92},{32,48}... | collective-permute-start | bytes 786440 | tf_op jit(solution)/shard_map/ppermute | solution.py:62
  53.7 9.3 %collective-permute-start.8 = (bf16[1024,128]{1,0:T(8,128)(2,1)S(1)}, bf16[1024,128]{1,0:T(8,128)(2,1)S(1)}, u32[]{:S(2)}, u32[]{:S(2)}) collective-permute-start(bf16[1024,128]{1,0:T(8,128)(2,1)S(1)} %broadcast_select_fusion), channel_id=1, source_target_pairs={{0,24},{4,100},{8,0},{12,108},{16,8},{20,116},{24,16},{28,124},{32... | collective-permute-start | bytes 786440 | tf_op jit(solution)/shard_map/ppermute | solution.py:62
  56.8 7.6 %collective-permute-start.7 = (bf16[1024,128]{1,0:T(8,128)(2,1)S(1)}, bf16[1024,128]{1,0:T(8,128)(2,1)S(1)}, u32[]{:S(2)}, u32[]{:S(2)}) collective-permute-start(bf16[1024,128]{1,0:T(8,128)(2,1)S(1)} %broadcast_select_fusion), channel_id=1, source_target_pairs={{0,8},{4,36},{8,16},{12,44},{16,24},{20,52},{24,0},{28,60},{32,40}... | collective-permute-start | bytes 786440 | tf_op jit(solution)/shard_map/ppermute | solution.py:62
  64.5 14.9 %collective-permute-start.11 = (bf16[4096,128]{1,0:T(8,128)(2,1)S(1)}, bf16[4096,128]{1,0:T(8,128)(2,1)S(1)}, u32[]{:S(2)}, u32[]{:S(2)}) collective-permute-start(bf16[4096,128]{1,0:T(8,128)(2,1)S(1)} %pad_maximum_fusion.refs_0_), channel_id=1, source_target_pairs={{0,96},{4,28},{8,104},{12,4},{16,112},{20,12},{24,120},{28,20},{32... | collective-permute-start | bytes 3145736 | tf_op jit(solution)/shard_map/ppermute | solution.py:48
  65.1 14.9 %collective-permute-start.10 = (bf16[4096,128]{1,0:T(8,128)(2,1)S(1)}, bf16[4096,128]{1,0:T(8,128)(2,1)S(1)}, u32[]{:S(2)}, u32[]{:S(2)}) collective-permute-start(bf16[4096,128]{1,0:T(8,128)(2,1)S(1)} %pad_maximum_fusion.refs_0_), channel_id=1, source_target_pairs={{0,32},{4,12},{8,40},{12,20},{16,48},{20,28},{24,56},{28,4},{32,64... | collective-permute-start | bytes 3145736 | tf_op jit(solution)/shard_map/ppermute | solution.py:47
  66.6 23.8 %collective-permute-start.14 = (bf16[4096,128]{1,0:T(8,128)(2,1)S(1)}, bf16[4096,128]{1,0:T(8,128)(2,1)S(1)}, u32[]{:S(2)}, u32[]{:S(2)}) collective-permute-start(bf16[4096,128]{1,0:T(8,128)(2,1)S(1)} %pad_maximum_fusion.refs_0_), channel_id=1, source_target_pairs={{0,4},{4,0},{8,12},{12,8},{16,20},{20,16},{24,28},{28,24},{32,36},... | collective-permute-start | bytes 3145736 | tf_op jit(solution)/shard_map/ppermute | solution.py:65
  79.4 9.6 %collective-permute-start.13 = (bf16[2048,128]{1,0:T(8,128)(2,1)S(1)}, bf16[2048,128]{1,0:T(8,128)(2,1)S(1)}, u32[]{:S(2)}, u32[]{:S(2)}) collective-permute-start(bf16[2048,128]{1,0:T(8,128)(2,1)S(1)} %slice.135), channel_id=1, source_target_pairs={{0,96},{4,28},{8,104},{12,4},{16,112},{20,12},{24,120},{28,20},{32... | collective-permute-start | bytes 1572872 | tf_op jit(solution)/shard_map/ppermute | solution.py:50
  80.0 10.9 %collective-permute-start.16 = (bf16[4096,128]{1,0:T(8,128)(2,1)S(1)}, bf16[4096,128]{1,0:T(8,128)(2,1)S(1)}, u32[]{:S(2)}, u32[]{:S(2)}) collective-permute-start(bf16[4096,128]{1,0:T(8,128)(2,1)S(1)} %collective-permute-done.11.refs_2_), channel_id=1, source_target_pairs={{0,4},{4,0},{8,12},{12,8},{16,20},{20,16},{24,28},{28,24},{32,36},... | collective-permute-start | bytes 3145736 | tf_op jit(solution)/shard_map/ppermute | solution.py:65
  80.0 9.3 %collective-permute-start.12 = (bf16[2048,128]{1,0:T(8,128)(2,1)S(1)}, bf16[2048,128]{1,0:T(8,128)(2,1)S(1)}, u32[]{:S(2)}, u32[]{:S(2)}) collective-permute-start(bf16[2048,128]{1,0:T(8,128)(2,1)S(1)} %slice.134), channel_id=1, source_target_pairs={{0,32},{4,12},{8,40},{12,20},{16,48},{20,28},{24,56},{28,4},{32,64... | collective-permute-start | bytes 1572872 | tf_op jit(solution)/shard_map/ppermute | solution.py:49
  82.1 9.6 %collective-permute-start.15 = (bf16[4096,128]{1,0:T(8,128)(2,1)S(1)}, bf16[4096,128]{1,0:T(8,128)(2,1)S(1)}, u32[]{:S(2)}, u32[]{:S(2)}) collective-permute-start(bf16[4096,128]{1,0:T(8,128)(2,1)S(1)} %collective-permute-done.10.refs_1_), channel_id=1, source_target_pairs={{0,4},{4,0},{8,12},{12,8},{16,20},{20,16},{24,28},{28,24},{32,36},... | collective-permute-start | bytes 3145736 | tf_op jit(solution)/shard_map/ppermute | solution.py:65
  89.0 1.9 %collective-permute-start.18 = (bf16[2048,128]{1,0:T(8,128)(2,1)S(1)}, bf16[2048,128]{1,0:T(8,128)(2,1)S(1)}, u32[]{:S(2)}, u32[]{:S(2)}) collective-permute-start(bf16[2048,128]{1,0:T(8,128)(2,1)S(1)} %collective-permute-done.13.refs_4_), channel_id=1, source_target_pairs={{0,4},{4,0},{8,12},{12,8},{16,20},{20,16},{24,28},{28,24},{32,36},... | collective-permute-start | bytes 1572872 | tf_op jit(solution)/shard_map/ppermute | solution.py:66
  89.3 2.4 %collective-permute-start.17 = (bf16[2048,128]{1,0:T(8,128)(2,1)S(1)}, bf16[2048,128]{1,0:T(8,128)(2,1)S(1)}, u32[]{:S(2)}, u32[]{:S(2)}) collective-permute-start(bf16[2048,128]{1,0:T(8,128)(2,1)S(1)} %collective-permute-done.12.refs_3_), channel_id=1, source_target_pairs={{0,4},{4,0},{8,12},{12,8},{16,20},{20,16},{24,28},{28,24},{32,36},... | collective-permute-start | bytes 1572872 | tf_op jit(solution)/shard_map/ppermute | solution.py:66
  90.4 11.6 %copy-start.3 = (bf16[512,4096]{1,0:T(8,128)(2,1)S(1)}, bf16[512,4096]{1,0:T(8,128)(2,1)}, u32[]{:S(2)}) copy-start(bf16[512,4096]{1,0:T(8,128)(2,1)} %param.13) | copy-start | bytes 12582916
  102.7 24.8 %collective-permute-start.20 = (bf16[128,2048]{1,0:T(8,128)(2,1)S(1)}, bf16[128,2048]{1,0:T(8,128)(2,1)S(1)}, u32[]{:S(2)}, u32[]{:S(2)}) collective-permute-start(bf16[128,2048]{1,0:T(8,128)(2,1)S(1)} %get-tuple-element.49), channel_id=1, source_target_pairs={{0,3},{1,0},{2,1},{3,2},{4,7},{5,4},{6,5},{7,6},{8,11},{9,8},{10,9... | collective-permute-start | bytes 1572872 | tf_op jit(solution)/shard_map/ppermute | solution.py:338
  106.0 21.6 %collective-permute-start.19 = (bf16[128,2048]{1,0:T(8,128)(2,1)S(1)}, bf16[128,2048]{1,0:T(8,128)(2,1)S(1)}, u32[]{:S(2)}, u32[]{:S(2)}) collective-permute-start(bf16[128,2048]{1,0:T(8,128)(2,1)S(1)} %get-tuple-element.50), channel_id=1, source_target_pairs={{0,1},{1,2},{2,3},{3,0},{4,5},{5,6},{6,7},{7,4},{8,9},{9,10},{10,1... | collective-permute-start | bytes 1572872 | tf_op jit(solution)/shard_map/ppermute | solution.py:337
  124.2 17.3 %collective-permute-start.22 = (bf16[128,2048]{1,0:T(8,128)(2,1)S(1)}, bf16[128,2048]{1,0:T(8,128)(2,1)S(1)}, u32[]{:S(2)}, u32[]{:S(2)}) collective-permute-start(bf16[128,2048]{1,0:T(8,128)(2,1)S(1)} %get-tuple-element.47), channel_id=1, source_target_pairs={{0,3},{1,0},{2,1},{3,2},{4,7},{5,4},{6,5},{7,6},{8,11},{9,8},{10,9... | collective-permute-start | bytes 1572872 | tf_op jit(solution)/shard_map/ppermute | solution.py:343
  127.9 16.1 %collective-permute-start.21 = (bf16[128,2048]{1,0:T(8,128)(2,1)S(1)}, bf16[128,2048]{1,0:T(8,128)(2,1)S(1)}, u32[]{:S(2)}, u32[]{:S(2)}) collective-permute-start(bf16[128,2048]{1,0:T(8,128)(2,1)S(1)} %get-tuple-element.41), channel_id=1, source_target_pairs={{0,1},{1,2},{2,3},{3,0},{4,5},{5,6},{6,7},{7,4},{8,9},{9,10},{10,1... | collective-permute-start | bytes 1572872 | tf_op jit(solution)/shard_map/ppermute | solution.py:347
  128.0 25.5 %collective-permute-start.23 = (bf16[128,2048]{1,0:T(8,128)(2,1)S(1)}, bf16[128,2048]{1,0:T(8,128)(2,1)S(1)}, u32[]{:S(2)}, u32[]{:S(2)}) collective-permute-start(bf16[128,2048]{1,0:T(8,128)(2,1)S(1)} %get-tuple-element.48), channel_id=1, source_target_pairs={{0,1},{1,2},{2,3},{3,0},{4,5},{5,6},{6,7},{7,4},{8,9},{9,10},{10,1... | collective-permute-start | bytes 1572872 | tf_op jit(solution)/shard_map/ppermute | solution.py:341
  128.0 25.5 %collective-permute-start.24 = (bf16[128,2048]{1,0:T(8,128)(2,1)S(1)}, bf16[128,2048]{1,0:T(8,128)(2,1)S(1)}, u32[]{:S(2)}, u32[]{:S(2)}) collective-permute-start(bf16[128,2048]{1,0:T(8,128)(2,1)S(1)} %get-tuple-element.42), channel_id=1, source_target_pairs={{0,3},{1,0},{2,1},{3,2},{4,7},{5,4},{6,5},{7,6},{8,11},{9,8},{10,9... | collective-permute-start | bytes 1572872 | tf_op jit(solution)/shard_map/ppermute | solution.py:348
  141.5 12.1 %copy-start.5 = (bf16[128,4096]{1,0:T(8,128)(2,1)S(1)}, bf16[128,4096]{1,0:T(8,128)(2,1)}, u32[]{:S(2)}) copy-start(bf16[128,4096]{1,0:T(8,128)(2,1)} %param.8) | copy-start | bytes 3145732

commit v4 on v3

--- a/solution.py
+++ b/solution.py
@@ -84,10 +84,32 @@
     return jnp.cos(angles), jnp.sin(angles) * sign[None, :]
 
 
+def norm_kernel(tokens, gain, normed, top, low):
+    count = tokens.shape[0]
+    half = count // 2
+    for at in range(0, count, 16):
+        wide = tokens[at : at + 16, :].astype(jnp.float32)
+        inverse = lax.rsqrt(jnp.mean(wide * wide, axis=1, keepdims=True) + epsilon)
+        rows = (wide * inverse * gain[...]).astype(jnp.bfloat16)
+        normed[at : at + 16, :] = rows
+        if at < half:
+            top[at : at + 16, :] = rows
+        else:
+            low[at - half : at - half + 16, :] = rows
+
+
 def norm(tokens, norm_gain):
-    wide = tokens.astype(jnp.float32)
-    inverse = lax.rsqrt(jnp.mean(wide * wide, axis=1, keepdims=True) + epsilon)
-    return (wide * inverse * norm_gain[None, :]).astype(jnp.bfloat16)
+    count, width = tokens.shape
+    vmem = pl.BlockSpec(memory_space=pltpu.VMEM)
+    shapes = [(count, width), (count // 2, width), (count // 2, width)]
+    return pl.pallas_call(
+        norm_kernel,
+        out_shape=[jax.ShapeDtypeStruct(shape, jnp.bfloat16) for shape in shapes],
+        in_specs=[vmem, vmem],
+        out_specs=[vmem] * 3,
+        compiler_params=pltpu.CompilerParams(vmem_limit_bytes=16 * 2**20),
+        name="norm",
+    )(tokens, norm_gain[None, :])
 
 
 def wide_dot(a, b):
@@ -198,21 +220,22 @@
             at = slice(r * ROWS, (r + 1) * ROWS)
             local = (r * ROWS) % max(count, ROWS)
 
-            def part(c):
-                here = scores[at, c : c + HEAD_SIZE]
+            columns = range(0, size, HEAD_SIZE)
+            old, best = peak[at, :], None
+            for c in columns:
+                part = scores[at, c : c + HEAD_SIZE]
                 if cut:
-                    here = jnp.where(
-                        scores_seen[local : local + ROWS, c : c + HEAD_SIZE], here, masked
-                    )
-                return here
-
-            old = peak[at, :]
-            columns = range(0, size, HEAD_SIZE)
-            best = functools.reduce(jnp.maximum, [part(c) for c in columns])
+                    seen = scores_seen[local : local + ROWS, c : c + HEAD_SIZE]
+                    part = jnp.where(seen, part, masked)
+                    scores[at, c : c + HEAD_SIZE] = part
+                best = part if best is None else jnp.maximum(best, part)
             fresh = jnp.maximum(old, jnp.max(best, axis=1, keepdims=True))
             peak[at, :] = fresh
             shrink = jnp.exp2((old - fresh) * exp2_scale)
-            probs = [jnp.exp2((part(c) - fresh) * exp2_scale).astype(jnp.bfloat16) for c in columns]
+            probs = [
+                jnp.exp2((scores[at, c : c + HEAD_SIZE] - fresh) * exp2_scale).astype(jnp.bfloat16)
+                for c in columns
+            ]
             update = wide_dot(jnp.concatenate(probs, axis=1), block_values)
             summed[at, :HEAD_SIZE] = summed[at, :HEAD_SIZE] * shrink + update[:, :HEAD_SIZE]
             summed[at, HEAD_SIZE:] = summed[at, HEAD_SIZE:] * shrink + update[:, HEAD_SIZE:]
@@ -283,7 +306,7 @@
 def body(tokens, norm_gain, w_query, key_weight, value_weight, w_out, lengths):
     count = tokens.shape[0]
     dp, mine = lax.axis_index("dp"), lax.axis_index("tensor")
-    normed = norm(tokens, norm_gain)
+    normed, normed_top, normed_low = norm(tokens, norm_gain)
     quarter = (mine + jnp.array(RELATIVE, jnp.int32)) & 3
     local = (quarter[:, None] * count + jnp.arange(count, dtype=jnp.int32)[None, :]).reshape(-1)
     positions = dp * (RING * count) + local
@@ -301,10 +324,10 @@
     query = [None] * RING
     kv_own = project(normed, 0)
     query[0] = wide_dot(normed, w_query)
-    behind_top = lax.ppermute(normed[:half], "tensor", ring_shift(1))
-    ahead_low = lax.ppermute(normed[half:], "tensor", ring_shift(-1))
-    behind_low = lax.ppermute(normed[half:], "tensor", ring_shift(1))
-    ahead_top = lax.ppermute(normed[:half], "tensor", ring_shift(-1))
+    behind_top = lax.ppermute(normed_top, "tensor", ring_shift(1))
+    ahead_low = lax.ppermute(normed_low, "tensor", ring_shift(-1))
+    behind_low = lax.ppermute(normed_low, "tensor", ring_shift(1))
+    ahead_top = lax.ppermute(normed_top, "tensor", ring_shift(-1))
     far_top = lax.ppermute(behind_top, "tensor", ring_shift(1))
     far_low = lax.ppermute(ahead_low, "tensor", ring_shift(-1))
     behind_low, ahead_top, query[0], kv_own, ids = lax.optimization_barrier(

time: 156 us -> 156 us (level)
  local copies, waits for them, and re-layouts: 5.03 us -> 7.1 us
    ppermute x1, waiting for transfers between devices: 0.01 us -> 9.79 us  [body(): far_low = lax.ppermute(ahead_low, 'tensor', ring_shift(-1))]
    ppermute x1, waiting for transfers between devices: 9.99 us -> 3.31 us  [body(): far_top = lax.ppermute(behind_top, 'tensor', ring_shift(1))]
    ppermute x4, waiting for transfers between devices: 14.5 us -> 10.6 us  [the longest x1 6.31 us: body(): ahead_top = lax.ppermute(normed_top, 'tensor', ring_shift(-1))]
    unnamed x24 -> x26, local copies, waits for them, and re-layouts: 1.27 us -> 4.34 us
    ppermute x1, starting transfers between devices: 3.25 us -> 0.35 us  [body(): from_ahead = lax.ppermute(far[:, half:], 'tensor', ring_shift(-1))]
    ppermute x1, starting transfers between devices: 0.01 us -> 1.75 us  [body(): from_behind = lax.ppermute(far[:, :half], 'tensor', ring_shift(1))]
    ppermute x1, starting transfers between devices: 3.3 us -> 1.56 us  [body(): plain_down = lax.ppermute(plain_down, 'tensor', ring_shift(-1))]
    reduce_sum x1 -> x0, other arithmetic: 1.63 us -> none  [norm(): inverse = lax.rsqrt(jnp.mean(wide * wide, axis=1, keepdims=True) + epsilon)]
  transfers between devices with their start and end apart: 25 -> 25, of which waited for: 14 -> 15; matrix products, arithmetic and copies ran while one was open for 9% -> 10% of each run, Pallas kernels for 17% -> 17%
where the time goes in v4:
time: 156 us
  waiting for transfers between devices  65.4 us (42%)
  Pallas kernels  38.7 us (25%)
  starting transfers between devices  25.9 us (17%)
  matrix products  13.6 us (9%)
  local copies, waits for them, and re-layouts  7.1 us (5%)
  other arithmetic  4.45 us (3%)
    pallas_call x3, Pallas kernels, attend(): pl.pallas_call(functools.partial(attend_kernel, quarters=quarters), out_s...  37.3 us
    dot_general x15, matrix products, wide_dot(): return jnp.dot(a, b, preferred_element_type=jnp.float32)  13.6 us
    ppermute x1, waiting for transfers between devices, ring_gather(): ahead = lax.ppermute(piece, axis, shift(-1))  12.8 us
    ppermute x1, waiting for transfers between devices, body(): far_low = lax.ppermute(ahead_low, 'tensor', ring_shift(-1))  9.79 us
    ppermute x1, waiting for transfers between devices, body(): plain_up = lax.ppermute(plain_up, 'tensor', ring_shift(1))  9.52 us
    ppermute x3, waiting for transfers between devices, gather_plane(): lax.ppermute(mine, 'dp', plane_shift(n, True))  7.59 us
    ppermute x1, waiting for transfers between devices, ring_gather(): lower = lax.ppermute(ahead[half:], axis, shift(-1))  6.93 us
    ppermute x1, waiting for transfers between devices, body(): ahead_top = lax.ppermute(normed_top, 'tensor', ring_shift(-1))  6.31 us
  transfers between devices with their start and end apart: 25, of which 15 were waited for; matrix products, arithmetic and copies ran while one was open for 10% of the time, Pallas kernels for 17%

profile of v4, /device:TPU:68, one launch (start us, length us, event | category | flops | bytes accessed | tf_op | source)
XLA Modules:
  0.0 155.6 jit_solution(17212656978041603086)
XLA Ops:
  0.0 1.3 copy-done.1
  2.0 1.4 norm.1
  3.4 3.0 %collective-permute-start.4 = (bf16[64,4096]{1,0:T(8,128)(2,1)}, bf16[64,4096]{1,0:T(8,128)(2,1)}, u32[]{:S(2)}, u32[]{:S(2)}) collective-permute-start(bf16[64,4096]{1,0:T(8,128)(2,1)} %get-tuple-element.27), channel_id=1, source_target_pairs={{0,3},{1,0},{2,1},{3,2},{4,7},{5,4},{6,5},{7,6},{8,11},{9,8},{10,9... | collective-permute-start | bytes 1572872 | tf_op jit(solution)/shard_map/ppermute | solution.py:328
  7.0 2.7 %collective-permute-start.1 = (bf16[64,4096]{1,0:T(8,128)(2,1)S(1)}, bf16[64,4096]{1,0:T(8,128)(2,1)}, u32[]{:S(2)}, u32[]{:S(2)}) collective-permute-start(bf16[64,4096]{1,0:T(8,128)(2,1)S(1)} %get-tuple-element.28), channel_id=1, source_target_pairs={{0,3},{1,0},{2,1},{3,2},{4,7},{5,4},{6,5},{7,6},{8,11},{9,8},{10,9... | collective-permute-start | bytes 1572872 | tf_op jit(solution)/shard_map/ppermute | solution.py:330
  12.4 1.7 %fusion.22 = f32[128,128]{1,0:T(8,128)S(1)} fusion(bf16[128,4096]{1,0:T(8,128)(2,1)S(1)} %get-tuple-element.29, bf16[4096,128]{1,0:T(8,128)(2,1)} %param.11), kind=kOutput, calls=%fused_computation.70 | convolution fusion | flops 134217728 | bytes 2162688 | tf_op jit(solution)/shard_map/dot_general | solution.py:116
  15.3 3.0 %fusion.21.query = f32[128,512]{1,0:T(8,128)S(1)} fusion(bf16[128,4096]{1,0:T(8,128)(2,1)S(1)} %get-tuple-element.29, bf16[4096,512]{1,0:T(8,128)(2,1)} %param.10), kind=kOutput, calls=%fused_computation.69 | convolution fusion | flops 536870912 | bytes 5505024 | tf_op jit(solution)/shard_map/dot_general | solution.py:116
  18.4 4.3 %collective-permute-done = bf16[64,4096]{1,0:T(8,128)(2,1)} collective-permute-done((bf16[64,4096]{1,0:T(8,128)(2,1)}, bf16[64,4096]{1,0:T(8,128)(2,1)}, u32[]{:S(2)}, u32[]{:S(2)}) %collective-permute-start) | collective-permute-done | bytes 524320 | tf_op jit(solution)/shard_map/ppermute | solution.py:329
  22.7 6.3 %collective-permute-done.1 = bf16[64,4096]{1,0:T(8,128)(2,1)} collective-permute-done((bf16[64,4096]{1,0:T(8,128)(2,1)S(1)}, bf16[64,4096]{1,0:T(8,128)(2,1)}, u32[]{:S(2)}, u32[]{:S(2)}) %collective-permute-start.1) | collective-permute-done | bytes 524320 | tf_op jit(solution)/shard_map/ppermute | solution.py:330
  30.1 1.1 constant_dynamic-update-slice_fusion.2
  33.9 1.1 constant_dynamic-update-slice_fusion
  36.0 3.8 %collective-permute-start.5 = (bf16[64,4096]{1,0:T(8,128)(2,1)}, bf16[64,4096]{1,0:T(8,128)(2,1)S(1)}, u32[]{:S(2)}, u32[]{:S(2)}) collective-permute-start(bf16[64,4096]{1,0:T(8,128)(2,1)} %collective-permute-done.4), channel_id=1, source_target_pairs={{0,3},{1,0},{2,1},{3,2},{4,7},{5,4},{6,5},{7,6},{8,11},{9,8},{10,9... | collective-permute-start | bytes 1572872 | tf_op jit(solution)/shard_map/ppermute | solution.py:332
  40.7 9.8 %collective-permute-done.5 = bf16[64,4096]{1,0:T(8,128)(2,1)S(1)} collective-permute-done((bf16[64,4096]{1,0:T(8,128)(2,1)}, bf16[64,4096]{1,0:T(8,128)(2,1)S(1)}, u32[]{:S(2)}, u32[]{:S(2)}) %collective-permute-start.5) | collective-permute-done | bytes 524320 | tf_op jit(solution)/shard_map/ppermute | solution.py:332
  50.5 3.3 %collective-permute-done.3 = bf16[64,4096]{1,0:T(8,128)(2,1)S(1)} collective-permute-done((bf16[64,4096]{1,0:T(8,128)(2,1)}, bf16[64,4096]{1,0:T(8,128)(2,1)S(1)}, u32[]{:S(2)}, u32[]{:S(2)}) %collective-permute-start.3) | collective-permute-done | bytes 524320 | tf_op jit(solution)/shard_map/ppermute | solution.py:331
  55.1 1.3 collective-permute-done.6
  56.7 3.1 %collective-permute-start.8 = (bf16[1024,128]{1,0:T(8,128)(2,1)S(1)}, bf16[1024,128]{1,0:T(8,128)(2,1)S(1)}, u32[]{:S(2)}, u32[]{:S(2)}) collective-permute-start(bf16[1024,128]{1,0:T(8,128)(2,1)S(1)} %broadcast_select_fusion), channel_id=1, source_target_pairs={{0,24},{4,100},{8,0},{12,108},{16,8},{20,116},{24,16},{28,124},{32... | collective-permute-start | bytes 786440 | tf_op jit(solution)/shard_map/ppermute | solution.py:62
  59.8 4.9 %collective-permute-done.9 = bf16[1024,128]{1,0:T(8,128)(2,1)S(1)} collective-permute-done((bf16[1024,128]{1,0:T(8,128)(2,1)S(1)}, bf16[1024,128]{1,0:T(8,128)(2,1)S(1)}, u32[]{:S(2)}, u32[]{:S(2)}) %collective-permute-start.9) | collective-permute-done | bytes 262176 | tf_op jit(solution)/shard_map/ppermute | solution.py:62
  64.7 1.4 collective-permute-done.8
  66.0 1.3 collective-permute-done.7
  68.1 1.5 collective-permute-start.10
  69.6 12.8 %collective-permute-done.11.refs_2_ = bf16[4096,128]{1,0:T(8,128)(2,1)S(1)} collective-permute-done((bf16[4096,128]{1,0:T(8,128)(2,1)S(1)}, bf16[4096,128]{1,0:T(8,128)(2,1)S(1)}, u32[]{:S(2)}, u32[]{:S(2)}) %collective-permute-start.11) | collective-permute-done | bytes 1048608 | tf_op jit(solution)/shard_map/ppermute | solution.py:48
  83.0 2.1 %collective-permute-start.12 = (bf16[2048,128]{1,0:T(8,128)(2,1)S(1)}, bf16[2048,128]{1,0:T(8,128)(2,1)S(1)}, u32[]{:S(2)}, u32[]{:S(2)}) collective-permute-start(bf16[2048,128]{1,0:T(8,128)(2,1)S(1)} %slice.122), channel_id=1, source_target_pairs={{0,32},{4,12},{8,40},{12,20},{16,48},{20,28},{24,56},{28,4},{32,64... | collective-permute-start | bytes 1572872 | tf_op jit(solution)/shard_map/ppermute | solution.py:49
  85.1 6.9 %collective-permute-done.13.refs_4_ = bf16[2048,128]{1,0:T(8,128)(2,1)S(1)} collective-permute-done((bf16[2048,128]{1,0:T(8,128)(2,1)S(1)}, bf16[2048,128]{1,0:T(8,128)(2,1)S(1)}, u32[]{:S(2)}, u32[]{:S(2)}) %collective-permute-start.13) | collective-permute-done | bytes 524320 | tf_op jit(solution)/shard_map/ppermute | solution.py:50
  94.7 10.2 %attend.3 = bf16[128,512]{1,0:T(8,128)(2,1)S(1)} custom-call(s32[2]{0:T(128)S(1)} %pad_add_fusion.ids, s32[16]{0:T(128)S(1)} %copy-done.4, f32[128,512]{1,0:T(8,128)S(1)} %fusion.27.query, f32[512,128]{1,0:T(8,128)S(1)} %get-tuple-element.69.cos_part, f32[512,128]{1,0:T(8,128)S(1)} %get-tuple-element.70.sin_part, ...), custom_call_target="tpu_custom_call" | custom-call | flops 1073741824 | bytes 4194304 | tf_op jit(solution)/shard_map/attend/pallas_call | solution.py:282
  106.1 1.7 %collective-permute-start.19 = (bf16[128,2048]{1,0:T(8,128)(2,1)S(1)}, bf16[128,2048]{1,0:T(8,128)(2,1)S(1)}, u32[]{:S(2)}, u32[]{:S(2)}) collective-permute-start(bf16[128,2048]{1,0:T(8,128)(2,1)S(1)} %get-tuple-element.56), channel_id=1, source_target_pairs={{0,1},{1,2},{2,3},{3,0},{4,5},{5,6},{6,7},{7,4},{8,9},{9,10},{10,1... | collective-permute-start | bytes 1572872 | tf_op jit(solution)/shard_map/ppermute | solution.py:360
  107.8 16.8 %attend.4 = bf16[256,512]{1,0:T(8,128)(2,1)S(1)} custom-call(s32[2]{0:T(128)S(1)} %pad_add_fusion.ids, s32[16]{0:T(128)S(1)} %copy-done.4, f32[256,512]{1,0:T(8,128)S(1)} %pad_maximum_fusion.1.query, f32[512,128]{1,0:T(8,128)S(1)} %get-tuple-element.69.cos_part, f32[512,128]{1,0:T(8,128)S(1)} %get-tuple-element.70.sin_part, ...), custom_call_target="tpu_custom_call" | custom-call | flops 2147483648 | bytes 4194304 | tf_op jit(solution)/shard_map/attend/pallas_call | solution.py:282
  124.7 1.3 fusion.20
  126.0 1.6 %collective-permute-start.22 = (bf16[128,2048]{1,0:T(8,128)(2,1)S(1)}, bf16[128,2048]{1,0:T(8,128)(2,1)S(1)}, u32[]{:S(2)}, u32[]{:S(2)}) collective-permute-start(bf16[128,2048]{1,0:T(8,128)(2,1)S(1)} %get-tuple-element.53), channel_id=1, source_target_pairs={{0,3},{1,0},{2,1},{3,2},{4,7},{5,4},{6,5},{7,6},{8,11},{9,8},{10,9... | collective-permute-start | bytes 1572872 | tf_op jit(solution)/shard_map/ppermute | solution.py:366
  128.6 3.2 %collective-permute-start.24 = (bf16[128,2048]{1,0:T(8,128)(2,1)S(1)}, bf16[128,2048]{1,0:T(8,128)(2,1)S(1)}, u32[]{:S(2)}, u32[]{:S(2)}) collective-permute-start(bf16[128,2048]{1,0:T(8,128)(2,1)S(1)} %get-tuple-element.48), channel_id=1, source_target_pairs={{0,3},{1,0},{2,1},{3,2},{4,7},{5,4},{6,5},{7,6},{8,11},{9,8},{10,9... | collective-permute-start | bytes 1572872 | tf_op jit(solution)/shard_map/ppermute | solution.py:371
  131.8 10.2 %attend.5 = bf16[128,512]{1,0:T(8,128)(2,1)S(1)} custom-call(s32[2]{0:T(128)S(1)} %pad_add_fusion.ids, s32[16]{0:T(128)S(1)} %copy-done.4, f32[128,512]{1,0:T(8,128)S(1)} %fusion.21.query, f32[512,128]{1,0:T(8,128)S(1)} %get-tuple-element.69.cos_part, f32[512,128]{1,0:T(8,128)S(1)} %get-tuple-element.70.sin_part, ...), custom_call_target="tpu_custom_call" | custom-call | flops 1073741824 | bytes 4194304 | tf_op jit(solution)/shard_map/attend/pallas_call | solution.py:282
  142.0 2.0 %collective-permute-done.21 = bf16[128,2048]{1,0:T(8,128)(2,1)S(1)} collective-permute-done((bf16[128,2048]{1,0:T(8,128)(2,1)S(1)}, bf16[128,2048]{1,0:T(8,128)(2,1)S(1)}, u32[]{:S(2)}, u32[]{:S(2)}) %collective-permute-start.21) | collective-permute-done | bytes 524320 | tf_op jit(solution)/shard_map/ppermute | solution.py:370
  144.1 9.5 %collective-permute-done.23 = bf16[128,2048]{1,0:T(8,128)(2,1)S(1)} collective-permute-done((bf16[128,2048]{1,0:T(8,128)(2,1)S(1)}, bf16[128,2048]{1,0:T(8,128)(2,1)S(1)}, u32[]{:S(2)}, u32[]{:S(2)}) %collective-permute-start.23) | collective-permute-done | bytes 524320 | tf_op jit(solution)/shard_map/ppermute | solution.py:364
  153.8 1.8 %fusion.1 = bf16[128,4096]{1,0:T(8,128)(2,1)} fusion(bf16[128,512]{1,0:T(8,128)(2,1)S(1)} %attend.5, bf16[512,4096]{1,0:T(8,128)(2,1)S(1)} %copy-done.6, f32[128,2048]{1,0:T(8,128)S(1)} %convert_add_fusion, f32[128,2048]{1,0:T(8,128)S(1)} %convert_add_fusion.1, bf16[128,4096]{1,0:T(8,128)(2,1)S(1)} %copy-done.2), kind=kOutput, calls=%fused_computation.2 | convolution fusion | flops 539492352 | bytes 8519680 | tf_op jit(solution)/shard_map/dot_general | solution.py:116
  (93 shorter events, 18.9 us)
Async XLA Ops:
  0.0 12.0 %copy-start = (bf16[4096,128]{1,0:T(8,128)(2,1)S(1)}, bf16[4096,128]{1,0:T(8,128)(2,1)}, u32[]{:S(2)}) copy-start(bf16[4096,128]{1,0:T(8,128)(2,1)} %param.12) | copy-start | bytes 3145732
  0.0 1.3 copy-start.1
  3.4 26.7 %collective-permute-start.4 = (bf16[64,4096]{1,0:T(8,128)(2,1)}, bf16[64,4096]{1,0:T(8,128)(2,1)}, u32[]{:S(2)}, u32[]{:S(2)}) collective-permute-start(bf16[64,4096]{1,0:T(8,128)(2,1)} %get-tuple-element.27), channel_id=1, source_target_pairs={{0,3},{1,0},{2,1},{3,2},{4,7},{5,4},{6,5},{7,6},{8,11},{9,8},{10,9... | collective-permute-start | bytes 1572872 | tf_op jit(solution)/shard_map/ppermute | solution.py:328
  6.4 16.3 %collective-permute-start = (bf16[64,4096]{1,0:T(8,128)(2,1)}, bf16[64,4096]{1,0:T(8,128)(2,1)}, u32[]{:S(2)}, u32[]{:S(2)}) collective-permute-start(bf16[64,4096]{1,0:T(8,128)(2,1)} %get-tuple-element.27), channel_id=1, source_target_pairs={{0,1},{1,2},{2,3},{3,0},{4,5},{5,6},{6,7},{7,4},{8,9},{9,10},{10,1... | collective-permute-start | bytes 1572872 | tf_op jit(solution)/shard_map/ppermute | solution.py:329
  6.4 26.4 %collective-permute-start.2 = (bf16[64,4096]{1,0:T(8,128)(2,1)S(1)}, bf16[64,4096]{1,0:T(8,128)(2,1)}, u32[]{:S(2)}, u32[]{:S(2)}) collective-permute-start(bf16[64,4096]{1,0:T(8,128)(2,1)S(1)} %get-tuple-element.28), channel_id=1, source_target_pairs={{0,1},{1,2},{2,3},{3,0},{4,5},{5,6},{6,7},{7,4},{8,9},{9,10},{10,1... | collective-permute-start | bytes 1572872 | tf_op jit(solution)/shard_map/ppermute | solution.py:327
  7.0 22.0 %collective-permute-start.1 = (bf16[64,4096]{1,0:T(8,128)(2,1)S(1)}, bf16[64,4096]{1,0:T(8,128)(2,1)}, u32[]{:S(2)}, u32[]{:S(2)}) collective-permute-start(bf16[64,4096]{1,0:T(8,128)(2,1)S(1)} %get-tuple-element.28), channel_id=1, source_target_pairs={{0,3},{1,0},{2,1},{3,2},{4,7},{5,4},{6,5},{7,6},{8,11},{9,8},{10,9... | collective-permute-start | bytes 1572872 | tf_op jit(solution)/shard_map/ppermute | solution.py:330
  15.3 15.9 %copy-start.7 = (bf16[4096,128]{1,0:T(8,128)(2,1)S(1)}, bf16[4096,128]{1,0:T(8,128)(2,1)}, u32[]{:S(2)}) copy-start(bf16[4096,128]{1,0:T(8,128)(2,1)} %param.11) | copy-start | bytes 3145732
  18.4 13.7 %copy-start.5 = (bf16[4096,512]{1,0:T(8,128)(2,1)S(1)}, bf16[4096,512]{1,0:T(8,128)(2,1)}, u32[]{:S(2)}) copy-start(bf16[4096,512]{1,0:T(8,128)(2,1)} %param.10) | copy-start | bytes 12582916
  36.0 14.5 %collective-permute-start.5 = (bf16[64,4096]{1,0:T(8,128)(2,1)}, bf16[64,4096]{1,0:T(8,128)(2,1)S(1)}, u32[]{:S(2)}, u32[]{:S(2)}) collective-permute-start(bf16[64,4096]{1,0:T(8,128)(2,1)} %collective-permute-done.4), channel_id=1, source_target_pairs={{0,3},{1,0},{2,1},{3,2},{4,7},{5,4},{6,5},{7,6},{8,11},{9,8},{10,9... | collective-permute-start | bytes 1572872 | tf_op jit(solution)/shard_map/ppermute | solution.py:332
  39.9 13.9 %collective-permute-start.3 = (bf16[64,4096]{1,0:T(8,128)(2,1)}, bf16[64,4096]{1,0:T(8,128)(2,1)S(1)}, u32[]{:S(2)}, u32[]{:S(2)}) collective-permute-start(bf16[64,4096]{1,0:T(8,128)(2,1)} %collective-permute-done.2), channel_id=1, source_target_pairs={{0,1},{1,2},{2,3},{3,0},{4,5},{5,6},{6,7},{7,4},{8,9},{9,10},{10,1... | collective-permute-start | bytes 1572872 | tf_op jit(solution)/shard_map/ppermute | solution.py:331
  55.0 1.4 collective-permute-start.6
  56.6 8.1 %collective-permute-start.9 = (bf16[1024,128]{1,0:T(8,128)(2,1)S(1)}, bf16[1024,128]{1,0:T(8,128)(2,1)S(1)}, u32[]{:S(2)}, u32[]{:S(2)}) collective-permute-start(bf16[1024,128]{1,0:T(8,128)(2,1)S(1)} %broadcast_select_fusion), channel_id=1, source_target_pairs={{0,16},{4,68},{8,24},{12,76},{16,0},{20,84},{24,8},{28,92},{32,48}... | collective-permute-start | bytes 786440 | tf_op jit(solution)/shard_map/ppermute | solution.py:62
  56.7 9.3 %collective-permute-start.8 = (bf16[1024,128]{1,0:T(8,128)(2,1)S(1)}, bf16[1024,128]{1,0:T(8,128)(2,1)S(1)}, u32[]{:S(2)}, u32[]{:S(2)}) collective-permute-start(bf16[1024,128]{1,0:T(8,128)(2,1)S(1)} %broadcast_select_fusion), channel_id=1, source_target_pairs={{0,24},{4,100},{8,0},{12,108},{16,8},{20,116},{24,16},{28,124},{32... | collective-permute-start | bytes 786440 | tf_op jit(solution)/shard_map/ppermute | solution.py:62
  59.8 7.6 %collective-permute-start.7 = (bf16[1024,128]{1,0:T(8,128)(2,1)S(1)}, bf16[1024,128]{1,0:T(8,128)(2,1)S(1)}, u32[]{:S(2)}, u32[]{:S(2)}) collective-permute-start(bf16[1024,128]{1,0:T(8,128)(2,1)S(1)} %broadcast_select_fusion), channel_id=1, source_target_pairs={{0,8},{4,36},{8,16},{12,44},{16,24},{20,52},{24,0},{28,60},{32,40}... | collective-permute-start | bytes 786440 | tf_op jit(solution)/shard_map/ppermute | solution.py:62
  67.4 27.2 %copy-start.4 = (s32[16]{0:T(128)S(1)}, s32[16]{0:T(128)}, u32[]{:S(2)}) copy-start(s32[16]{0:T(128)} %lengths.5) | copy-start | bytes 196
  67.5 14.9 %collective-permute-start.11 = (bf16[4096,128]{1,0:T(8,128)(2,1)S(1)}, bf16[4096,128]{1,0:T(8,128)(2,1)S(1)}, u32[]{:S(2)}, u32[]{:S(2)}) collective-permute-start(bf16[4096,128]{1,0:T(8,128)(2,1)S(1)} %pad_maximum_fusion.refs_0_), channel_id=1, source_target_pairs={{0,96},{4,28},{8,104},{12,4},{16,112},{20,12},{24,120},{28,20},{32... | collective-permute-start | bytes 3145736 | tf_op jit(solution)/shard_map/ppermute | solution.py:48
  68.1 14.9 %collective-permute-start.10 = (bf16[4096,128]{1,0:T(8,128)(2,1)S(1)}, bf16[4096,128]{1,0:T(8,128)(2,1)S(1)}, u32[]{:S(2)}, u32[]{:S(2)}) collective-permute-start(bf16[4096,128]{1,0:T(8,128)(2,1)S(1)} %pad_maximum_fusion.refs_0_), channel_id=1, source_target_pairs={{0,32},{4,12},{8,40},{12,20},{16,48},{20,28},{24,56},{28,4},{32,64... | collective-permute-start | bytes 3145736 | tf_op jit(solution)/shard_map/ppermute | solution.py:47
  69.6 23.8 %collective-permute-start.14 = (bf16[4096,128]{1,0:T(8,128)(2,1)S(1)}, bf16[4096,128]{1,0:T(8,128)(2,1)S(1)}, u32[]{:S(2)}, u32[]{:S(2)}) collective-permute-start(bf16[4096,128]{1,0:T(8,128)(2,1)S(1)} %pad_maximum_fusion.refs_0_), channel_id=1, source_target_pairs={{0,4},{4,0},{8,12},{12,8},{16,20},{20,16},{24,28},{28,24},{32,36},... | collective-permute-start | bytes 3145736 | tf_op jit(solution)/shard_map/ppermute | solution.py:65
  82.4 9.6 %collective-permute-start.13 = (bf16[2048,128]{1,0:T(8,128)(2,1)S(1)}, bf16[2048,128]{1,0:T(8,128)(2,1)S(1)}, u32[]{:S(2)}, u32[]{:S(2)}) collective-permute-start(bf16[2048,128]{1,0:T(8,128)(2,1)S(1)} %slice.123), channel_id=1, source_target_pairs={{0,96},{4,28},{8,104},{12,4},{16,112},{20,12},{24,120},{28,20},{32... | collective-permute-start | bytes 1572872 | tf_op jit(solution)/shard_map/ppermute | solution.py:50
  83.0 10.9 %collective-permute-start.16 = (bf16[4096,128]{1,0:T(8,128)(2,1)S(1)}, bf16[4096,128]{1,0:T(8,128)(2,1)S(1)}, u32[]{:S(2)}, u32[]{:S(2)}) collective-permute-start(bf16[4096,128]{1,0:T(8,128)(2,1)S(1)} %collective-permute-done.11.refs_2_), channel_id=1, source_target_pairs={{0,4},{4,0},{8,12},{12,8},{16,20},{20,16},{24,28},{28,24},{32,36},... | collective-permute-start | bytes 3145736 | tf_op jit(solution)/shard_map/ppermute | solution.py:65
  83.0 9.3 %collective-permute-start.12 = (bf16[2048,128]{1,0:T(8,128)(2,1)S(1)}, bf16[2048,128]{1,0:T(8,128)(2,1)S(1)}, u32[]{:S(2)}, u32[]{:S(2)}) collective-permute-start(bf16[2048,128]{1,0:T(8,128)(2,1)S(1)} %slice.122), channel_id=1, source_target_pairs={{0,32},{4,12},{8,40},{12,20},{16,48},{20,28},{24,56},{28,4},{32,64... | collective-permute-start | bytes 1572872 | tf_op jit(solution)/shard_map/ppermute | solution.py:49
  85.1 9.6 %collective-permute-start.15 = (bf16[4096,128]{1,0:T(8,128)(2,1)S(1)}, bf16[4096,128]{1,0:T(8,128)(2,1)S(1)}, u32[]{:S(2)}, u32[]{:S(2)}) collective-permute-start(bf16[4096,128]{1,0:T(8,128)(2,1)S(1)} %collective-permute-done.10.refs_1_), channel_id=1, source_target_pairs={{0,4},{4,0},{8,12},{12,8},{16,20},{20,16},{24,28},{28,24},{32,36},... | collective-permute-start | bytes 3145736 | tf_op jit(solution)/shard_map/ppermute | solution.py:65
  92.0 1.9 %collective-permute-start.18 = (bf16[2048,128]{1,0:T(8,128)(2,1)S(1)}, bf16[2048,128]{1,0:T(8,128)(2,1)S(1)}, u32[]{:S(2)}, u32[]{:S(2)}) collective-permute-start(bf16[2048,128]{1,0:T(8,128)(2,1)S(1)} %collective-permute-done.13.refs_4_), channel_id=1, source_target_pairs={{0,4},{4,0},{8,12},{12,8},{16,20},{20,16},{24,28},{28,24},{32,36},... | collective-permute-start | bytes 1572872 | tf_op jit(solution)/shard_map/ppermute | solution.py:66
  92.3 2.4 %collective-permute-start.17 = (bf16[2048,128]{1,0:T(8,128)(2,1)S(1)}, bf16[2048,128]{1,0:T(8,128)(2,1)S(1)}, u32[]{:S(2)}, u32[]{:S(2)}) collective-permute-start(bf16[2048,128]{1,0:T(8,128)(2,1)S(1)} %collective-permute-done.12.refs_3_), channel_id=1, source_target_pairs={{0,4},{4,0},{8,12},{12,8},{16,20},{20,16},{24,28},{28,24},{32,36},... | collective-permute-start | bytes 1572872 | tf_op jit(solution)/shard_map/ppermute | solution.py:66
  93.3 11.6 %copy-start.6 = (bf16[512,4096]{1,0:T(8,128)(2,1)S(1)}, bf16[512,4096]{1,0:T(8,128)(2,1)}, u32[]{:S(2)}) copy-start(bf16[512,4096]{1,0:T(8,128)(2,1)} %param.13) | copy-start | bytes 12582916
  105.7 21.9 %collective-permute-start.20 = (bf16[128,2048]{1,0:T(8,128)(2,1)S(1)}, bf16[128,2048]{1,0:T(8,128)(2,1)S(1)}, u32[]{:S(2)}, u32[]{:S(2)}) collective-permute-start(bf16[128,2048]{1,0:T(8,128)(2,1)S(1)} %get-tuple-element.55), channel_id=1, source_target_pairs={{0,3},{1,0},{2,1},{3,2},{4,7},{5,4},{6,5},{7,6},{8,11},{9,8},{10,9... | collective-permute-start | bytes 1572872 | tf_op jit(solution)/shard_map/ppermute | solution.py:361
  106.1 21.5 %collective-permute-start.19 = (bf16[128,2048]{1,0:T(8,128)(2,1)S(1)}, bf16[128,2048]{1,0:T(8,128)(2,1)S(1)}, u32[]{:S(2)}, u32[]{:S(2)}) collective-permute-start(bf16[128,2048]{1,0:T(8,128)(2,1)S(1)} %get-tuple-element.56), channel_id=1, source_target_pairs={{0,1},{1,2},{2,3},{3,0},{4,5},{5,6},{6,7},{7,4},{8,9},{9,10},{10,1... | collective-permute-start | bytes 1572872 | tf_op jit(solution)/shard_map/ppermute | solution.py:360
  126.0 16.0 %collective-permute-start.22 = (bf16[128,2048]{1,0:T(8,128)(2,1)S(1)}, bf16[128,2048]{1,0:T(8,128)(2,1)S(1)}, u32[]{:S(2)}, u32[]{:S(2)}) collective-permute-start(bf16[128,2048]{1,0:T(8,128)(2,1)S(1)} %get-tuple-element.53), channel_id=1, source_target_pairs={{0,3},{1,0},{2,1},{3,2},{4,7},{5,4},{6,5},{7,6},{8,11},{9,8},{10,9... | collective-permute-start | bytes 1572872 | tf_op jit(solution)/shard_map/ppermute | solution.py:366
  127.9 16.1 %collective-permute-start.21 = (bf16[128,2048]{1,0:T(8,128)(2,1)S(1)}, bf16[128,2048]{1,0:T(8,128)(2,1)S(1)}, u32[]{:S(2)}, u32[]{:S(2)}) collective-permute-start(bf16[128,2048]{1,0:T(8,128)(2,1)S(1)} %get-tuple-element.47), channel_id=1, source_target_pairs={{0,1},{1,2},{2,3},{3,0},{4,5},{5,6},{6,7},{7,4},{8,9},{9,10},{10,1... | collective-permute-start | bytes 1572872 | tf_op jit(solution)/shard_map/ppermute | solution.py:370
  128.5 25.1 %collective-permute-start.23 = (bf16[128,2048]{1,0:T(8,128)(2,1)S(1)}, bf16[128,2048]{1,0:T(8,128)(2,1)S(1)}, u32[]{:S(2)}, u32[]{:S(2)}) collective-permute-start(bf16[128,2048]{1,0:T(8,128)(2,1)S(1)} %get-tuple-element.54), channel_id=1, source_target_pairs={{0,1},{1,2},{2,3},{3,0},{4,5},{5,6},{6,7},{7,4},{8,9},{9,10},{10,1... | collective-permute-start | bytes 1572872 | tf_op jit(solution)/shard_map/ppermute | solution.py:364
  128.6 25.0 %collective-permute-start.24 = (bf16[128,2048]{1,0:T(8,128)(2,1)S(1)}, bf16[128,2048]{1,0:T(8,128)(2,1)S(1)}, u32[]{:S(2)}, u32[]{:S(2)}) collective-permute-start(bf16[128,2048]{1,0:T(8,128)(2,1)S(1)} %get-tuple-element.48), channel_id=1, source_target_pairs={{0,3},{1,0},{2,1},{3,2},{4,7},{5,4},{6,5},{7,6},{8,11},{9,8},{10,9... | collective-permute-start | bytes 1572872 | tf_op jit(solution)/shard_map/ppermute | solution.py:371
  142.0 11.8 %copy-start.2 = (bf16[128,4096]{1,0:T(8,128)(2,1)S(1)}, bf16[128,4096]{1,0:T(8,128)(2,1)}, u32[]{:S(2)}) copy-start(bf16[128,4096]{1,0:T(8,128)(2,1)} %tokens.1) | copy-start | bytes 3145732
  (1 other events, 0.7 us)
